TPU v7x, 32 devices: a whole 2x2x4 slice. The times are simulated.
32 devices in a mesh: fsdp: 32 (over z, y, x, core).
Axes of the slice: x: 2, y: 2, z: 4, core: 2. Of those that a mesh axis runs over, the one named last changes fastest.
Arguments:
- x: bfloat16 [32, 192, 1024], P('fsdp')
- lengths: int32 [32], P('fsdp')
- d_y: bfloat16 [32, 192, 1024], P('fsdp')
- w_attn: bfloat16 [2, 4, 1024, 1024], P(None, None, 'fsdp')
- b_attn: bfloat16 [2, 4, 1024], P(None, None, 'fsdp')
- ln_par: bfloat16 [2, 4, 1024], P(None, None, 'fsdp')
- w_up: bfloat16 [2, 1024, 4096], P(None, 'fsdp')
- b_up: bfloat16 [2, 4096], P(None, 'fsdp')
- w_down: bfloat16 [2, 4096, 1024], P(None, 'fsdp')
- b_down: bfloat16 [2, 1024], P(None, 'fsdp')
Outputs:
- output 1: bfloat16 [32, 192, 1024], P('fsdp')
- output 2: float32 [2, 4, 1024, 1024], P(None, None, 'fsdp')
- output 3: float32 [2, 4, 1024], P(None, None, 'fsdp')
- output 4: float32 [2, 4, 1024], P(None, None, 'fsdp')
- output 5: float32 [2, 1024, 4096], P(None, 'fsdp')
- output 6: float32 [2, 4096], P(None, 'fsdp')
- output 7: float32 [2, 4096, 1024], P(None, 'fsdp')
- output 8: float32 [2, 1024], P(None, 'fsdp')
All inputs are finite; a program needn't handle non-finite values.
Results may differ from a plain program's by a relative error of at most 0.0160853.
Values are sent between devices in bfloat16 or wider.
A program may use at most 1 GiB of HBM per device.

v0:
```python
import math
import functools
import jax
import jax.numpy as jnp
from jax import lax
from jax.sharding import PartitionSpec as P

HEAD_DIM = 64
EPS = 1e-5
THETA = 10000.0
NEG_BIG = -1e30


def rotary_tables(seq_len):
    half_dim = HEAD_DIM // 2
    inv_freq = 1.0 / (THETA ** (jnp.arange(half_dim, dtype=jnp.float32) * (2.0 / HEAD_DIM)))
    angles = jnp.arange(seq_len, dtype=jnp.float32)[:, None] * inv_freq[None, :]
    return jnp.cos(angles)[:, None, :], jnp.sin(angles)[:, None, :]


def rotate(tensor, cos_tab, sin_tab):
    half_dim = HEAD_DIM // 2
    first_half = tensor[..., :half_dim]
    second_half = tensor[..., half_dim:]
    return jnp.concatenate([first_half * cos_tab - second_half * sin_tab, second_half * cos_tab + first_half * sin_tab], axis=-1)


def rotate_back(tensor, cos_tab, sin_tab):
    half_dim = HEAD_DIM // 2
    first_half = tensor[..., :half_dim]
    second_half = tensor[..., half_dim:]
    return jnp.concatenate([first_half * cos_tab + second_half * sin_tab, second_half * cos_tab - first_half * sin_tab], axis=-1)


def norm_fwd(x_in, gain, shift):
    row_mean = jnp.mean(x_in, axis=-1, keepdims=True)
    centered = x_in - row_mean
    variance = jnp.mean(centered * centered, axis=-1, keepdims=True)
    return centered * lax.rsqrt(variance + EPS) * gain + shift


def gelu_slope(pre_act):
    normal_cdf = 0.5 * (1.0 + lax.erf(pre_act * (1.0 / math.sqrt(2.0))))
    density = jnp.exp(-0.5 * pre_act * pre_act) * (1.0 / math.sqrt(2.0 * math.pi))
    return normal_cdf + pre_act * density


def layer_forward(x, weights, lengths, tables):
    w_attn, b_attn, ln_par, w_up, b_up, w_down, b_down = weights
    cos_tab, sin_tab = tables
    num_seq, seq_len, model_dim = x.shape
    num_heads = model_dim // HEAD_DIM
    x_f32 = x.astype(jnp.float32)
    h_one = norm_fwd(x_f32, ln_par[0].astype(jnp.float32), ln_par[1].astype(jnp.float32)).astype(jnp.bfloat16)
    projected = jnp.einsum('bld,kde->kble', h_one, w_attn[:3], preferred_element_type=jnp.float32)
    projected = (projected + b_attn[:3, None, None, :].astype(jnp.float32)).reshape(3, num_seq, seq_len, num_heads, HEAD_DIM)
    query_rot = rotate(projected[0] * (HEAD_DIM ** -0.5), cos_tab, sin_tab).astype(jnp.bfloat16)
    key_rot = rotate(projected[1], cos_tab, sin_tab).astype(jnp.bfloat16)
    values = projected[2].astype(jnp.bfloat16)
    scores = jnp.einsum('bqhd,bkhd->bhqk', query_rot, key_rot, preferred_element_type=jnp.float32)
    key_valid = jnp.arange(seq_len)[None, None, None, :] < lengths[:, None, None, None]
    probs_bf = jax.nn.softmax(jnp.where(key_valid, scores, NEG_BIG), axis=-1).astype(jnp.bfloat16)
    context = jnp.einsum('bhqk,bkhd->bqhd', probs_bf, values, preferred_element_type=jnp.float32)
    context = context.astype(jnp.bfloat16).reshape(num_seq, seq_len, model_dim)
    attn_out = jnp.einsum('bld,de->ble', context, w_attn[3], preferred_element_type=jnp.float32)
    x_mid = (x_f32 + attn_out + b_attn[3].astype(jnp.float32)).astype(jnp.bfloat16)
    mid_f32 = x_mid.astype(jnp.float32)
    h_two = norm_fwd(mid_f32, ln_par[2].astype(jnp.float32), ln_par[3].astype(jnp.float32)).astype(jnp.bfloat16)
    pre_act = jnp.einsum('bld,df->blf', h_two, w_up, preferred_element_type=jnp.float32) + b_up.astype(jnp.float32)
    act_bf = jax.nn.gelu(pre_act, approximate=False).astype(jnp.bfloat16)
    mlp_out = jnp.einsum('blf,fd->bld', act_bf, w_down, preferred_element_type=jnp.float32)
    y_out = (mid_f32 + mlp_out + b_down.astype(jnp.float32)).astype(jnp.bfloat16)
    saved_acts = (x, h_one, query_rot, key_rot, values, probs_bf, context, x_mid, h_two, pre_act, act_bf)
    return y_out, saved_acts


def layer_backward(d_out, saved_acts, weights, tables):
    w_attn, ln_par, w_up, w_down = weights[0], weights[2], weights[3], weights[5]
    cos_tab, sin_tab = tables
    x, h_one, query_rot, key_rot, values, probs_bf, context, x_mid, h_two, pre_act, act_bf = saved_acts
    num_seq, seq_len, model_dim = x.shape
    num_heads = model_dim // HEAD_DIM
    gb_down = jnp.sum(d_out, axis=(0, 1), dtype=jnp.float32)
    gw_down = jnp.einsum('blf,bld->fd', act_bf, d_out, preferred_element_type=jnp.float32)
    d_act = jnp.einsum('bld,fd->blf', d_out, w_down, preferred_element_type=jnp.float32)
    d_pre = d_act * gelu_slope(pre_act)
    gb_up = jnp.sum(d_pre, axis=(0, 1))
    d_pre_bf = d_pre.astype(jnp.bfloat16)
    gw_up = jnp.einsum('bld,blf->df', h_two, d_pre_bf, preferred_element_type=jnp.float32)
    d_h_two = jnp.einsum('blf,df->bld', d_pre_bf, w_up, preferred_element_type=jnp.float32)
    _, norm_pull_two = jax.vjp(norm_fwd, x_mid.astype(jnp.float32), ln_par[2].astype(jnp.float32), ln_par[3].astype(jnp.float32))
    d_mid_norm, g_gain_two, g_shift_two = norm_pull_two(d_h_two)
    d_mid = (d_out.astype(jnp.float32) + d_mid_norm).astype(jnp.bfloat16)
    gb_out = jnp.sum(d_mid, axis=(0, 1), dtype=jnp.float32)
    gw_out = jnp.einsum('bld,ble->de', context, d_mid, preferred_element_type=jnp.float32)
    d_context = jnp.einsum('ble,de->bld', d_mid, w_attn[3], preferred_element_type=jnp.float32)
    d_context = d_context.astype(jnp.bfloat16).reshape(num_seq, seq_len, num_heads, HEAD_DIM)
    d_probs = jnp.einsum('bqhd,bkhd->bhqk', d_context, values, preferred_element_type=jnp.float32)
    d_values = jnp.einsum('bhqk,bqhd->bkhd', probs_bf, d_context, preferred_element_type=jnp.float32)
    probs_f32 = probs_bf.astype(jnp.float32)
    d_scores = (probs_f32 * (d_probs - jnp.sum(d_probs * probs_f32, axis=-1, keepdims=True))).astype(jnp.bfloat16)
    d_query = jnp.einsum('bhqk,bkhd->bqhd', d_scores, key_rot, preferred_element_type=jnp.float32)
    d_key = jnp.einsum('bhqk,bqhd->bkhd', d_scores, query_rot, preferred_element_type=jnp.float32)
    d_proj = jnp.stack([
        (rotate_back(d_query, cos_tab, sin_tab) * (HEAD_DIM ** -0.5)).astype(jnp.bfloat16),
        rotate_back(d_key, cos_tab, sin_tab).astype(jnp.bfloat16),
        d_values.astype(jnp.bfloat16)]).reshape(3, num_seq, seq_len, model_dim)
    gb_qkv = jnp.sum(d_proj, axis=(1, 2), dtype=jnp.float32)
    gw_qkv = jnp.einsum('bld,kble->kde', h_one, d_proj, preferred_element_type=jnp.float32)
    d_h_one = jnp.einsum('kble,kde->bld', d_proj, w_attn[:3], preferred_element_type=jnp.float32)
    _, norm_pull_one = jax.vjp(norm_fwd, x.astype(jnp.float32), ln_par[0].astype(jnp.float32), ln_par[1].astype(jnp.float32))
    d_x_norm, g_gain_one, g_shift_one = norm_pull_one(d_h_one)
    d_x = (d_mid.astype(jnp.float32) + d_x_norm).astype(jnp.bfloat16)
    gb_attn = jnp.concatenate([gb_qkv, gb_out[None]], axis=0)
    g_ln = jnp.stack([g_gain_one, g_shift_one, g_gain_two, g_shift_two])
    return d_x, (gw_qkv, gw_out, gb_attn, g_ln, gw_up, gb_up, gw_down, gb_down)


def gather_layer(layer_shards, axis_name):
    w_attn, b_attn, ln_par, w_up, b_up, w_down, b_down = layer_shards
    return (lax.all_gather(w_attn, axis_name, axis=1, tiled=True),
            lax.all_gather(b_attn, axis_name, axis=1, tiled=True),
            lax.all_gather(ln_par, axis_name, axis=1, tiled=True),
            lax.all_gather(w_up, axis_name, axis=0, tiled=True),
            lax.all_gather(b_up, axis_name, axis=0, tiled=True),
            lax.all_gather(w_down, axis_name, axis=0, tiled=True),
            lax.all_gather(b_down, axis_name, axis=0, tiled=True))


def scatter_grads(layer_grads, axis_name):
    gw_qkv, gw_out, gb_attn, g_ln, gw_up, gb_up, gw_down, gb_down = layer_grads
    reduce_rows = functools.partial(lax.psum_scatter, axis_name=axis_name, tiled=True)
    attn_part = jnp.concatenate([reduce_rows(gw_qkv, scatter_dimension=1), reduce_rows(gw_out, scatter_dimension=0)[None]], axis=0)
    return (attn_part,
            reduce_rows(gb_attn, scatter_dimension=1),
            reduce_rows(g_ln, scatter_dimension=1),
            reduce_rows(gw_up, scatter_dimension=0),
            reduce_rows(gb_up, scatter_dimension=0),
            reduce_rows(gw_down, scatter_dimension=0),
            reduce_rows(gb_down, scatter_dimension=0))


def solution(mesh):
    axis_name = mesh.axis_names[0]
    batch_spec = P(axis_name)
    weight_specs = (P(None, None, axis_name, None), P(None, None, axis_name), P(None, None, axis_name),
                    P(None, axis_name, None), P(None, axis_name), P(None, axis_name, None), P(None, axis_name))

    def device_step(x, lengths, d_y, w_attn, b_attn, ln_par, w_up, b_up, w_down, b_down):
        shards = (w_attn, b_attn, ln_par, w_up, b_up, w_down, b_down)
        num_layers = w_attn.shape[0]
        tables = rotary_tables(x.shape[1])
        hidden = x
        saved_list = []
        for layer_idx in range(num_layers):
            full_wts = gather_layer(tuple(shard[layer_idx] for shard in shards), axis_name)
            hidden, saved_acts = layer_forward(hidden, full_wts, lengths, tables)
            saved_list.append(saved_acts)
        grad_x = d_y
        grads_list = [None] * num_layers
        for layer_idx in reversed(range(num_layers)):
            layer_shards, grad_x = lax.optimization_barrier((tuple(shard[layer_idx] for shard in shards), grad_x))
            full_wts = gather_layer(layer_shards, axis_name)
            grad_x, layer_grads = layer_backward(grad_x, saved_list[layer_idx], full_wts, tables)
            grads_list[layer_idx] = scatter_grads(layer_grads, axis_name)
        stacked = tuple(jnp.stack([grads_list[layer_pos][field_pos] for layer_pos in range(num_layers)]) for field_pos in range(7))
        return (grad_x,) + stacked

    return jax.shard_map(device_step, mesh=mesh,
                         in_specs=(batch_spec, batch_spec, batch_spec) + weight_specs,
                         out_specs=(batch_spec,) + weight_specs,
                         check_vma=False)
```

profile of v0, /device:TPU:0, one launch (start us, length us, event | category | flops | bytes accessed | tf_op | source)
XLA Modules:
  0.0 2988.8 jit_solution(11755827591861514582)
XLA Ops:
  16.0 46.4 %all-gather.2 = bf16[1,4,1024]{1,0,2:T(2,128)(2,1)S(1)} all-gather(bf16[1,4,32]{1,0,2:T(2,128)(2,1)S(1)} %copy.206), channel_id=4, replica_groups=mesh['fsdp'=32] {'fsdp'}, dimensions={2}, use_global_device_ids=true | all-gather | bytes 8448 | tf_op jit(solution)/shard_map/all_gather | solution.py:122
  63.1 40.2 %all-gather.9 = bf16[1,4,1024]{1,0,2:T(2,128)(2,1)S(1)} all-gather(bf16[1,4,32]{1,0,2:T(2,128)(2,1)S(1)} %copy.207), channel_id=11, replica_groups=mesh['fsdp'=32] {'fsdp'}, dimensions={2}, use_global_device_ids=true | all-gather | bytes 8448 | tf_op jit(solution)/shard_map/all_gather | solution.py:122
  104.8 37.6 %all-gather.4 = bf16[1,4096]{1,0:T(2,128)(2,1)S(1)} all-gather(bf16[1,128]{1,0:T(2,128)(2,1)S(1)} %get-tuple-element.123), channel_id=6, replica_groups=mesh['fsdp'=32] {'fsdp'}, dimensions={1}, use_global_device_ids=true | all-gather | bytes 8448 | tf_op jit(solution)/shard_map/all_gather | solution.py:125
  143.1 38.8 %all-reduce = bf16[1024]{0:T(1024)(128)(2,1)S(1)} all-reduce(bf16[1024]{0:T(1024)(128)(2,1)S(1)} %dynamic-update-slice), channel_id=8, replica_groups=mesh['fsdp'=32] {'fsdp'}, use_global_device_ids=true, to_apply=%add | all-reduce | flops 1024 | bytes 4096
  183.5 40.1 %all-gather.11 = bf16[1,4096]{1,0:T(2,128)(2,1)S(1)} all-gather(bf16[1,128]{1,0:T(2,128)(2,1)S(1)} %get-tuple-element.124), channel_id=13, replica_groups=mesh['fsdp'=32] {'fsdp'}, dimensions={1}, use_global_device_ids=true | all-gather | bytes 8448 | tf_op jit(solution)/shard_map/all_gather | solution.py:125
  224.2 36.9 %all-gather.12 = bf16[32,32,4]{1,2,0:T(4,128)(2,1)S(1)} all-gather(bf16[1,32,4]{1,2,0:T(4,128)(2,1)S(1)} %bitcast.508), channel_id=1, replica_groups=mesh['fsdp'=32] {'fsdp'}, dimensions={0}, use_global_device_ids=true | all-gather | bytes 8448 | tf_op jit(solution)/shard_map/all_gather | solution.py:123
  261.2 40.8 %all-gather = bf16[1,4,1024]{1,0,2:T(2,128)(2,1)S(1)} all-gather(bf16[1,4,32]{1,0,2:T(2,128)(2,1)S(1)} %copy.204), channel_id=2, replica_groups=mesh['fsdp'=32] {'fsdp'}, dimensions={2}, use_global_device_ids=true | all-gather | bytes 8448 | tf_op jit(solution)/shard_map/all_gather | solution.py:123
  302.0 40.1 %all-gather.7 = bf16[1,4,1024]{1,0,2:T(2,128)(2,1)S(1)} all-gather(bf16[1,4,32]{1,0,2:T(2,128)(2,1)S(1)} %copy.205), channel_id=9, replica_groups=mesh['fsdp'=32] {'fsdp'}, dimensions={2}, use_global_device_ids=true | all-gather | bytes 8448 | tf_op jit(solution)/shard_map/all_gather | solution.py:123
  503.9 70.7 %all-gather.28.cloned.1.call-done = bf16[1024,4096]{1,0:T(8,128)(2,1)} async-done(((bf16[32,4096]{1,0:T(8,128)(2,1)}), bf16[1024,4096]{1,0:T(8,128)(2,1)}) %all-gather.28.cloned.1.call-update) | async-done | bytes 8388624 | tf_op jit(solution)/shard_map/all_gather | solution.py:124
  584.8 68.8 %all-gather.30.cloned.1.call-done = bf16[4,1024,1024]{2,1,0:T(8,128)(2,1)} async-done(((bf16[4,32,1024]{2,1,0:T(8,128)(2,1)}), bf16[4,1024,1024]{2,1,0:T(8,128)(2,1)}) %all-gather.30.cloned.1.call-update) | async-done | bytes 8388624 | tf_op jit(solution)/shard_map/all_gather | solution.py:121
  705.0 40.2 %all-gather.13 = bf16[32,32,4]{1,2,0:T(4,128)(2,1)S(1)} all-gather(bf16[1,32,4]{1,2,0:T(4,128)(2,1)S(1)} %bitcast.507), channel_id=1, replica_groups=mesh['fsdp'=32] {'fsdp'}, dimensions={0}, use_global_device_ids=true | all-gather | bytes 8448 | tf_op jit(solution)/shard_map/all_gather | solution.py:123
  768.0 70.6 %all-gather.34.cloned.1.call-done = bf16[1024,4096]{1,0:T(8,128)(2,1)} async-done(((bf16[32,4096]{1,0:T(8,128)(2,1)}), bf16[1024,4096]{1,0:T(8,128)(2,1)}) %all-gather.34.cloned.1.call-update) | async-done | bytes 8388624 | tf_op jit(solution)/shard_map/all_gather | solution.py:124
  853.7 63.8 %all-gather.36.cloned.1.call-done = bf16[4,1024,1024]{2,1,0:T(8,128)(2,1)} async-done(((bf16[4,32,1024]{2,1,0:T(8,128)(2,1)}), bf16[4,1024,1024]{2,1,0:T(8,128)(2,1)}) %all-gather.36.cloned.1.call-update) | async-done | bytes 8388624 | tf_op jit(solution)/shard_map/all_gather | solution.py:121
  1055.6 133.1 %reduce-scatter.37.cloned.1.call-done = f32[32,4]{1,0:T(8,128)} async-done(((f32[1024,4]{1,0:T(8,128)}), f32[32,4]{1,0:T(8,128)}) %reduce-scatter.37.cloned.1.call-update) | async-done | bytes 528
  1189.4 139.3 %reduce-scatter.33.cloned.1.call-done = f32[32,1024]{1,0:T(8,128)} async-done(((f32[1024,1024]{1,0:T(8,128)}), f32[32,1024]{1,0:T(8,128)}) %reduce-scatter.33.cloned.1.call-update) | async-done | bytes 131088
  1330.1 37.7 %all-reduce.7 = (f32[4096]{0:T(1024)S(1)}, f32[4096]{0:T(1024)S(1)}, f32[1024]{0:T(1024)S(1)}, f32[1024]{0:T(1024)S(1)}) all-reduce(f32[4096]{0:T(1024)S(1)} %copy-done.92, f32[4096]{0:T(1024)S(1)} %copy-done.93, f32[1024]{0:T(1024)S(1)} %copy-done.86, f32[1024]{0:T(1024)S(1)} %copy-done.87), channel_id=25, replica_groups=mesh['fsdp'=32] {'fsdp'}, use_global_device_ids=true, to_apply=%region_47.48.clone | all-reduce | flops 10240 | bytes 81920
  1370.1 92.3 %reduce-scatter.39.cloned.1.call-done = f32[32,4]{1,0:T(8,128)} async-done(((f32[1024,4]{1,0:T(8,128)}), f32[32,4]{1,0:T(8,128)}) %reduce-scatter.39.cloned.1.call-update) | async-done | bytes 528
  1463.2 133.6 %reduce-scatter.35.cloned.1.call-done = f32[32,4]{1,0:T(8,128)} async-done(((f32[1024,4]{1,0:T(8,128)}), f32[32,4]{1,0:T(8,128)}) %reduce-scatter.35.cloned.1.call-update) | async-done | bytes 528
  1598.3 138.3 %reduce-scatter.31.cloned.1.call-done = f32[32,1024]{1,0:T(8,128)} async-done(((f32[1024,1024]{1,0:T(8,128)}), f32[32,1024]{1,0:T(8,128)}) %reduce-scatter.31.cloned.1.call-update) | async-done | bytes 131088
  1737.9 496.6 %all-reduce.11.cloned.1.call-done = (f32[3,1024,1024]{2,0,1:T(4,128)}, f32[3,1024,1024]{2,0,1:T(4,128)}) async-done(((f32[3,1024,1024]{2,0,1:T(4,128)}, f32[3,1024,1024]{2,0,1:T(4,128)}), (f32[3,1024,1024]{2,0,1:T(4,128)}, f32[3,1024,1024]{2,0,1:T(4,128)})) %all-reduce.11.cloned.1.call-update) | async-done | bytes 25165840
  2238.4 180.7 %reduce-scatter.27.cloned.1.call-done = f32[128,1024]{1,0:T(8,128)} async-done(((f32[4096,1024]{1,0:T(8,128)}), f32[128,1024]{1,0:T(8,128)}) %reduce-scatter.27.cloned.1.call-update) | async-done | bytes 524304 | tf_op jit(solution)/shard_map/reduce_scatter | solution.py:139
  2419.1 186.7 %reduce-scatter.29.cloned.1.call-done = f32[128,1024]{1,0:T(8,128)} async-done(((f32[4096,1024]{1,0:T(8,128)}), f32[128,1024]{1,0:T(8,128)}) %reduce-scatter.29.cloned.1.call-update) | async-done | bytes 524304 | tf_op jit(solution)/shard_map/reduce_scatter | solution.py:139
  2608.1 184.6 %reduce-scatter.25.cloned.1.call-done = f32[32,4096]{1,0:T(8,128)} async-done(((f32[1024,4096]{1,0:T(8,128)}), f32[32,4096]{1,0:T(8,128)}) %reduce-scatter.25.cloned.1.call-update) | async-done | bytes 524304 | tf_op jit(solution)/shard_map/reduce_scatter | solution.py:137
  2792.6 186.8 %reduce-scatter.23.cloned.1.call-done = f32[32,4096]{1,0:T(8,128)} async-done(((f32[1024,4096]{1,0:T(8,128)}), f32[32,4096]{1,0:T(8,128)}) %reduce-scatter.23.cloned.1.call-update) | async-done | bytes 524304 | tf_op jit(solution)/shard_map/reduce_scatter | solution.py:137
  (454 shorter events, 427.5 us)
Async XLA Ops:
  7.2 390.4 %all-gather.38.cloned.1.call-start = ((), (), s32[]{:S(2)}) async-start(), calls=%async_computation.20 | async-start | bytes 8650752 | tf_op jit(solution)/shard_map/all_gather | solution.py:121
  9.4 406.5 %all-gather.40.cloned.1.call-start = ((), (), s32[]{:S(2)}) async-start(), calls=%async_computation.21 | async-start | bytes 8650752 | tf_op jit(solution)/shard_map/all_gather | solution.py:124
  11.5 417.4 %all-gather.42.cloned.1.call-start = ((), (), s32[]{:S(2)}) async-start(), calls=%async_computation.22 | async-start | bytes 8650752 | tf_op jit(solution)/shard_map/all_gather | solution.py:126
  12.5 424.6 %all-gather.44.cloned.1.call-start = ((), (), s32[]{:S(2)}) async-start(), calls=%async_computation.23 | async-start | bytes 8650752 | tf_op jit(solution)/shard_map/all_gather | solution.py:121
  13.1 448.5 %all-gather.46.cloned.1.call-start = ((), (), s32[]{:S(2)}) async-start(), calls=%async_computation.24 | async-start | bytes 8650752 | tf_op jit(solution)/shard_map/all_gather | solution.py:124
  13.7 482.2 %all-gather.26.cloned.1.call-start = ((), (), s32[]{:S(2)}) async-start(), calls=%async_computation.10 | async-start | bytes 8650752 | tf_op jit(solution)/shard_map/all_gather | solution.py:126
  14.3 328.3 %copy-start.6 = (bf16[1,192,1024]{2,1,0:T(8,128)(2,1)S(1)}, bf16[1,192,1024]{2,1,0:T(8,128)(2,1)}, u32[]{:S(2)}) copy-start(bf16[1,192,1024]{2,1,0:T(8,128)(2,1)} %param.10) | copy-start | bytes 1179652
  14.3 560.3 %all-gather.28.cloned.1.call-start = ((), (), s32[]{:S(2)}) async-start(), calls=%async_computation.11 | async-start | bytes 8650752 | tf_op jit(solution)/shard_map/all_gather | solution.py:124
  15.1 638.5 %all-gather.30.cloned.1.call-start = ((), (), s32[]{:S(2)}) async-start(), calls=%async_computation.12 | async-start | bytes 8650752 | tf_op jit(solution)/shard_map/all_gather | solution.py:121
  15.8 744.2 %all-gather.32.cloned.1.call-start = ((), (), s32[]{:S(2)}) async-start(), calls=%async_computation.13 | async-start | bytes 8650752 | tf_op jit(solution)/shard_map/all_gather | solution.py:126
  683.7 154.9 %all-gather.34.cloned.1.call-start = ((), (), s32[]{:S(2)}) async-start(), calls=%async_computation.14 | async-start | bytes 8650752 | tf_op jit(solution)/shard_map/all_gather | solution.py:124
  684.3 233.3 %all-gather.36.cloned.1.call-start = ((), (), s32[]{:S(2)}) async-start(), calls=%async_computation.15 | async-start | bytes 8650752 | tf_op jit(solution)/shard_map/all_gather | solution.py:121
  685.0 369.7 %reduce-scatter.41.cloned.1.call-start = ((), (), s32[]{:S(2)}) async-start(), calls=%async_computation.30 | async-start | bytes 540672
  696.5 492.1 %reduce-scatter.37.cloned.1.call-start = ((), (), s32[]{:S(2)}) async-start(), calls=%async_computation.28 | async-start | bytes 540672
  700.4 628.4 %reduce-scatter.33.cloned.1.call-start = ((), (), s32[]{:S(2)}) async-start(), calls=%async_computation.26 | async-start | bytes 4325376
  704.3 758.1 %reduce-scatter.39.cloned.1.call-start = ((), (), s32[]{:S(2)}) async-start(), calls=%async_computation.29 | async-start | bytes 540672
  944.9 652.0 %reduce-scatter.35.cloned.1.call-start = ((), (), s32[]{:S(2)}) async-start(), calls=%async_computation.27 | async-start | bytes 540672
  947.7 788.9 %reduce-scatter.31.cloned.1.call-start = ((), (), s32[]{:S(2)}) async-start(), calls=%async_computation.25 | async-start | bytes 4325376
  950.6 1283.9 %all-reduce.11.cloned.1.call-start = ((), (), s32[]{:S(2)}) async-start(), calls=%async_computation.31 | async-start | bytes 67108864
  1002.7 1416.4 %reduce-scatter.27.cloned.1.call-start = ((), (), s32[]{:S(2)}) async-start(), calls=%async_computation.18 | async-start | bytes 17301504 | tf_op jit(solution)/shard_map/reduce_scatter | solution.py:139
  1013.3 1592.4 %reduce-scatter.29.cloned.1.call-start = ((), (), s32[]{:S(2)}) async-start(), calls=%async_computation.19 | async-start | bytes 17301504 | tf_op jit(solution)/shard_map/reduce_scatter | solution.py:139
  1027.8 1764.8 %reduce-scatter.25.cloned.1.call-start = ((), (), s32[]{:S(2)}) async-start(), calls=%async_computation.17 | async-start | bytes 17301504 | tf_op jit(solution)/shard_map/reduce_scatter | solution.py:137
  1038.6 1940.9 %reduce-scatter.23.cloned.1.call-start = ((), (), s32[]{:S(2)}) async-start(), calls=%async_computation.16 | async-start | bytes 17301504 | tf_op jit(solution)/shard_map/reduce_scatter | solution.py:137
  1049.4 319.7 %copy-start.107 = (f32[192]{0:T(256)S(1)}, f32[192]{0:T(256)}, u32[]{:S(2)}) copy-start(f32[192]{0:T(256)} %get-tuple-element.51) | copy-start | bytes 2308
  (112 other events, 2601.8 us)
Sparse Core Ops, SparseCore 0:
  11.5 83.8 all-gather.37
  98.8 76.9 all-gather.39
  178.6 76.1 all-gather.41
  258.2 79.3 all-gather.43
  340.3 77.0 all-gather.45
  420.1 75.8 all-gather.25
  498.8 75.7 all-gather.27
  577.5 76.0 all-gather.29
  683.8 76.2 all-gather.31
  762.8 75.7 all-gather.33
  841.5 76.0 all-gather.35
  919.7 135.0 reduce-scatter.40
  1057.0 131.5 reduce-scatter.36
  1190.7 137.9 reduce-scatter.32
  1330.8 131.5 reduce-scatter.38
  1465.1 131.7 reduce-scatter.34
  1599.0 137.5 reduce-scatter.30
  1742.9 491.5 all-reduce.10
  2236.7 182.3 reduce-scatter.26
  2421.2 184.4 reduce-scatter.28
  2608.1 184.4 reduce-scatter.24
  2794.9 184.4 reduce-scatter.22
where the time goes:
time: 3000 us; the launch traced here: 2990 us
  waiting for transfers between devices  2190 us (73%)
  blocking collectives  399 us (13%)
  matrix products  167 us (6%)
  local copies, waits for them, and re-layouts  109 us (4%)
  other arithmetic  102 us (3%)
    unnamed x29, waiting for transfers between devices  1140 us
    reduce_scatter x2, waiting for transfers between devices, scatter_grads(): reduce_rows(gw_up, scatter_dimension=0)  371 us
    reduce_scatter x2, waiting for transfers between devices, scatter_grads(): reduce_rows(gw_down, scatter_dimension=0)  367 us
    all_gather x4, blocking collectives, gather_layer(): lax.all_gather(ln_par, axis_name, axis=1, tiled=True)  158 us
    all_gather x4, waiting for transfers between devices, gather_layer(): lax.all_gather(w_up, axis_name, axis=0, tiled=True)  141 us
    all_gather x4, waiting for transfers between devices, gather_layer(): lax.all_gather(w_attn, axis_name, axis=1, tiled=True)  133 us
    all_gather x2, blocking collectives, gather_layer(): lax.all_gather(b_attn, axis_name, axis=1, tiled=True)  86.6 us
    all_gather x2, blocking collectives, gather_layer(): lax.all_gather(b_up, axis_name, axis=0, tiled=True)  77.6 us
  transfers between devices with their start and end apart: 22, of which 17 were waited for; matrix products, arithmetic and copies ran while one was open for 11% of the time, Pallas kernels for 0%

commit v1 on v0

v1 whole, which is shorter than its diff:
```python
import functools
import math
import jax
import jax.numpy as jnp
from jax import lax
from jax.experimental import pallas as pl
from jax.experimental.pallas import tpu as pltpu
from jax.sharding import PartitionSpec as P

MESH = pl.DeviceIdType.MESH
LAYERS = 2
ORDERS = (("b", 0, 1), ("b", 1, 0), ("a", 0, 1), ("a", 1, 0), ("b", 0, 1), ("b", 1, 0))
UNITS = [(layer, piece) for layer in range(LAYERS) for piece in range(6)] + [(0, 6)]
STAGE_LAG = (0, 0, 1, 3)
AHEAD = 2


def gather_kernel(wa, wu, wd, sm, fa, fu, fd, fs, va, vu, vd, vs, load_sem, own_sem, xy_sem, z_sem,
                  push_send, push_recv, recv_sem):
    me = lax.axis_index("fsdp")
    core, xc, yc, zc = me % 2, (me // 2) % 2, (me // 4) % 2, me // 8
    partner = me + 1 - 2 * core
    near = (me + 2 - 4 * xc, me + 4 - 8 * yc)
    up, down = me + 8, me - 8
    has_up, has_down = zc < 3, zc > 0

    def full(u, src):
        layer, piece = UNITS[u]
        if piece < 2:
            return fa.at[layer, pl.ds(2 * piece, 2), pl.ds(pl.multiple_of(32 * src, 32), 32), :]
        if piece < 4:
            return fu.at[layer, pl.ds(pl.multiple_of(32 * src + 16 * (piece - 2), 16), 16), :]
        if piece < 6:
            return fd.at[pl.ds(pl.multiple_of(4096 * layer + 128 * src + 64 * (piece - 4), 64), 64), :]
        return fs.at[pl.ds(pl.multiple_of(8 * src, 8), 8), :]

    def own(u):
        layer, piece = UNITS[u]
        if piece < 2:
            return va.at[layer, pl.ds(2 * piece, 2)]
        if piece < 4:
            return vu.at[layer, pl.ds(16 * (piece - 2), 16), :]
        if piece < 6:
            return vd.at[layer, pl.ds(64 * (piece - 4), 64), :]
        return vs

    def kind(u):
        return (UNITS[u][1] + 0) // 2

    def order(u):
        return ORDERS[UNITS[u][1] % 6]

    def tiny(u):
        return 1 if UNITS[u][1] == 6 else 0

    barrier = pltpu.get_barrier_semaphore()
    for peer in (partner,) + near:
        pl.semaphore_signal(barrier, inc=1, device_id=(peer,), device_id_type=MESH)

    @pl.when(has_up)
    def _():
        pl.semaphore_signal(barrier, inc=1, device_id=(up,), device_id_type=MESH)

    @pl.when(has_down)
    def _():
        pl.semaphore_signal(barrier, inc=1, device_id=(down,), device_id_type=MESH)

    loads = [pltpu.make_async_copy(src, dst, load_sem.at[i])
             for i, (src, dst) in enumerate(((wa, va), (wu, vu), (wd, vd), (sm, vs)))]
    for load in loads:
        load.start()
    for load in loads:
        load.wait()
    pl.semaphore_wait(barrier, 3 + has_up.astype(jnp.int32) + has_down.astype(jnp.int32))

    def remote(u, src_ref, src, send, recv, dev):
        return pltpu.make_async_remote_copy(src_ref=src_ref, dst_ref=full(u, src), send_sem=send, recv_sem=recv,
                                            device_id=(dev,), device_id_type=MESH)

    def send_z(u, src_ref, src, slot, above, below):
        if above is not None:
            @pl.when(above)
            def _():
                remote(u, src_ref, src, z_sem.at[tiny(u)], recv_sem.at[u, slot], up).start()
        if below is not None:
            @pl.when(below)
            def _():
                remote(u, src_ref, src, z_sem.at[tiny(u)], recv_sem.at[u, slot], down).start()

    def send_xy(u, src_ref, src, dim, slot):
        remote(u, src_ref, src, xy_sem.at[tiny(u)], recv_sem.at[u, slot], near[dim]).start()

    def push(u, src_ref, src):
        remote(u, src_ref, src, push_send.at[kind(u)], push_recv.at[kind(u)], partner).start()

    def column(flip_p, p):
        base = me - 8 * zc
        if flip_p:
            base = base + (near[p] - me)
        return base

    def arrived(u, src, slot):
        remote(u, full(u, src), src, xy_sem.at[tiny(u)], recv_sem.at[u, slot], me).wait_recv()
        return full(u, src)

    def stage0(u):
        col, p, q = order(u)
        mine = own(u)
        send_z(u, mine, me, zc, has_up, has_down)
        send_xy(u, mine, me, p, 4 + zc)
        send_xy(u, mine, me, q, 8)
        push(u, mine, me)
        pltpu.make_async_copy(mine, full(u, me), own_sem.at[kind(u)]).start()

    def z_arrivals(u, flips, send_p):
        col, p, q = order(u)
        for dz in (1, 2, 3):
            for step in (-1, 1):
                for flip_p in flips:
                    zs = zc + step * dz
                    src = column(flip_p, p) + 8 * zs
                    slot = 4 * flip_p + zs
                    present = (zc >= dz) if step < 0 else (zc <= 3 - dz)

                    @pl.when(present)
                    def _(src=src, slot=slot, step=step):
                        ref = arrived(u, src, slot)
                        send_z(u, ref, src, slot, has_up if step < 0 else None, has_down if step > 0 else None)
                        if send_p:
                            send_xy(u, ref, src, p, 4 + slot)
                        send_xy(u, ref, src, q, 8)
                        push(u, ref, src)

    def stage1(u):
        col, p, q = order(u)
        if col == "a":
            z_arrivals(u, (0,), True)
        else:
            src = near[p]
            ref = arrived(u, src, 4 + zc)
            send_z(u, ref, src, 4 + zc, has_up, has_down)
            send_xy(u, ref, src, q, 8)
            push(u, ref, src)

    def stage2(u):
        col, p, q = order(u)
        if col == "a":
            for hop in range(4):
                zs = lax.rem(zc + hop, 4)
                src = column(1, p) + 8 * zs
                ref = arrived(u, src, 4 + zs)
                send_xy(u, ref, src, q, 8)
                push(u, ref, src)
        else:
            z_arrivals(u, (0, 1), False)

    def stage3(u):
        col, p, q = order(u)
        rows = fs.at[pl.ds(0, 64), :] if tiny(u) else fd.at[pl.ds(0, 512), :]
        pltpu.make_async_copy(rows, rows, recv_sem.at[u, 8]).wait()
        for flip_p in (0, 1):
            base = column(flip_p, p) + (near[q] - me)

            def body(zs, carry, base=base):
                src = base + 8 * zs
                push(u, full(u, src), src)
                return carry

            lax.fori_loop(0, 4, body, 0)

    stages = (stage0, stage1, stage2, stage3)
    count = len(UNITS)
    for rnd in range(count + STAGE_LAG[3]):
        for k in range(4):
            if k == 0:
                todo = range(AHEAD + 1) if rnd == 0 else [rnd + AHEAD]
            else:
                todo = [rnd - STAGE_LAG[k]]
            for u in todo:
                if 0 <= u < count:
                    stages[k](u)

    def drain(ref, sem):
        pltpu.make_async_copy(ref, ref, sem).wait()

    per_layer = 64 * LAYERS
    drain(fd.at[pl.ds(0, 60 * per_layer), :], xy_sem.at[0])
    drain(fs.at[pl.ds(0, 9 * 8), :], xy_sem.at[1])
    ends = jnp.logical_or(zc == 0, zc == 3)

    @pl.when(ends)
    def _():
        drain(fd.at[pl.ds(0, 10 * per_layer), :], z_sem.at[0])
        drain(fs.at[pl.ds(0, 2 * 8), :], z_sem.at[1])

    @pl.when(jnp.logical_not(ends))
    def _():
        drain(fd.at[pl.ds(0, 50 * per_layer), :], z_sem.at[0])
        drain(fs.at[pl.ds(0, 10 * 8), :], z_sem.at[1])

    halves = (fa.at[0], fu.at[0], fd.at[pl.ds(0, 4096), :], fs.at[pl.ds(0, 128), :])
    for i, half in enumerate(halves):
        drain(half, push_send.at[i])
        drain(half, push_recv.at[i])
    for i, ref in enumerate((va, vu, vd, vs)):
        drain(ref, own_sem.at[i])


def gather_weights(w_attn, w_up, w_down, small):
    shapes = (w_attn.shape, w_up.shape, w_down.shape, small.shape)
    dt = jnp.bfloat16
    return pl.pallas_call(
        gather_kernel,
        out_shape=(jax.ShapeDtypeStruct((LAYERS, 4, 1024, 1024), dt), jax.ShapeDtypeStruct((LAYERS, 1024, 4096), dt),
                   jax.ShapeDtypeStruct((LAYERS * 4096, 1024), dt), jax.ShapeDtypeStruct((32 * 8, 128), dt)),
        in_specs=[pl.BlockSpec(memory_space=pltpu.HBM)] * 4,
        out_specs=[pl.BlockSpec(memory_space=pltpu.HBM)] * 4,
        scratch_shapes=[pltpu.VMEM(s, dt) for s in shapes] + [
            pltpu.SemaphoreType.DMA((4,)), pltpu.SemaphoreType.DMA((4,)), pltpu.SemaphoreType.DMA((2,)),
            pltpu.SemaphoreType.DMA((2,)), pltpu.SemaphoreType.DMA((4,)), pltpu.SemaphoreType.DMA((4,)),
            pltpu.SemaphoreType.DMA((len(UNITS), 9))],
        compiler_params=pltpu.CompilerParams(collective_id=0, has_side_effects=True),
        name="gather_weights",
    )(w_attn, w_up, w_down, small)


HEAD_DIM = 64
EPS = 1e-5
THETA = 10000.0
NEG_BIG = -1e30


def rotary_tables(seq_len):
    half_dim = HEAD_DIM // 2
    inv_freq = 1.0 / (THETA ** (jnp.arange(half_dim, dtype=jnp.float32) * (2.0 / HEAD_DIM)))
    angles = jnp.arange(seq_len, dtype=jnp.float32)[:, None] * inv_freq[None, :]
    return jnp.cos(angles)[:, None, :], jnp.sin(angles)[:, None, :]


def rotate(tensor, cos_tab, sin_tab):
    half_dim = HEAD_DIM // 2
    first_half = tensor[..., :half_dim]
    second_half = tensor[..., half_dim:]
    return jnp.concatenate([first_half * cos_tab - second_half * sin_tab, second_half * cos_tab + first_half * sin_tab], axis=-1)


def rotate_back(tensor, cos_tab, sin_tab):
    return rotate(tensor, cos_tab, -sin_tab)


def norm_fwd(x_in, gain, shift):
    row_mean = jnp.mean(x_in, axis=-1, keepdims=True)
    centered = x_in - row_mean
    variance = jnp.mean(centered * centered, axis=-1, keepdims=True)
    return centered * lax.rsqrt(variance + EPS) * gain + shift


def gelu_slope(pre_act):
    normal_cdf = 0.5 * (1.0 + lax.erf(pre_act * (1.0 / math.sqrt(2.0))))
    density = jnp.exp(-0.5 * pre_act * pre_act) * (1.0 / math.sqrt(2.0 * math.pi))
    return normal_cdf + pre_act * density


def dot(a, b):
    return jnp.dot(a, b, preferred_element_type=jnp.float32)


def dot_t(a, b):
    return lax.dot_general(a, b, (((1,), (1,)), ((), ())), preferred_element_type=jnp.float32)


def dot_g(a, b):
    return lax.dot_general(a, b, (((0,), (0,)), ((), ())), preferred_element_type=jnp.float32)


def heads(tensor):
    return tensor.reshape(tensor.shape[0], -1, HEAD_DIM)


def layer_forward(x, weights, length, tables, last):
    w_attn, w_up, w_down, b_attn, ln_par, b_up, b_down = weights
    cos_tab, sin_tab = tables
    seq_len = x.shape[0]
    x_f32 = x.astype(jnp.float32)
    h_one = norm_fwd(x_f32, ln_par[0], ln_par[1]).astype(jnp.bfloat16)
    query, key, values = (heads(dot(h_one, w_attn[i]) + b_attn[i]) for i in range(3))
    query_rot = rotate(query * (HEAD_DIM ** -0.5), cos_tab, sin_tab).astype(jnp.bfloat16)
    key_rot = rotate(key, cos_tab, sin_tab).astype(jnp.bfloat16)
    values = values.astype(jnp.bfloat16)
    scores = jnp.einsum('qhd,khd->hqk', query_rot, key_rot, preferred_element_type=jnp.float32)
    key_valid = jnp.arange(seq_len)[None, None, :] < length
    probs_bf = jax.nn.softmax(jnp.where(key_valid, scores, NEG_BIG), axis=-1).astype(jnp.bfloat16)
    context = jnp.einsum('hqk,khd->qhd', probs_bf, values, preferred_element_type=jnp.float32)
    context = context.astype(jnp.bfloat16).reshape(seq_len, -1)
    x_mid = (x_f32 + dot(context, w_attn[3]) + b_attn[3]).astype(jnp.bfloat16)
    mid_f32 = x_mid.astype(jnp.float32)
    h_two = norm_fwd(mid_f32, ln_par[2], ln_par[3]).astype(jnp.bfloat16)
    pre_act = dot(h_two, w_up) + b_up
    act_bf = jax.nn.gelu(pre_act, approximate=False).astype(jnp.bfloat16)
    y_out = None
    if not last:
        y_out = (mid_f32 + dot(act_bf, w_down) + b_down).astype(jnp.bfloat16)
    return y_out, (x, h_one, query_rot, key_rot, values, probs_bf, context, x_mid, h_two, pre_act, act_bf)


def layer_backward(d_out, saved_acts, weights, tables):
    w_attn, w_up, w_down, b_attn, ln_par, b_up, b_down = weights
    cos_tab, sin_tab = tables
    x, h_one, query_rot, key_rot, values, probs_bf, context, x_mid, h_two, pre_act, act_bf = saved_acts
    seq_len = x.shape[0]
    gb_down = jnp.sum(d_out, axis=0, dtype=jnp.float32)
    d_pre = dot_t(d_out, w_down) * gelu_slope(pre_act)
    gb_up = jnp.sum(d_pre, axis=0)
    d_pre_bf = d_pre.astype(jnp.bfloat16)
    d_h_two = dot_t(d_pre_bf, w_up)
    _, norm_pull_two = jax.vjp(norm_fwd, x_mid.astype(jnp.float32), ln_par[2], ln_par[3])
    d_mid_norm, g_gain_two, g_shift_two = norm_pull_two(d_h_two)
    d_mid = (d_out.astype(jnp.float32) + d_mid_norm).astype(jnp.bfloat16)
    gb_out = jnp.sum(d_mid, axis=0, dtype=jnp.float32)
    d_context = heads(dot_t(d_mid, w_attn[3]).astype(jnp.bfloat16))
    d_probs = jnp.einsum('qhd,khd->hqk', d_context, values, preferred_element_type=jnp.float32)
    d_values = jnp.einsum('hqk,qhd->khd', probs_bf, d_context, preferred_element_type=jnp.float32)
    probs_f32 = probs_bf.astype(jnp.float32)
    d_scores = (probs_f32 * (d_probs - jnp.sum(d_probs * probs_f32, axis=-1, keepdims=True))).astype(jnp.bfloat16)
    d_query = jnp.einsum('hqk,khd->qhd', d_scores, key_rot, preferred_element_type=jnp.float32)
    d_key = jnp.einsum('hqk,qhd->khd', d_scores, query_rot, preferred_element_type=jnp.float32)
    d_proj = jnp.concatenate([
        (rotate_back(d_query, cos_tab, sin_tab) * (HEAD_DIM ** -0.5)).astype(jnp.bfloat16).reshape(seq_len, -1),
        rotate_back(d_key, cos_tab, sin_tab).astype(jnp.bfloat16).reshape(seq_len, -1),
        d_values.astype(jnp.bfloat16).reshape(seq_len, -1)], axis=1)
    gb_qkv = jnp.sum(d_proj, axis=0, dtype=jnp.float32)
    d_h_one = sum(dot_t(d_proj[:, 1024 * i:1024 * i + 1024], w_attn[i]) for i in range(3))
    _, norm_pull_one = jax.vjp(norm_fwd, x.astype(jnp.float32), ln_par[0], ln_par[1])
    d_x_norm, g_gain_one, g_shift_one = norm_pull_one(d_h_one)
    d_x = (d_mid.astype(jnp.float32) + d_x_norm).astype(jnp.bfloat16)
    small = (jnp.concatenate([gb_qkv, gb_out]).reshape(4, -1),
             jnp.stack([g_gain_one, g_shift_one, g_gain_two, g_shift_two]), gb_up, gb_down)
    return d_x, (h_one, context, h_two, act_bf, d_proj, d_mid, d_pre_bf, d_out), small


def pack_small(b_attn, ln_par, b_up, b_down):
    rows = [b_attn.reshape(2, 128), ln_par.reshape(2, 128), b_up, jnp.pad(b_down, ((0, 0), (0, 96)))]
    return jnp.stack(rows, axis=1).reshape(8, 128)


def unpack_small(gathered):
    rows = gathered.reshape(32, 2, 4, 128).astype(jnp.float32)

    def fours(row):
        return row.reshape(32, 4, 32).transpose(1, 0, 2).reshape(4, 1024)

    return [(fours(rows[:, l, 0]), fours(rows[:, l, 1]), rows[:, l, 2].reshape(4096), rows[:, l, 3, :32].reshape(1024))
            for l in range(2)]


def solution(mesh):
    axis_name = mesh.axis_names[0]
    batch_spec = P(axis_name)
    weight_specs = (P(None, None, axis_name, None), P(None, None, axis_name), P(None, None, axis_name),
                    P(None, axis_name, None), P(None, axis_name), P(None, axis_name, None), P(None, axis_name))

    def device_step(x, lengths, d_y, w_attn, b_attn, ln_par, w_up, b_up, w_down, b_down):
        tables = rotary_tables(x.shape[1])
        fa, fu, fd, fs = gather_weights(w_attn, w_up, w_down, pack_small(b_attn, ln_par, b_up, b_down))
        smalls = unpack_small(fs)
        weights = [(fa[l], fu[l], fd[4096 * l:4096 * l + 4096]) + smalls[l] for l in range(2)]
        hidden, saved = x[0], []
        for l in range(2):
            hidden, acts = layer_forward(hidden, weights[l], lengths[0], tables, l == 1)
            saved.append(acts)
        grad, big, tiny = d_y[0], [None] * 2, [None] * 2
        scatter = functools.partial(lax.psum_scatter, axis_name=axis_name, scatter_dimension=0, tiled=True)
        for l in (1, 0):
            grad, (h1, ctx, h2, act, d_proj, d_mid, d_pre, d_out), small = layer_backward(grad, saved[l], weights[l], tables)
            g_qkv = scatter(dot_g(h1, d_proj))
            g_o = scatter(dot_g(ctx, d_mid))
            big[l] = (jnp.stack([g_qkv[:, :1024], g_qkv[:, 1024:2048], g_qkv[:, 2048:], g_o]),
                      scatter(dot_g(h2, d_pre)), scatter(dot_g(act, d_out)))
            gb, gl, gu, gd = small
            tiny[l] = jnp.concatenate([gb.reshape(4, 32, 32).transpose(1, 0, 2).reshape(32, 128),
                                       gl.reshape(4, 32, 32).transpose(1, 0, 2).reshape(32, 128),
                                       gu.reshape(32, 128), gd.reshape(32, 32)], axis=1)
        tiny = scatter(jnp.concatenate(tiny, axis=1)).reshape(2, 416)
        return (grad[None], jnp.stack([big[0][0], big[1][0]]), tiny[:, :128].reshape(2, 4, 32),
                tiny[:, 128:256].reshape(2, 4, 32), jnp.stack([big[0][1], big[1][1]]), tiny[:, 256:384],
                jnp.stack([big[0][2], big[1][2]]), tiny[:, 384:])

    return jax.shard_map(device_step, mesh=mesh,
                         in_specs=(batch_spec, batch_spec, batch_spec) + weight_specs,
                         out_specs=(batch_spec,) + weight_specs,
                         check_vma=False)
```

time: 3000 us -> 1860 us (0.62)
  waiting for transfers between devices: 2190 us -> 1390 us
  blocking collectives: 399 us -> 0 us
  Pallas kernels: 0 us -> 194 us
  other arithmetic: 102 us -> 30 us
  local copies, waits for them, and re-layouts: 109 us -> 63.2 us
    unnamed x29 -> x10, waiting for transfers between devices: 1140 us -> 58.4 us
    reduce_scatter x4 -> x8, waiting for transfers between devices: 739 us -> 1330 us  [the longest x2 371 us: device_step(): scatter(dot_g(act, d_out))]
    all_gather x8 -> x0, blocking collectives: 322 us -> none  [the longest x4 158 us: gather_layer(): lax.all_gather(ln_par, axis_name, axis=1, tiled=True)]
    all_gather x11 -> x0, waiting for transfers between devices: 313 us -> none  [the longest x4 141 us: gather_layer(): lax.all_gather(w_up, axis_name, axis=0, tiled=True)]
    pallas_call x0 -> x1, Pallas kernels: none -> 194 us  [gather_weights(): pl.pallas_call(gather_kernel, out_shape=(jax.ShapeDtypeStruct((LAYERS, 4,...]
    unnamed x2 -> x0, blocking collectives: 76.5 us -> none
    convert_element_type x13 -> x2, other arithmetic: 59.9 us -> 1.06 us  [the longest x1 0.85 us: unpack_small(): rows = gathered.reshape(32, 2, 4, 128).astype(jnp.float32)]
    transpose x2, local copies, waits for them, and re-layouts: 36.9 us -> 0.1 us  [device_step(): gb.reshape(4, 32, 32).transpose(1, 0, 2).reshape(32, 128)]
  transfers between devices with their start and end apart: 22 -> 9, of which waited for: 17 -> 9; matrix products, arithmetic and copies ran while one was open for 11% -> 4% of each run, Pallas kernels for 0% -> 0%
where the time goes in v1:
time: 1860 us; the launch traced here: 1850 us
  waiting for transfers between devices  1390 us (75%)
  Pallas kernels  194 us (10%)
  matrix products  156 us (8%)
  local copies, waits for them, and re-layouts  63.2 us (3%)
  other arithmetic  30 us (2%)
    reduce_scatter x2, waiting for transfers between devices, device_step(): scatter(dot_g(act, d_out))  371 us
    reduce_scatter x2, waiting for transfers between devices, device_step(): scatter(dot_g(h2, d_pre))  366 us
    reduce_scatter x2, waiting for transfers between devices, device_step(): g_qkv = scatter(dot_g(h1, d_proj))  312 us
    reduce_scatter x2, waiting for transfers between devices, device_step(): g_o = scatter(dot_g(ctx, d_mid))  284 us
    pallas_call x1, Pallas kernels, gather_weights(): pl.pallas_call(gather_kernel, out_shape=(jax.ShapeDtypeStruct((LAYERS, 4,...  194 us
    unnamed x10, waiting for transfers between devices  58.4 us
    dot_general x8, matrix products, dot_g(): lax.dot_general(a, b, (((0,), (0,)), ((), ())), preferred_element_type=jn...  57.2 us
    dot_general x12, matrix products, dot_t(): lax.dot_general(a, b, (((1,), (1,)), ((), ())), preferred_element_type=jn...  44.8 us
  transfers between devices with their start and end apart: 9, of which 9 were waited for; matrix products, arithmetic and copies ran while one was open for 4% of the time, Pallas kernels for 0%

profile of v1, /device:TPU:0, one launch (start us, length us, event | category | flops | bytes accessed | tf_op | source)
XLA Modules:
  0.0 1851.8 jit_solution(17057483634672081074)
XLA Ops:
  10.7 194.0 %gather_weights.1 = (bf16[2,4,1024,1024]{3,2,1,0:T(8,128)(2,1)}, bf16[2,1024,4096]{2,1,0:T(8,128)(2,1)}, bf16[8192,1024]{1,0:T(8,128)(2,1)}, bf16[256,128]{1,0:T(8,128)(2,1)}) custom-call(bf16[2,4,32,1024]{3,2,1,0:T(8,128)(2,1)} %wa.1, bf16[2,32,4096]{2,1,0:T(8,128)(2,1)} %wu.1, bf16[2,128,1024]{2,1,0:T(8,128)(2,1)} %wd.1, bf16[8,128]{1,0:T(8,128)(2,1)} %bitcast.342), custom_call_target="tpu_custom_call" | custom-call | tf_op jit(solution)/shard_map/gather_weights/pallas_call | solution.py:212
  236.6 12.4 fusion.41
  279.0 5.4 fusion.32
  284.5 8.1 fusion.347
  292.6 3.6 multiply_reduce_fusion
  298.2 3.2 fusion.232
  317.5 3.3 multiply_reduce_fusion.1
  322.8 7.1 fusion.346
  330.6 3.6 multiply_reduce_fusion.2
  372.8 7.4 fusion.269
  384.6 6.5 fusion.270
  396.7 8.2 fusion.263
  406.6 8.2 fusion.266
  415.8 13.4 fusion.121
  430.7 8.1 fusion.350
  441.0 58.3 %all-reduce.4.cloned.1.call-done = f32[32,832]{1,0:T(8,128)} async-done(((f32[32,832]{1,0:T(8,128)}), f32[32,832]{1,0:T(8,128)}) %all-reduce.4.cloned.1.call-update) | async-done | bytes 106512
  502.6 156.3 %reduce-scatter.13.cloned.1.call-done = f32[32,3072]{1,0:T(8,128)} async-done(((f32[1024,3072]{1,0:T(8,128)}), f32[32,3072]{1,0:T(8,128)}) %reduce-scatter.13.cloned.1.call-update) | async-done | bytes 393232 | tf_op jit(solution)/shard_map/reduce_scatter | solution.py:375
  659.9 142.1 %reduce-scatter.15.cloned.1.call-done = f32[32,1024]{1,0:T(8,128)} async-done(((f32[1024,1024]{1,0:T(8,128)}), f32[32,1024]{1,0:T(8,128)}) %reduce-scatter.15.cloned.1.call-update) | async-done | bytes 131088 | tf_op jit(solution)/shard_map/reduce_scatter | solution.py:376
  802.9 155.3 %reduce-scatter.9.cloned.1.call-done = f32[32,3072]{1,0:T(8,128)} async-done(((f32[1024,3072]{1,0:T(8,128)}), f32[32,3072]{1,0:T(8,128)}) %reduce-scatter.9.cloned.1.call-update) | async-done | bytes 393232 | tf_op jit(solution)/shard_map/reduce_scatter | solution.py:375
  959.3 141.9 %reduce-scatter.11.cloned.1.call-done = f32[32,1024]{1,0:T(8,128)} async-done(((f32[1024,1024]{1,0:T(8,128)}), f32[32,1024]{1,0:T(8,128)}) %reduce-scatter.11.cloned.1.call-update) | async-done | bytes 131088 | tf_op jit(solution)/shard_map/reduce_scatter | solution.py:376
  1103.3 178.8 %reduce-scatter.17.cloned.1.call-done = f32[32,4096]{1,0:T(8,128)} async-done(((f32[1024,4096]{1,0:T(8,128)}), f32[32,4096]{1,0:T(8,128)}) %reduce-scatter.17.cloned.1.call-update) | async-done | bytes 524304 | tf_op jit(solution)/shard_map/reduce_scatter | solution.py:378
  1282.0 186.8 %reduce-scatter.19.cloned.1.call-done = f32[32,4096]{1,0:T(8,128)} async-done(((f32[1024,4096]{1,0:T(8,128)}), f32[32,4096]{1,0:T(8,128)}) %reduce-scatter.19.cloned.1.call-update) | async-done | bytes 524304 | tf_op jit(solution)/shard_map/reduce_scatter | solution.py:378
  1471.1 184.6 %reduce-scatter.23.cloned.1.call-done = f32[128,1024]{1,0:T(8,128)} async-done(((f32[4096,1024]{1,0:T(8,128)}), f32[128,1024]{1,0:T(8,128)}) %reduce-scatter.23.cloned.1.call-update) | async-done | bytes 524304 | tf_op jit(solution)/shard_map/reduce_scatter | solution.py:378
  1655.7 186.8 %reduce-scatter.21.cloned.1.call-done = f32[128,1024]{1,0:T(8,128)} async-done(((f32[4096,1024]{1,0:T(8,128)}), f32[128,1024]{1,0:T(8,128)}) %reduce-scatter.21.cloned.1.call-update) | async-done | bytes 524304 | tf_op jit(solution)/shard_map/reduce_scatter | solution.py:378
  (459 shorter events, 151.6 us)
Async XLA Ops:
  7.2 212.8 %copy-start.6 = (bf16[1,192,1024]{2,1,0:T(8,128)(2,1)S(1)}, bf16[1,192,1024]{2,1,0:T(8,128)(2,1)}, u32[]{:S(2)}) copy-start(bf16[1,192,1024]{2,1,0:T(8,128)(2,1)} %param.10) | copy-start | bytes 1179652
  7.2 492.1 %all-reduce.4.cloned.1.call-start = ((), (), s32[]{:S(2)}) async-start(), calls=%async_computation.16 | async-start | bytes 229376
  209.6 16.2 copy-start.76
  210.8 14.9 copy-start.80
  211.6 16.7 copy-start.56
  211.6 16.7 copy-start.67
  233.1 15.9 slice-start.8
  235.7 13.4 copy-start.7
  235.7 13.3 copy-start.86
  235.9 13.1 copy-start.91
  278.7 17.6 copy-start.12
  278.7 17.6 copy-start.89
  279.0 17.3 copy-start.94
  279.0 13.6 slice-start
  279.0 13.6 slice-start.1
  322.0 12.6 copy-start.31
  372.5 286.4 %reduce-scatter.13.cloned.1.call-start = ((), (), s32[]{:S(2)}) async-start(), calls=%async_computation.10 | async-start | bytes 12976128 | tf_op jit(solution)/shard_map/reduce_scatter | solution.py:375
  380.2 421.8 %reduce-scatter.15.cloned.1.call-start = ((), (), s32[]{:S(2)}) async-start(), calls=%async_computation.11 | async-start | bytes 4325376 | tf_op jit(solution)/shard_map/reduce_scatter | solution.py:376
  384.0 574.2 %reduce-scatter.9.cloned.1.call-start = ((), (), s32[]{:S(2)}) async-start(), calls=%async_computation.8 | async-start | bytes 12976128 | tf_op jit(solution)/shard_map/reduce_scatter | solution.py:375
  391.2 710.0 %reduce-scatter.11.cloned.1.call-start = ((), (), s32[]{:S(2)}) async-start(), calls=%async_computation.9 | async-start | bytes 4325376 | tf_op jit(solution)/shard_map/reduce_scatter | solution.py:376
  395.1 887.0 %reduce-scatter.17.cloned.1.call-start = ((), (), s32[]{:S(2)}) async-start(), calls=%async_computation.12 | async-start | bytes 17301504 | tf_op jit(solution)/shard_map/reduce_scatter | solution.py:378
  404.9 1063.9 %reduce-scatter.19.cloned.1.call-start = ((), (), s32[]{:S(2)}) async-start(), calls=%async_computation.13 | async-start | bytes 17301504 | tf_op jit(solution)/shard_map/reduce_scatter | solution.py:378
  414.8 1240.9 %reduce-scatter.23.cloned.1.call-start = ((), (), s32[]{:S(2)}) async-start(), calls=%async_computation.15 | async-start | bytes 17301504 | tf_op jit(solution)/shard_map/reduce_scatter | solution.py:378
  429.2 1413.4 %reduce-scatter.21.cloned.1.call-start = ((), (), s32[]{:S(2)}) async-start(), calls=%async_computation.14 | async-start | bytes 17301504 | tf_op jit(solution)/shard_map/reduce_scatter | solution.py:378
  (126 other events, 411.4 us)
Sparse Core Ops, SparseCore 0:
  372.6 126.6 all-reduce.3
  505.3 153.5 reduce-scatter.12
  661.2 140.7 reduce-scatter.14
  807.9 150.3 reduce-scatter.8
  960.4 140.8 reduce-scatter.10
  1103.4 178.5 reduce-scatter.16
  1284.3 184.4 reduce-scatter.18
  1471.2 184.4 reduce-scatter.22
  1658.0 184.5 reduce-scatter.20

commit v2 on v1

--- a/solution.py
+++ b/solution.py
@@ -7,6 +7,21 @@
 from jax.experimental.pallas import tpu as pltpu
 from jax.sharding import PartitionSpec as P
 
+LINE = 4
+PLANE = 8
+HEADS = 16
+SHARD = 32
+HEAD_DIM = 64
+HALF_SEQ = 96
+TILE = 128
+SEQ = 192
+SPREAD = 224
+BAND = 256
+WIDE = 512
+DIM = 1024
+FAR = 1344
+FFN = 4096
+
 MESH = pl.DeviceIdType.MESH
 LAYERS = 2
 ORDERS = (("b", 0, 1), ("b", 1, 0), ("a", 0, 1), ("a", 1, 0), ("b", 0, 1), ("b", 1, 0))
@@ -18,30 +33,30 @@
 def gather_kernel(wa, wu, wd, sm, fa, fu, fd, fs, va, vu, vd, vs, load_sem, own_sem, xy_sem, z_sem,
                   push_send, push_recv, recv_sem):
     me = lax.axis_index("fsdp")
-    core, xc, yc, zc = me % 2, (me // 2) % 2, (me // 4) % 2, me // 8
+    core, xc, yc, zc = me % 2, (me // 2) % 2, (me // LINE) % 2, me // PLANE
     partner = me + 1 - 2 * core
-    near = (me + 2 - 4 * xc, me + 4 - 8 * yc)
-    up, down = me + 8, me - 8
+    near = (me + 2 - LINE * xc, me + LINE - PLANE * yc)
+    up, down = me + PLANE, me - PLANE
     has_up, has_down = zc < 3, zc > 0
 
     def full(u, src):
         layer, piece = UNITS[u]
         if piece < 2:
-            return fa.at[layer, pl.ds(2 * piece, 2), pl.ds(pl.multiple_of(32 * src, 32), 32), :]
-        if piece < 4:
-            return fu.at[layer, pl.ds(pl.multiple_of(32 * src + 16 * (piece - 2), 16), 16), :]
+            return fa.at[layer, pl.ds(2 * piece, 2), pl.ds(pl.multiple_of(SHARD * src, SHARD), SHARD), :]
+        if piece < LINE:
+            return fu.at[layer, pl.ds(pl.multiple_of(SHARD * src + HEADS * (piece - 2), HEADS), HEADS), :]
         if piece < 6:
-            return fd.at[pl.ds(pl.multiple_of(4096 * layer + 128 * src + 64 * (piece - 4), 64), 64), :]
-        return fs.at[pl.ds(pl.multiple_of(8 * src, 8), 8), :]
+            return fd.at[pl.ds(pl.multiple_of(FFN * layer + TILE * src + HEAD_DIM * (piece - LINE), HEAD_DIM), HEAD_DIM), :]
+        return fs.at[pl.ds(pl.multiple_of(PLANE * src, PLANE), PLANE), :]
 
     def own(u):
         layer, piece = UNITS[u]
         if piece < 2:
             return va.at[layer, pl.ds(2 * piece, 2)]
-        if piece < 4:
-            return vu.at[layer, pl.ds(16 * (piece - 2), 16), :]
+        if piece < LINE:
+            return vu.at[layer, pl.ds(HEADS * (piece - 2), HEADS), :]
         if piece < 6:
-            return vd.at[layer, pl.ds(64 * (piece - 4), 64), :]
+            return vd.at[layer, pl.ds(HEAD_DIM * (piece - LINE), HEAD_DIM), :]
         return vs
 
     def kind(u):
@@ -94,7 +109,7 @@
         remote(u, src_ref, src, push_send.at[kind(u)], push_recv.at[kind(u)], partner).start()
 
     def column(flip_p, p):
-        base = me - 8 * zc
+        base = me - PLANE * zc
         if flip_p:
             base = base + (near[p] - me)
         return base
@@ -107,8 +122,8 @@
         col, p, q = order(u)
         mine = own(u)
         send_z(u, mine, me, zc, has_up, has_down)
-        send_xy(u, mine, me, p, 4 + zc)
-        send_xy(u, mine, me, q, 8)
+        send_xy(u, mine, me, p, LINE + zc)
+        send_xy(u, mine, me, q, PLANE)
         push(u, mine, me)
         pltpu.make_async_copy(mine, full(u, me), own_sem.at[kind(u)]).start()
 
@@ -118,8 +133,8 @@
             for step in (-1, 1):
                 for flip_p in flips:
                     zs = zc + step * dz
-                    src = column(flip_p, p) + 8 * zs
-                    slot = 4 * flip_p + zs
+                    src = column(flip_p, p) + PLANE * zs
+                    slot = LINE * flip_p + zs
                     present = (zc >= dz) if step < 0 else (zc <= 3 - dz)
 
                     @pl.when(present)
@@ -127,8 +142,8 @@
                         ref = arrived(u, src, slot)
                         send_z(u, ref, src, slot, has_up if step < 0 else None, has_down if step > 0 else None)
                         if send_p:
-                            send_xy(u, ref, src, p, 4 + slot)
-                        send_xy(u, ref, src, q, 8)
+                            send_xy(u, ref, src, p, LINE + slot)
+                        send_xy(u, ref, src, q, PLANE)
                         push(u, ref, src)
 
     def stage1(u):
@@ -137,41 +152,41 @@
             z_arrivals(u, (0,), True)
         else:
             src = near[p]
-            ref = arrived(u, src, 4 + zc)
-            send_z(u, ref, src, 4 + zc, has_up, has_down)
-            send_xy(u, ref, src, q, 8)
+            ref = arrived(u, src, LINE + zc)
+            send_z(u, ref, src, LINE + zc, has_up, has_down)
+            send_xy(u, ref, src, q, PLANE)
             push(u, ref, src)
 
     def stage2(u):
         col, p, q = order(u)
         if col == "a":
-            for hop in range(4):
-                zs = lax.rem(zc + hop, 4)
-                src = column(1, p) + 8 * zs
-                ref = arrived(u, src, 4 + zs)
-                send_xy(u, ref, src, q, 8)
+            for hop in range(LINE):
+                zs = lax.rem(zc + hop, LINE)
+                src = column(1, p) + PLANE * zs
+                ref = arrived(u, src, LINE + zs)
+                send_xy(u, ref, src, q, PLANE)
                 push(u, ref, src)
         else:
             z_arrivals(u, (0, 1), False)
 
     def stage3(u):
         col, p, q = order(u)
-        rows = fs.at[pl.ds(0, 64), :] if tiny(u) else fd.at[pl.ds(0, 512), :]
-        pltpu.make_async_copy(rows, rows, recv_sem.at[u, 8]).wait()
+        rows = fs.at[pl.ds(0, HEAD_DIM), :] if tiny(u) else fd.at[pl.ds(0, WIDE), :]
+        pltpu.make_async_copy(rows, rows, recv_sem.at[u, PLANE]).wait()
         for flip_p in (0, 1):
             base = column(flip_p, p) + (near[q] - me)
 
             def body(zs, carry, base=base):
-                src = base + 8 * zs
+                src = base + PLANE * zs
                 push(u, full(u, src), src)
                 return carry
 
-            lax.fori_loop(0, 4, body, 0)
+            lax.fori_loop(0, LINE, body, 0)
 
     stages = (stage0, stage1, stage2, stage3)
     count = len(UNITS)
     for rnd in range(count + STAGE_LAG[3]):
-        for k in range(4):
+        for k in range(LINE):
             if k == 0:
                 todo = range(AHEAD + 1) if rnd == 0 else [rnd + AHEAD]
             else:
@@ -183,22 +198,22 @@
     def drain(ref, sem):
         pltpu.make_async_copy(ref, ref, sem).wait()
 
-    per_layer = 64 * LAYERS
+    per_layer = HEAD_DIM * LAYERS
     drain(fd.at[pl.ds(0, 60 * per_layer), :], xy_sem.at[0])
-    drain(fs.at[pl.ds(0, 9 * 8), :], xy_sem.at[1])
+    drain(fs.at[pl.ds(0, 9 * PLANE), :], xy_sem.at[1])
     ends = jnp.logical_or(zc == 0, zc == 3)
 
     @pl.when(ends)
     def _():
         drain(fd.at[pl.ds(0, 10 * per_layer), :], z_sem.at[0])
-        drain(fs.at[pl.ds(0, 2 * 8), :], z_sem.at[1])
+        drain(fs.at[pl.ds(0, 2 * PLANE), :], z_sem.at[1])
 
     @pl.when(jnp.logical_not(ends))
     def _():
         drain(fd.at[pl.ds(0, 50 * per_layer), :], z_sem.at[0])
-        drain(fs.at[pl.ds(0, 10 * 8), :], z_sem.at[1])
-
-    halves = (fa.at[0], fu.at[0], fd.at[pl.ds(0, 4096), :], fs.at[pl.ds(0, 128), :])
+        drain(fs.at[pl.ds(0, 10 * PLANE), :], z_sem.at[1])
+
+    halves = (fa.at[0], fu.at[0], fd.at[pl.ds(0, FFN), :], fs.at[pl.ds(0, TILE), :])
     for i, half in enumerate(halves):
         drain(half, push_send.at[i])
         drain(half, push_recv.at[i])
@@ -211,20 +226,19 @@
     dt = jnp.bfloat16
     return pl.pallas_call(
         gather_kernel,
-        out_shape=(jax.ShapeDtypeStruct((LAYERS, 4, 1024, 1024), dt), jax.ShapeDtypeStruct((LAYERS, 1024, 4096), dt),
-                   jax.ShapeDtypeStruct((LAYERS * 4096, 1024), dt), jax.ShapeDtypeStruct((32 * 8, 128), dt)),
-        in_specs=[pl.BlockSpec(memory_space=pltpu.HBM)] * 4,
-        out_specs=[pl.BlockSpec(memory_space=pltpu.HBM)] * 4,
+        out_shape=(jax.ShapeDtypeStruct((LAYERS, LINE, DIM, DIM), dt), jax.ShapeDtypeStruct((LAYERS, DIM, FFN), dt),
+                   jax.ShapeDtypeStruct((LAYERS * FFN, DIM), dt), jax.ShapeDtypeStruct((SHARD * PLANE, TILE), dt)),
+        in_specs=[pl.BlockSpec(memory_space=pltpu.HBM)] * LINE,
+        out_specs=[pl.BlockSpec(memory_space=pltpu.HBM)] * LINE,
         scratch_shapes=[pltpu.VMEM(s, dt) for s in shapes] + [
-            pltpu.SemaphoreType.DMA((4,)), pltpu.SemaphoreType.DMA((4,)), pltpu.SemaphoreType.DMA((2,)),
-            pltpu.SemaphoreType.DMA((2,)), pltpu.SemaphoreType.DMA((4,)), pltpu.SemaphoreType.DMA((4,)),
+            pltpu.SemaphoreType.DMA((LINE,)), pltpu.SemaphoreType.DMA((LINE,)), pltpu.SemaphoreType.DMA((2,)),
+            pltpu.SemaphoreType.DMA((2,)), pltpu.SemaphoreType.DMA((LINE,)), pltpu.SemaphoreType.DMA((LINE,)),
             pltpu.SemaphoreType.DMA((len(UNITS), 9))],
         compiler_params=pltpu.CompilerParams(collective_id=0, has_side_effects=True),
         name="gather_weights",
     )(w_attn, w_up, w_down, small)
 
 
-HEAD_DIM = 64
 EPS = 1e-5
 THETA = 10000.0
 NEG_BIG = -1e30
@@ -329,28 +343,312 @@
         rotate_back(d_key, cos_tab, sin_tab).astype(jnp.bfloat16).reshape(seq_len, -1),
         d_values.astype(jnp.bfloat16).reshape(seq_len, -1)], axis=1)
     gb_qkv = jnp.sum(d_proj, axis=0, dtype=jnp.float32)
-    d_h_one = sum(dot_t(d_proj[:, 1024 * i:1024 * i + 1024], w_attn[i]) for i in range(3))
+    d_h_one = sum(dot_t(d_proj[:, DIM * i:DIM * i + DIM], w_attn[i]) for i in range(3))
     _, norm_pull_one = jax.vjp(norm_fwd, x.astype(jnp.float32), ln_par[0], ln_par[1])
     d_x_norm, g_gain_one, g_shift_one = norm_pull_one(d_h_one)
     d_x = (d_mid.astype(jnp.float32) + d_x_norm).astype(jnp.bfloat16)
-    small = (jnp.concatenate([gb_qkv, gb_out]).reshape(4, -1),
+    small = (jnp.concatenate([gb_qkv, gb_out]).reshape(LINE, -1),
              jnp.stack([g_gain_one, g_shift_one, g_gain_two, g_shift_two]), gb_up, gb_down)
     return d_x, (h_one, context, h_two, act_bf, d_proj, d_mid, d_pre_bf, d_out), small
 
 
 def pack_small(b_attn, ln_par, b_up, b_down):
-    rows = [b_attn.reshape(2, 128), ln_par.reshape(2, 128), b_up, jnp.pad(b_down, ((0, 0), (0, 96)))]
-    return jnp.stack(rows, axis=1).reshape(8, 128)
+    rows = [b_attn.reshape(2, TILE), ln_par.reshape(2, TILE), b_up, jnp.pad(b_down, ((0, 0), (0, HALF_SEQ)))]
+    return jnp.stack(rows, axis=1).reshape(PLANE, TILE)
 
 
 def unpack_small(gathered):
-    rows = gathered.reshape(32, 2, 4, 128).astype(jnp.float32)
+    rows = gathered.reshape(SHARD, 2, LINE, TILE).astype(jnp.float32)
 
     def fours(row):
-        return row.reshape(32, 4, 32).transpose(1, 0, 2).reshape(4, 1024)
-
-    return [(fours(rows[:, l, 0]), fours(rows[:, l, 1]), rows[:, l, 2].reshape(4096), rows[:, l, 3, :32].reshape(1024))
+        return row.reshape(SHARD, LINE, SHARD).transpose(1, 0, 2).reshape(LINE, DIM)
+
+    return [(fours(rows[:, l, 0]), fours(rows[:, l, 1]), rows[:, l, 2].reshape(FFN), rows[:, l, 3, :SHARD].reshape(DIM))
             for l in range(2)]
+
+
+PIECES = [(layer, name) for layer in (1, 0) for name in "DUOQ"]
+WIDTH = {"D": WIDE, "U": WIDE, "O": TILE, "Q": 384}
+ROWS = SEQ
+LAG = (1, 2, 3)
+
+
+def acc_shape(name):
+    return (WIDE, DIM) if name == "D" else (DIM, WIDTH[name])
+
+
+def grad_kernel(*refs):
+    n = len(PIECES)
+    bc_in, sl_in, sums = refs[:n], refs[n:2 * n], refs[2 * n]
+    refs = refs[2 * n + 1:]
+    g_attn, g_up, g_down, g_small, bc_far = refs[:5]
+    sl_far = refs[5:5 + n]
+    refs = refs[5 + n:]
+    bc_v, sl_v = refs[:2]
+    acc, got = refs[2:2 + n], refs[2 + n:2 + 2 * n]
+    sum_v, sum_got, sum_line = refs[2 + 2 * n:5 + 2 * n]
+    (bc_send, bc_recv, push_send, push_recv, sl_send, sl_recv, load_sem, rs_send, rs_recv, out_send, out_recv, own_sem,
+     sum_send, sum_recv) = refs[5 + 2 * n:]
+
+    me = lax.axis_index("fsdp")
+    core, xc, yc, zc = me % 2, (me // 2) % 2, (me // LINE) % 2, me // PLANE
+    place = me % PLANE
+
+    def peer(r):
+        out = me
+        if r & 1:
+            out = out + 1 - 2 * core
+        if r & 2:
+            out = out + 2 - LINE * xc
+        if r & LINE:
+            out = out + LINE - PLANE * yc
+        return out
+
+    def line(k):
+        return place + PLANE * lax.rem(zc + k, LINE)
+
+    def remote(src, dst, send, recv, dev):
+        return pltpu.make_async_remote_copy(src_ref=src, dst_ref=dst, send_sem=send, recv_sem=recv,
+                                            device_id=(dev,), device_id_type=MESH)
+
+    def local(src, dst, sem):
+        return pltpu.make_async_copy(src, dst, sem)
+
+    def drain(ref, sem):
+        local(ref, ref, sem).wait()
+
+    barrier = pltpu.get_barrier_semaphore()
+    for r in range(1, PLANE):
+        pl.semaphore_signal(barrier, inc=1, device_id=(peer(r),), device_id_type=MESH)
+    for k in range(1, LINE):
+        pl.semaphore_signal(barrier, inc=1, device_id=(line(k),), device_id_type=MESH)
+    local(sums, sum_v, load_sem.at[0]).start()
+    drain(sum_v, load_sem.at[0])
+    pl.semaphore_wait(barrier, 10)
+
+    def far(u, r, half=None):
+        start = FAR * u + SEQ * (r - 1)
+        return bc_far.at[pl.ds(start, SEQ), :] if half is None else bc_far.at[pl.ds(start + HALF_SEQ * half, HALF_SEQ), :]
+
+    def blocks(u, where):
+        name = PIECES[u][1]
+        if name == "D":
+            return [(pl.multiple_of(DIM * i + TILE * where, TILE), TILE * i, TILE) for i in range(LINE)]
+        if name == "Q":
+            return [(pl.multiple_of(DIM * i + TILE * where, TILE), TILE * i, TILE) for i in range(3)]
+        return [(pl.multiple_of(WIDTH[name] * where, TILE), 0, WIDTH[name])]
+
+    def send_bc(u):
+        for r in (2, LINE):
+            for half in (0, 1):
+                slot = (0 if r == 2 else 2) + half
+                remote(bc_in[u].at[pl.ds(HALF_SEQ * half, HALF_SEQ), :], far(u, r, half), bc_send, bc_recv.at[u, slot], peer(r)).start()
+        remote(bc_in[u], far(u, 1), push_send, push_recv.at[u], peer(1)).start()
+
+    def send_sl(u):
+        for r in (2, 6, LINE, 3, 7, 5, 1):
+            for src, dst, width in blocks(u, peer(r) % PLANE):
+                remote(sl_in[u].at[:, pl.ds(src, width)], sl_far[u].at[pl.ds(SEQ * (r - 1), SEQ), pl.ds(dst, width)],
+                       sl_send.at[u], sl_recv.at[u], peer(r)).start()
+
+    def push(u, r, half):
+        remote(far(u, r, half), far(u, r + 1, half), push_send, push_recv.at[u], peer(1)).start()
+
+    def relay_bc(u):
+        for slot, r, half, onward in ((0, 2, 0, LINE), (3, LINE, 1, 2), (1, 2, 1, None), (2, LINE, 0, None)):
+            drain(far(u, r, half), bc_recv.at[u, slot])
+            if onward is not None:
+                remote(far(u, r, half), far(u, 6, half), bc_send, bc_recv.at[u, LINE + half], peer(onward)).start()
+            push(u, r, half)
+
+    def collect(u):
+        name = PIECES[u][1]
+        own = [local(bc_in[u], bc_v.at[pl.ds(0, SEQ), :], load_sem.at[0])]
+        for i, (src, dst, width) in enumerate(blocks(u, place)):
+            own.append(local(sl_in[u].at[:, pl.ds(src, width)], sl_v.at[pl.ds(0, SEQ), pl.ds(dst, width)],
+                             load_sem.at[1 + i]))
+        for c in own:
+            c.start()
+        for half in (0, 1):
+            drain(far(u, 6, half), bc_recv.at[u, LINE + half])
+            push(u, 6, half)
+        drain(sl_far[u], sl_recv.at[u])
+        drain(bc_far.at[pl.ds(0, 768), :], push_recv.at[u])
+        rest = [local(bc_far.at[pl.ds(FAR * u, FAR), :], bc_v.at[pl.ds(SEQ, FAR), :], load_sem.at[5]),
+                local(sl_far[u], sl_v.at[pl.ds(SEQ, FAR), pl.ds(0, WIDTH[name])], load_sem.at[6])]
+        for c in rest:
+            c.start()
+        for c in own + rest:
+            c.wait()
+
+    def piece_rows(u):
+        return acc_shape(PIECES[u][1])[0] // LINE
+
+    def piece(ref, u, d):
+        pr = piece_rows(u)
+        return ref.at[pl.ds(pl.multiple_of(pr * d, pr), pr), :]
+
+    def step_down_line(u, d, up):
+        side = jnp.where(up, 0, 1)
+        dst = got[u].at[side, pl.ds(pl.multiple_of(piece_rows(u) * d, piece_rows(u)), piece_rows(u)), :]
+        remote(piece(acc[u], u, d), dst, rs_send.at[u], rs_recv.at[u, side, d], me + jnp.where(up, PLANE, -PLANE)).start()
+
+    def add_piece(u, side, d):
+        pr = piece_rows(u)
+        drain(piece(acc[u], u, d), rs_recv.at[u, side, d])
+        rows = SHARD
+
+        def body(i, carry):
+            at = pl.ds(pl.multiple_of(pr * d + rows * i, rows), rows)
+            acc[u][at, :] = acc[u][at, :] + got[u][side, at, :]
+            return carry
+
+        lax.fori_loop(0, pr // rows, body, 0)
+
+    def product(u):
+        name = PIECES[u][1]
+        pr, width = piece_rows(u), WIDTH[name]
+
+        def body(d, carry):
+            at = pl.ds(pl.multiple_of(pr * d, pr), pr)
+            if name == "D":
+                lhs, rhs = sl_v[:, at], bc_v[...]
+            else:
+                lhs, rhs = bc_v[:, at], sl_v[:, pl.ds(0, width)]
+            acc[u][at, :] = lax.dot_general(lhs, rhs, (((0,), (0,)), ((), ())), preferred_element_type=jnp.float32)
+            return carry
+
+        lax.fori_loop(0, LINE, body, 0)
+
+        @pl.when(jnp.logical_or(zc == 0, zc == 3))
+        def _():
+            for hop in range(3):
+                step_down_line(u, jnp.where(zc == 0, 3 - hop, hop), zc == 0)
+
+    def second_hop(u):
+        @pl.when(jnp.logical_or(zc == 1, zc == 2))
+        def _():
+            for hop in range(2):
+                d = jnp.where(zc == 1, 3 - hop, hop)
+                add_piece(u, jnp.where(zc == 1, 0, 1), d)
+                step_down_line(u, d, zc == 1)
+
+    def third_hop(u):
+        @pl.when(jnp.logical_or(zc == 1, zc == 2))
+        def _():
+            d = jnp.where(zc == 1, 0, 3)
+            add_piece(u, jnp.where(zc == 1, 1, 0), d)
+            step_down_line(u, d, zc == 2)
+
+    def finish(u):
+        layer, name = PIECES[u]
+
+        @pl.when(zc > 0)
+        def _():
+            add_piece(u, 0, zc)
+
+        @pl.when(zc < 3)
+        def _():
+            add_piece(u, 1, zc)
+
+        if name == "D":
+            local(piece(acc[u], u, zc), g_down.at[layer], own_sem.at[u]).start()
+            return
+        for r in range(PLANE):
+            at = pl.ds(pl.multiple_of(BAND * zc + SHARD * (peer(r) % PLANE), SHARD), SHARD)
+            if name == "U":
+                pairs = [(acc[u].at[at, :], g_up.at[layer, :, pl.ds(pl.multiple_of(WIDE * place, WIDE), WIDE)])]
+            else:
+                mats = (3,) if name == "O" else (0, 1, 2)
+                pairs = [(acc[u].at[at, pl.ds(TILE * i, TILE)],
+                          g_attn.at[layer, m, :, pl.ds(pl.multiple_of(TILE * place, TILE), TILE)]) for i, m in enumerate(mats)]
+            for src, dst in pairs:
+                if r == 0:
+                    local(src, dst, own_sem.at[u]).start()
+                else:
+                    remote(src, dst, out_send.at[u], out_recv.at[u], peer(r)).start()
+
+    def sums_plane():
+        for r in range(1, PLANE):
+            remote(sum_v.at[pl.ds(pl.multiple_of(SHARD * (peer(r) % PLANE), SHARD), SHARD), :], sum_got.at[pl.ds(SHARD * (r - 1), SHARD), :],
+                   sum_send.at[0], sum_recv.at[0], peer(r)).start()
+
+    def sums_line():
+        drain(sum_got, sum_recv.at[0])
+        total = sum_v[pl.ds(pl.multiple_of(SHARD * place, SHARD), SHARD), :]
+        for r in range(1, PLANE):
+            total = total + sum_got[pl.ds(SHARD * (r - 1), SHARD), :]
+        sum_line[pl.ds(0, SHARD), :] = total
+        for k in range(1, LINE):
+            remote(sum_line.at[pl.ds(pl.multiple_of(PLANE * lax.rem(zc + k, LINE), PLANE), PLANE), :],
+                   sum_line.at[pl.ds(SHARD + PLANE * (k - 1), PLANE), :], sum_send.at[1], sum_recv.at[1], line(k)).start()
+
+    def sums_end():
+        drain(sum_line.at[pl.ds(0, 24), :], sum_recv.at[1])
+        total = sum_line[pl.ds(pl.multiple_of(PLANE * zc, PLANE), PLANE), :]
+        for k in range(1, LINE):
+            total = total + sum_line[pl.ds(SHARD + PLANE * (k - 1), PLANE), :]
+        g_small[...] = total
+
+    send_bc(0)
+    relay_bc(0)
+    send_sl(0)
+    sums_plane()
+    send_bc(1)
+    for s in range(n + LAG[2]):
+        if s < n:
+            if s + 1 < n:
+                relay_bc(s + 1)
+                send_sl(s + 1)
+            if s + 2 < n:
+                send_bc(s + 2)
+            collect(s)
+            product(s)
+        for lag, hop in zip(LAG, (second_hop, third_hop, finish)):
+            if 0 <= s - lag < n:
+                hop(s - lag)
+        if s == 0:
+            sums_line()
+        if s == 1:
+            sums_end()
+
+    drain(bc_far.at[pl.ds(0, n * 576), :], bc_send)
+    drain(bc_far.at[pl.ds(0, n * 768), :], push_send)
+    drain(sum_got, sum_send.at[0])
+    drain(sum_line.at[pl.ds(0, 24), :], sum_send.at[1])
+    for u in range(n):
+        name = PIECES[u][1]
+        drain(sl_far[u], sl_send.at[u])
+        drain(acc[u].at[pl.ds(0, 3 * piece_rows(u)), :], rs_send.at[u])
+        if name == "D":
+            drain(acc[u].at[pl.ds(0, TILE), :], own_sem.at[u])
+        else:
+            drain(acc[u].at[pl.ds(0, SHARD), :], own_sem.at[u])
+            drain(acc[u].at[pl.ds(0, SPREAD), :], out_send.at[u])
+            drain(acc[u].at[pl.ds(0, SPREAD), :], out_recv.at[u])
+
+
+def reduce_grads(bc, sl, sums):
+    n = len(PIECES)
+    f32, bf16, dma = jnp.float32, jnp.bfloat16, pltpu.SemaphoreType.DMA
+    hbm = pl.BlockSpec(memory_space=pltpu.HBM)
+    shape = jax.ShapeDtypeStruct
+    outs = pl.pallas_call(
+        grad_kernel,
+        out_shape=[shape((2, LINE, SHARD, DIM), f32), shape((2, SHARD, FFN), f32), shape((2, TILE, DIM), f32), shape((PLANE, TILE), f32),
+                   shape((n * FAR, DIM), bf16)] + [shape((FAR, WIDTH[name]), bf16) for _, name in PIECES],
+        in_specs=[hbm] * (2 * n + 1),
+        out_specs=[hbm] * 3 + [pl.BlockSpec(memory_space=pltpu.VMEM)] + [hbm] * (n + 1),
+        scratch_shapes=[pltpu.VMEM((1536, DIM), bf16), pltpu.VMEM((1536, WIDE), bf16)]
+        + [pltpu.VMEM(acc_shape(name), f32) for _, name in PIECES]
+        + [pltpu.VMEM((2,) + acc_shape(name), f32) for _, name in PIECES]
+        + [pltpu.VMEM((BAND, TILE), f32), pltpu.VMEM((SPREAD, TILE), f32), pltpu.VMEM((56, TILE), f32)]
+        + [dma, dma((n, 6)), dma, dma((n,)), dma((n,)), dma((n,)), dma((7,)), dma((n,)), dma((n, 2, LINE)),
+           dma((n,)), dma((n,)), dma((n,)), dma((2,)), dma((2,))],
+        compiler_params=pltpu.CompilerParams(collective_id=1, has_side_effects=True, vmem_limit_bytes=58 * DIM * DIM),
+        name="reduce_grads",
+    )(*bc, *sl, sums)
+    return outs[:LINE]
 
 
 def solution(mesh):
@@ -363,27 +661,25 @@
         tables = rotary_tables(x.shape[1])
         fa, fu, fd, fs = gather_weights(w_attn, w_up, w_down, pack_small(b_attn, ln_par, b_up, b_down))
         smalls = unpack_small(fs)
-        weights = [(fa[l], fu[l], fd[4096 * l:4096 * l + 4096]) + smalls[l] for l in range(2)]
+        weights = [(fa[l], fu[l], fd[FFN * l:FFN * l + FFN]) + smalls[l] for l in range(2)]
         hidden, saved = x[0], []
         for l in range(2):
             hidden, acts = layer_forward(hidden, weights[l], lengths[0], tables, l == 1)
             saved.append(acts)
-        grad, big, tiny = d_y[0], [None] * 2, [None] * 2
-        scatter = functools.partial(lax.psum_scatter, axis_name=axis_name, scatter_dimension=0, tiled=True)
+        grad, bc, sl, tiny = d_y[0], [], [], [None] * 2
         for l in (1, 0):
             grad, (h1, ctx, h2, act, d_proj, d_mid, d_pre, d_out), small = layer_backward(grad, saved[l], weights[l], tables)
-            g_qkv = scatter(dot_g(h1, d_proj))
-            g_o = scatter(dot_g(ctx, d_mid))
-            big[l] = (jnp.stack([g_qkv[:, :1024], g_qkv[:, 1024:2048], g_qkv[:, 2048:], g_o]),
-                      scatter(dot_g(h2, d_pre)), scatter(dot_g(act, d_out)))
+            bc += [d_out, h2, ctx, h1]
+            sl += [act, d_pre, d_mid, d_proj]
             gb, gl, gu, gd = small
-            tiny[l] = jnp.concatenate([gb.reshape(4, 32, 32).transpose(1, 0, 2).reshape(32, 128),
-                                       gl.reshape(4, 32, 32).transpose(1, 0, 2).reshape(32, 128),
-                                       gu.reshape(32, 128), gd.reshape(32, 32)], axis=1)
-        tiny = scatter(jnp.concatenate(tiny, axis=1)).reshape(2, 416)
-        return (grad[None], jnp.stack([big[0][0], big[1][0]]), tiny[:, :128].reshape(2, 4, 32),
-                tiny[:, 128:256].reshape(2, 4, 32), jnp.stack([big[0][1], big[1][1]]), tiny[:, 256:384],
-                jnp.stack([big[0][2], big[1][2]]), tiny[:, 384:])
+            tiny[l] = jnp.concatenate([gb.reshape(LINE, SHARD, SHARD).transpose(1, 0, 2).reshape(SHARD, TILE),
+                                       gl.reshape(LINE, SHARD, SHARD).transpose(1, 0, 2).reshape(SHARD, TILE),
+                                       gu.reshape(SHARD, TILE), gd.reshape(SHARD, SHARD), jnp.zeros((SHARD, HALF_SEQ), jnp.float32)], axis=1)
+        sums = jnp.concatenate(tiny, axis=1).reshape(LINE, PLANE, PLANE, TILE).transpose(1, 0, 2, 3).reshape(BAND, TILE)
+        g_attn, g_up, g_down, g_small = reduce_grads(bc, sl, sums)
+        rows = g_small.reshape(2, LINE, TILE)
+        return (grad[None], g_attn, rows[:, 0].reshape(2, LINE, SHARD), rows[:, 1].reshape(2, LINE, SHARD), g_up, rows[:, 2],
+                g_down, rows[:, 3, :SHARD])
 
     return jax.shard_map(device_step, mesh=mesh,
                          in_specs=(batch_spec, batch_spec, batch_spec) + weight_specs,

time: 1860 us -> 723 us (0.39)
  waiting for transfers between devices: 1390 us -> 0 us
  Pallas kernels: 194 us -> 465 us
  matrix products: 156 us -> 118 us
  local copies, waits for them, and re-layouts: 63.2 us -> 87.3 us
    reduce_scatter x8 -> x0, waiting for transfers between devices: 1330 us -> none  [the longest x2 371 us: device_step(): scatter(dot_g(act, d_out))]
    pallas_call x1 -> x2, Pallas kernels: 194 us -> 465 us  [the longest x1 271 us: reduce_grads(): pl.pallas_call(grad_kernel, out_shape=[shape((2, LINE, SHARD, DIM), f32),...]
    unnamed x10 -> x0, waiting for transfers between devices: 58.4 us -> none
    dot_general x8 -> x0, matrix products: 57.2 us -> none  [dot_g(): lax.dot_general(a, b, (((0,), (0,)), ((), ())), preferred_element_type=jn...]
  transfers between devices with their start and end apart: 9 -> 0, of which waited for: 9 -> 0; matrix products, arithmetic and copies ran while one was open for 4% -> 0% of each run, Pallas kernels for 0% -> 0%
where the time goes in v2:
time: 723 us; the launch traced here: 711 us
  Pallas kernels  465 us (64%)
  matrix products  118 us (16%)
  local copies, waits for them, and re-layouts  87.3 us (12%)
  other arithmetic  37.1 us (5%)
    pallas_call x1, Pallas kernels, reduce_grads(): pl.pallas_call(grad_kernel, out_shape=[shape((2, LINE, SHARD, DIM), f32),...  271 us
    pallas_call x1, Pallas kernels, gather_weights(): pl.pallas_call(gather_kernel, out_shape=(jax.ShapeDtypeStruct((LAYERS, LI...  194 us
    dot_general x11, matrix products, dot(): return jnp.dot(a, b, preferred_element_type=jnp.float32)  51.9 us
    dot_general x12, matrix products, dot_t(): lax.dot_general(a, b, (((1,), (1,)), ((), ())), preferred_element_type=jn...  50 us
    unnamed x190, local copies, waits for them, and re-layouts  15.6 us

profile of v2, /device:TPU:0, one launch (start us, length us, event | category | flops | bytes accessed | tf_op | source)
XLA Modules:
  0.0 710.7 jit_solution(11218575271082713419)
XLA Ops:
  4.1 194.0 %gather_weights.1 = (bf16[2,4,1024,1024]{3,2,1,0:T(8,128)(2,1)}, bf16[2,1024,4096]{2,1,0:T(8,128)(2,1)}, bf16[8192,1024]{1,0:T(8,128)(2,1)}, bf16[256,128]{1,0:T(8,128)(2,1)}) custom-call(bf16[2,4,32,1024]{3,2,1,0:T(8,128)(2,1)} %wa.1, bf16[2,32,4096]{2,1,0:T(8,128)(2,1)} %wu.1, bf16[2,128,1024]{2,1,0:T(8,128)(2,1)} %wd.1, bf16[8,128]{1,0:T(8,128)(2,1)} %bitcast.320), custom_call_target="tpu_custom_call" | custom-call | tf_op jit(solution)/shard_map/gather_weights/pallas_call | solution.py:227
  216.7 3.0 fusion.194
  221.7 2.8 convolution_convert_fusion.3
  235.6 12.5 %fusion.41 = (bf16[192,4096]{1,0:T(8,128)(2,1)}, f32[192,4096]{1,0:T(8,128)}) fusion(f32[4096]{0:T(1024)S(1)} %bitcast.319, bf16[192,1024]{1,0:T(8,128)(2,1)S(1)} %add_convert_fusion.2.refs_5_, bf16[2,1024,4096]{2,1,0:T(8,128)(2,1)} %get-tuple-element.19), kind=kOutput, calls=%fused_computation.39 | convolution fusion | flops 1662517248 | bytes 13516800 | tf_op jit(solution)/shard_map/dot_general | solution.py:279
  251.0 5.9 fusion.266
  269.9 3.0 fusion.185
  276.3 3.1 fusion.164
  283.2 3.1 fusion.158
  297.7 2.6 fusion.268
  306.2 11.9 %fusion.52 = (bf16[192,4096]{1,0:T(8,128)(2,1)}, f32[192,4096]{1,0:T(8,128)S(1)}) fusion(f32[4096]{0:T(1024)} %bitcast.318, bf16[192,1024]{1,0:T(8,128)(2,1)S(1)} %add_convert_fusion.refs_1_, bf16[2,1024,4096]{2,1,0:T(8,128)(2,1)} %get-tuple-element.19), kind=kOutput, calls=%fused_computation.50 | convolution fusion | flops 1662517248 | bytes 13516800 | tf_op jit(solution)/shard_map/dot_general | solution.py:279
  318.1 6.6 fusion.261
  324.8 6.9 multiply_reduce_fusion
  333.6 3.2 fusion.200
  347.3 2.5 fusion.77
  349.8 2.5 fusion.161
  352.4 4.1 multiply_reduce_fusion.1
  370.8 2.5 convert_reduce_fusion
  383.6 6.7 fusion.262
  390.3 6.9 multiply_reduce_fusion.2
  399.1 3.2 fusion.197
  411.8 2.5 fusion.93
  414.2 2.4 fusion.137
  416.7 2.6 fusion.226
  429.6 271.2 %reduce_grads.1 = (f32[2,4,32,1024]{3,2,1,0:T(8,128)}, f32[2,32,4096]{2,1,0:T(8,128)}, f32[2,128,1024]{2,1,0:T(8,128)}, f32[8,128]{1,0:T(8,128)}, bf16[10752,102...) custom-call(bf16[192,1024]{1,0:T(8,128)(2,1)} %bitcast.304, ...), custom_call_target="tpu_custom_call" | custom-call | tf_op jit(solution)/shard_map/reduce_grads/pallas_call | solution.py:636
  (333 shorter events, 142.2 us)
Async XLA Ops:
  0.6 204.1 %copy-start.7 = (bf16[1,192,1024]{2,1,0:T(8,128)(2,1)S(1)}, bf16[1,192,1024]{2,1,0:T(8,128)(2,1)}, u32[]{:S(2)}) copy-start(bf16[1,192,1024]{2,1,0:T(8,128)(2,1)} %param.10) | copy-start | bytes 1179652
  201.6 5.8 copy-start.56
  234.1 14.0 %copy-start.43 = (bf16[192,1024]{1,0:T(8,128)(2,1)}, bf16[192,1024]{1,0:T(8,128)(2,1)S(1)}, u32[]{:S(2)}) copy-start(bf16[192,1024]{1,0:T(8,128)(2,1)S(1)} %add_convert_fusion.2.refs_5_) | copy-start | bytes 1179652
  306.2 11.9 %copy-start.44 = (bf16[192,1024]{1,0:T(8,128)(2,1)}, bf16[192,1024]{1,0:T(8,128)(2,1)S(1)}, u32[]{:S(2)}) copy-start(bf16[192,1024]{1,0:T(8,128)(2,1)S(1)} %add_convert_fusion.refs_1_) | copy-start | bytes 1179652
  306.2 11.9 %copy-start.42 = (bf16[1,192,1024]{2,1,0:T(8,128)(2,1)S(1)}, bf16[1,192,1024]{2,1,0:T(8,128)(2,1)}, u32[]{:S(2)}) copy-start(bf16[1,192,1024]{2,1,0:T(8,128)(2,1)} %param.12) | copy-start | bytes 1179652
  318.1 6.7 copy-start.11
  318.1 6.7 copy-start.60
  318.1 6.7 copy-start.68
  318.1 6.7 copy-start.80
  324.8 6.9 copy-start.45
  324.8 6.9 copy-start.87
  341.1 11.2 %copy-start.37 = (bf16[16,64,192]{2,1,0:T(8,128)(2,1)}, bf16[16,64,192]{2,1,0:T(8,128)(2,1)S(1)}, u32[]{:S(2)}) copy-start(bf16[16,64,192]{2,1,0:T(8,128)(2,1)S(1)} %convolution_convert_fusion.1) | copy-start | bytes 1179652
  383.5 14.1 %copy-start.18 = (bf16[192,1024]{1,0:T(8,128)(2,1)}, bf16[192,1024]{1,0:T(8,128)(2,1)S(1)}, u32[]{:S(2)}) copy-start(bf16[192,1024]{1,0:T(8,128)(2,1)S(1)} %get-tuple-element.63.refs_4_) | copy-start | bytes 1179652
  383.5 6.7 copy-start.6
  383.5 6.7 copy-start.58
  383.5 6.7 copy-start.64
  383.5 6.7 copy-start.78
  390.3 6.9 copy-start.46
  390.3 6.9 copy-start.84
  406.6 10.1 %copy-start.36 = (bf16[16,64,192]{2,1,0:T(8,128)(2,1)}, bf16[16,64,192]{2,1,0:T(8,128)(2,1)S(1)}, u32[]{:S(2)}) copy-start(bf16[16,64,192]{2,1,0:T(8,128)(2,1)S(1)} %convolution_convert_fusion) | copy-start | bytes 1179652
  419.4 5.9 copy-start.73
  420.5 6.0 copy-start.16
  420.5 6.0 copy-start.70
  700.8 8.5 %copy-start.47 = (f32[2,128,1024]{2,1,0:T(8,128)S(1)}, f32[2,128,1024]{2,1,0:T(8,128)}, u32[]{:S(2)}) copy-start(f32[2,128,1024]{2,1,0:T(8,128)} %get-tuple-element.154) | copy-start | bytes 3145732
  (69 other events, 164.1 us)

commit v3 on v2

v3 whole, which is shorter than its diff:
```python
import functools
import math
import jax
import jax.numpy as jnp
import numpy as np
from jax import lax
from jax.experimental import pallas as pl
from jax.experimental.pallas import tpu as pltpu
from jax.sharding import PartitionSpec as P

PAIR = 2
TRIO = 3
LINE = 4
PLANE = 8
HEADS = 16
SHARD = 32
HEAD_DIM = 64
HALF_SEQ = 96
TILE = 128
SEQ = 192
SPREAD = 224
BAND = 256
WIDE = 512
DIM = 1024
FAR = 1344
FFN = 4096

MESH = pl.DeviceIdType.MESH
EPS = 1e-5
THETA = 10000.0
NEG_BIG = -1e30
SQRT_HALF = math.sqrt(0.5)
DENSITY = 1.0 / math.sqrt(2.0 * math.pi)
SCALE = HEAD_DIM ** -0.5
F32, BF16 = jnp.float32, jnp.bfloat16
DMA = pltpu.SemaphoreType.DMA


def dot(a, b, ca=1, cb=0, precision=None):
    return lax.dot_general(a, b, (((ca,), (cb,)), ((), ())), preferred_element_type=F32, precision=precision)


def span(index, size):
    return pl.ds(pl.multiple_of(size * index, size), size)


def repeat(count, body):
    def step(i, carry):
        body(i)
        return carry

    lax.fori_loop(0, count, step, 0)


def local(src, dst, sem):
    return pltpu.make_async_copy(src, dst, sem)


def drain(ref, sem):
    local(ref, ref, sem).wait()


def remote(src, dst, send, recv, dev):
    return pltpu.make_async_remote_copy(src_ref=src, dst_ref=dst, send_sem=send, recv_sem=recv,
                                        device_id=(dev,), device_id_type=MESH)


def rotary_tables():
    lane = np.arange(TILE)
    angles = np.arange(SEQ)[:, None] * THETA ** (-(lane % SHARD) / SHARD)[None, :]
    sign = np.where(lane % HEAD_DIM < SHARD, -1.0, 1.0)
    return np.cos(angles).astype(np.float32), (np.sin(angles) * sign).astype(np.float32)


def rotate(block, cos, sin):
    lane = lax.broadcasted_iota(jnp.int32, block.shape, 1)
    return block * cos + jnp.where((lane & SHARD) == 0, pltpu.roll(block, HALF_SEQ, 1), pltpu.roll(block, SHARD, 1)) * sin


def head_masks(block):
    lane = lax.broadcasted_iota(jnp.int32, block.shape, 1)
    zero = jnp.zeros_like(block)
    return jnp.where(lane < HEAD_DIM, block, zero), jnp.where(lane < HEAD_DIM, zero, block)


def row_mean(x):
    return jnp.mean(x, axis=-1, keepdims=True)


def row_sum(x):
    return jnp.sum(x, axis=-1, keepdims=True)


def column_sum(x):
    return jnp.sum(x, axis=0, keepdims=True)


def normed(x):
    centered = x - row_mean(x)
    inv = lax.rsqrt(row_mean(centered * centered) + EPS)
    return centered * inv, inv


def pick(kind):
    shape = (TILE, DIM)
    return lax.broadcasted_iota(jnp.int32, shape, 0) == SHARD * kind + (lax.broadcasted_iota(jnp.int32, shape, 1) & 31)


def owned(swap):
    shape = (SHARD, DIM)
    row = lax.broadcasted_iota(jnp.int32, shape, 0)
    if swap:
        row = (row & TRIO) * PLANE + (row >> PAIR)
    return row == lax.broadcasted_iota(jnp.int32, shape, 1) >> 5


def unpack_vectors(small, vec):
    for l in range(PAIR):
        for t in (0, 1, TRIO):
            rows = small[pl.ds(LINE * l + t, SHARD, stride=PLANE), :].astype(BF16)
            for kind in range(1 if t == TRIO else LINE):
                spread = dot(rows, pick(kind).astype(BF16))
                at = 24 + l if t == TRIO else PLANE * l + LINE * t + kind
                vec[pl.ds(at, 1), :] = column_sum(jnp.where(owned(False), spread, 0.0))
        for d in range(SHARD):
            vec[pl.ds(HEADS + LINE * l + d // PLANE, 1), pl.ds(d % PLANE * TILE, TILE)] = small[pl.ds(PLANE * d + LINE * l + PAIR, 1), :]


def pack_vectors(vec, packed):
    for l in range(PAIR):
        for t in (0, 1, TRIO):
            total = None
            for kind in range(1 if t == TRIO else LINE):
                at = 24 + l if t == TRIO else PLANE * l + LINE * t + kind
                mine = jnp.where(owned(True), vec[pl.ds(at, 1), :], 0.0)
                part = dot(mine, pick(kind).astype(F32), 1, 1, lax.Precision.HIGHEST)
                total = part if total is None else total + part
            packed[pl.ds(LINE * l + t, SHARD, stride=PLANE), :] = total
        for d in range(SHARD):
            packed[pl.ds(SHARD * (d % PLANE) + PLANE * (d // PLANE) + LINE * l + PAIR, 1), :] = vec[pl.ds(HEADS + LINE * l + d // PLANE, 1),
                                                                              pl.ds(d % PLANE * TILE, TILE)]


def norm_stage(src, vec, at, dst):
    def body(i):
        rows = span(i, SHARD)
        unit, _ = normed(src[rows, :].astype(F32))
        dst[rows, :] = (unit * vec[pl.ds(at, 1), :] + vec[pl.ds(at + 1, 1), :]).astype(BF16)

    repeat(6, body)


def project_stage(l, h, w, vec, cos, sin, qkv):
    for kind in range(TRIO):
        def body(n, kind=kind):
            cols = span(n, BAND)
            out = dot(h[...], w[pl.ds(DIM * kind, DIM), cols]) + vec[pl.ds(PLANE * l + kind, 1), cols]
            if kind == 0:
                out = out * SCALE
            if kind < PAIR:
                out = jnp.concatenate([rotate(out[:, :TILE], cos[...], sin[...]), rotate(out[:, TILE:], cos[...], sin[...])], axis=1)
            qkv[:, pl.ds(pl.multiple_of(DIM * kind + BAND * n, BAND), BAND)] = out.astype(BF16)

        repeat(LINE, body)


def attend_stage(qkv, keep, probs, ctx):
    def body(p):
        query = qkv[:, span(p, TILE)]
        keys = head_masks(qkv[:, span(p + PLANE, TILE)])
        vals = head_masks(qkv[:, span(p + HEADS, TILE)])
        out = None
        for h in range(PAIR):
            scores = jnp.where(keep[...] > 0.5, dot(query, keys[h], 1, 1), NEG_BIG)
            grown = jnp.exp(scores - jnp.max(scores, axis=-1, keepdims=True))
            weight = (grown / row_sum(grown)).astype(BF16)
            probs[PAIR * p + h] = weight
            part = dot(weight, vals[h])
            out = part if out is None else out + part
        ctx[:, span(p, TILE)] = out.astype(BF16)

    repeat(PLANE, body)


def residual_stage(a, w, base, bias, vec, dst):
    def body(n):
        cols = span(n, BAND)
        dst[:, cols] = (base[:, cols].astype(F32) + dot(a[...], w[:, cols]) + vec[pl.ds(bias, 1), cols]).astype(BF16)

    repeat(LINE, body)


def up_stage(l, h, w, vec, act, slope):
    def body(c):
        part, n = lax.div(c, LINE), lax.rem(c, LINE)
        cols = span(c, BAND)
        pre = dot(h[...], w[span(part, DIM), span(n, BAND)]) + vec[pl.ds(HEADS + LINE * l + part, 1), span(n, BAND)]
        cdf = 0.5 * (1.0 + lax.erf(pre * SQRT_HALF))
        act[:, cols] = (pre * cdf).astype(BF16)
        slope[:, cols] = cdf + pre * (jnp.exp(-0.5 * pre * pre) * DENSITY)

    repeat(HEADS, body)


def fold(block):
    return sum(block[PLANE * i:PLANE * i + PLANE] for i in range(block.shape[0] // PLANE))


def act_grad_stage(part, d_out, w, slope, d_pre, vec, row):
    def body(n):
        cols, local_cols = span(LINE * part + n, BAND), span(n, BAND)
        grad = dot(d_out[...], w[span(n, BAND), :], 1, 1) * slope[:, local_cols]
        d_pre[:, cols] = grad.astype(BF16)
        vec[pl.ds(row + part, 1), local_cols] = column_sum(grad)

    repeat(LINE, body)


def norm_grad_stage(src, d_h, d_res, gain, vec, row_gain, row_out, row_res, dst):
    zero = jnp.zeros((PLANE, DIM), F32)

    def body(i, carry):
        rows = span(i, SHARD)
        unit, inv = normed(src[rows, :].astype(F32))
        grad = d_h[rows, :]
        scaled = grad * gain
        inner = scaled - row_mean(scaled) - unit * row_mean(scaled * unit)
        res = d_res[rows, :].astype(F32)
        out = (res + inv * inner).astype(BF16)
        dst[rows, :] = out
        return tuple(c + fold(v) for c, v in zip(carry, (grad * unit, grad, out.astype(F32), res)))

    sums = lax.fori_loop(0, 6, body, (zero,) * LINE)
    for at, value in zip((row_gain, row_gain + 1, row_out, row_res), sums):
        if at is not None:
            vec[pl.ds(at, 1), :] = column_sum(value)


def attend_grad_stage(l, qkv, probs, d_ctx, cos, sin, d_proj, vec):
    def body(p):
        keys = head_masks(qkv[:, span(p + PLANE, TILE)])
        queries = head_masks(qkv[:, span(p, TILE)])
        vals = qkv[:, span(p + HEADS, TILE)]
        outs = head_masks(d_ctx[:, span(p, TILE)])
        d_q = d_k = d_v = 0.0
        for h in range(PAIR):
            weight = probs[PAIR * p + h]
            wide = weight.astype(F32)
            d_weight = dot(outs[h], vals, 1, 1)
            d_score = (wide * (d_weight - row_sum(d_weight * wide))).astype(BF16)
            d_v = d_v + dot(weight, outs[h], 0, 0)
            d_q = d_q + dot(d_score, keys[h])
            d_k = d_k + dot(d_score, queries[h], 0, 0)
        d_q = rotate(d_q, cos[...], -sin[...]) * SCALE
        d_k = rotate(d_k, cos[...], -sin[...])
        for kind, grad in enumerate((d_q, d_k, d_v)):
            grad = grad.astype(BF16)
            d_proj[:, span(p + PLANE * kind, TILE)] = grad
            vec[pl.ds(PLANE * l + kind, 1), span(p, TILE)] = column_sum(grad.astype(F32))

    repeat(PLANE, body)
LAYERS = PAIR
ORDERS = (("b", 0, 1), ("b", 1, 0), ("a", 0, 1), ("a", 1, 0), ("b", 0, 1), ("b", 1, 0))
UNITS = [(0, 6)] + [(layer, piece) for layer in range(LAYERS) for piece in range(6)]
STAGE_LAG = (0, 0, 1, TRIO)
AHEAD = PAIR


SAVED = ("h1", "qkv", "probs", "ctx", "mid", "h2", "act", "slope")
SAVED_SHAPES = {"h1": (SEQ, DIM), "qkv": (SEQ, 3072), "probs": (HEADS, SEQ, SEQ), "ctx": (SEQ, DIM), "mid": (SEQ, DIM),
                "h2": (SEQ, DIM), "act": (SEQ, FFN), "slope": (SEQ, FFN)}


def saved_type(name):
    return F32 if name == "slope" else BF16


def forward_kernel(*refs):
    (wa, wu, wd, sm, x, keep, cos, sin), refs = refs[:PLANE], refs[PLANE:]
    (fa, fu, fd, fs, out_vec, out_mid), refs = refs[:6], refs[6:]
    saved = [dict(zip(SAVED, refs[PLANE * l:PLANE * l + PLANE])) for l in range(LAYERS)]
    refs = refs[HEADS:]
    (va, vu, vd, vs), refs = refs[:LINE], refs[LINE:]
    acts = [dict(zip(SAVED, refs[PLANE * l:PLANE * l + PLANE])) for l in range(LAYERS)]
    refs = refs[HEADS:]
    (y, vec, small_in, small, w_even, w_odd, load_sem, save_sem, own_sem, xy_sem, z_sem, push_send, push_recv,
     recv_sem) = refs
    me = lax.axis_index("fsdp")
    core, xc, yc, zc = me % PAIR, (me // PAIR) % PAIR, (me // LINE) % PAIR, me // PLANE
    partner = me + 1 - PAIR * core
    near = (me + PAIR - LINE * xc, me + LINE - PLANE * yc)
    up, down = me + PLANE, me - PLANE
    has_up, has_down = zc < TRIO, zc > 0

    def full(u, src):
        layer, piece = UNITS[u]
        if piece < PAIR:
            return fa.at[layer, pl.ds(PAIR * piece, PAIR), pl.ds(pl.multiple_of(SHARD * src, SHARD), SHARD), :]
        if piece < LINE:
            return fu.at[layer, pl.ds(pl.multiple_of(SHARD * src + HEADS * (piece - PAIR), HEADS), HEADS), :]
        if piece < 6:
            return fd.at[pl.ds(pl.multiple_of(FFN * layer + TILE * src + HEAD_DIM * (piece - LINE), HEAD_DIM), HEAD_DIM), :]
        return fs.at[pl.ds(pl.multiple_of(PLANE * src, PLANE), PLANE), :]

    def own(u):
        layer, piece = UNITS[u]
        if piece < PAIR:
            return va.at[layer, pl.ds(PAIR * piece, PAIR)]
        if piece < LINE:
            return vu.at[layer, pl.ds(HEADS * (piece - PAIR), HEADS), :]
        if piece < 6:
            return vd.at[layer, pl.ds(HEAD_DIM * (piece - LINE), HEAD_DIM), :]
        return vs

    def kind(u):
        return (UNITS[u][1] + 0) // PAIR

    def order(u):
        return ORDERS[UNITS[u][1] % 6]

    def tiny(u):
        return 1 if UNITS[u][1] == 6 else 0

    barrier = pltpu.get_barrier_semaphore()
    for peer in (partner,) + near:
        pl.semaphore_signal(barrier, inc=1, device_id=(peer,), device_id_type=MESH)

    @pl.when(has_up)
    def _():
        pl.semaphore_signal(barrier, inc=1, device_id=(up,), device_id_type=MESH)

    @pl.when(has_down)
    def _():
        pl.semaphore_signal(barrier, inc=1, device_id=(down,), device_id_type=MESH)

    loads = [local(src, dst, load_sem.at[i])
             for i, (src, dst) in enumerate(((wa, va), (wu, vu), (wd, vd), (sm, vs)))]
    for load in loads:
        load.start()
    for load in loads:
        load.wait()
    pl.semaphore_wait(barrier, TRIO + has_up.astype(jnp.int32) + has_down.astype(jnp.int32))

    def slab(u, src_ref, src, send, recv, dev):
        return remote(src_ref, full(u, src), send, recv, dev)

    def send_z(u, src_ref, src, slot, above, below):
        if above is not None:
            @pl.when(above)
            def _():
                slab(u, src_ref, src, z_sem.at[tiny(u)], recv_sem.at[u, slot], up).start()
        if below is not None:
            @pl.when(below)
            def _():
                slab(u, src_ref, src, z_sem.at[tiny(u)], recv_sem.at[u, slot], down).start()

    def send_xy(u, src_ref, src, dim, slot):
        slab(u, src_ref, src, xy_sem.at[tiny(u)], recv_sem.at[u, slot], near[dim]).start()

    def push(u, src_ref, src):
        slab(u, src_ref, src, push_send.at[kind(u)], push_recv.at[u], partner).start()

    def column(flip_p, p):
        base = me - PLANE * zc
        if flip_p:
            base = base + (near[p] - me)
        return base

    def arrived(u, src, slot):
        slab(u, full(u, src), src, xy_sem.at[tiny(u)], recv_sem.at[u, slot], me).wait_recv()
        return full(u, src)

    def stage0(u):
        col, p, q = order(u)
        mine = own(u)
        send_z(u, mine, me, zc, has_up, has_down)
        send_xy(u, mine, me, p, LINE + zc)
        send_xy(u, mine, me, q, PLANE)
        push(u, mine, me)
        local(mine, full(u, me), own_sem.at[u]).start()

    def z_arrivals(u, flips, send_p):
        col, p, q = order(u)
        for dz in (1, PAIR, TRIO):
            for step in (-1, 1):
                for flip_p in flips:
                    zs = zc + step * dz
                    src = column(flip_p, p) + PLANE * zs
                    slot = LINE * flip_p + zs
                    present = (zc >= dz) if step < 0 else (zc <= TRIO - dz)

                    @pl.when(present)
                    def _(src=src, slot=slot, step=step):
                        ref = arrived(u, src, slot)
                        send_z(u, ref, src, slot, has_up if step < 0 else None, has_down if step > 0 else None)
                        if send_p:
                            send_xy(u, ref, src, p, LINE + slot)
                        send_xy(u, ref, src, q, PLANE)
                        push(u, ref, src)

    def stage1(u):
        col, p, q = order(u)
        if col == "a":
            z_arrivals(u, (0,), True)
        else:
            src = near[p]
            ref = arrived(u, src, LINE + zc)
            send_z(u, ref, src, LINE + zc, has_up, has_down)
            send_xy(u, ref, src, q, PLANE)
            push(u, ref, src)

    def stage2(u):
        col, p, q = order(u)
        if col == "a":
            for hop in range(LINE):
                zs = lax.rem(zc + hop, LINE)
                src = column(1, p) + PLANE * zs
                ref = arrived(u, src, LINE + zs)
                send_xy(u, ref, src, q, PLANE)
                push(u, ref, src)
        else:
            z_arrivals(u, (0, 1), False)

    def stage3(u):
        col, p, q = order(u)
        rows = fs.at[pl.ds(0, HEAD_DIM), :] if tiny(u) else fd.at[pl.ds(0, WIDE), :]
        drain(rows, recv_sem.at[u, PLANE])
        for flip_p in (0, 1):
            base = column(flip_p, p) + (near[q] - me)

            def body(zs, carry, base=base):
                src = base + PLANE * zs
                push(u, full(u, src), src)
                return carry

            lax.fori_loop(0, LINE, body, 0)

    def ready(*units):
        for u in units:
            drain(fs.at[pl.ds(0, TILE), :] if tiny(u) else fd.at[pl.ds(0, DIM), :], push_recv.at[u])
            drain(own(u), own_sem.at[u])

    def fetch(l, what, buf):
        for i in range(LINE):
            src = {"a": lambda: fa.at[l, i], "u": lambda: fu.at[l, :, pl.ds(DIM * i, DIM)],
                   "d": lambda: fd.at[pl.ds(FFN * l + DIM * i, DIM), :]}[what]()
            local(src, buf.at[pl.ds(DIM * i, DIM), :], load_sem.at[i]).start()

    def fetched(buf):
        for i in range(LINE):
            drain(buf.at[pl.ds(DIM * i, DIM), :], load_sem.at[i])

    def save(l, *names):
        for name in names:
            local(acts[l][name], saved[l][name], save_sem.at[l, SAVED.index(name)]).start()

    def source(l):
        return y if l else x

    def begin():
        ready(0)
        local(fs, small_in, load_sem.at[0]).start()
        drain(small_in, load_sem.at[0])
        small[...] = small_in[...].astype(F32)
        unpack_vectors(small, vec)
        local(vec, out_vec, save_sem.at[0, PLANE]).start()
        norm_stage(x, vec, LINE, acts[0]["h1"])
        save(0, "h1")

    def project(l, buf):
        fetched(buf)
        project_stage(l, acts[l]["h1"], buf, vec, cos, sin, acts[l]["qkv"])
        save(l, "qkv")

    def attend(l, buf):
        got = acts[l]
        attend_stage(got["qkv"], keep, got["probs"], got["ctx"])
        residual_stage(got["ctx"], buf.at[pl.ds(3072, DIM), :], source(l), PLANE * l + TRIO, vec, got["mid"])
        norm_stage(got["mid"], vec, PLANE * l + 6, got["h2"])
        save(l, "probs", "ctx", "mid", "h2")

    def grow(l, buf):
        fetched(buf)
        up_stage(l, acts[l]["h2"], buf, vec, acts[l]["act"], acts[l]["slope"])
        save(l, "act", "slope")

    def shrink(buf):
        fetched(buf)
        residual_stage(acts[0]["act"], buf, acts[0]["mid"], 24, vec, y)
        local(y, out_mid, save_sem.at[1, PLANE]).start()
        norm_stage(y, vec, 12, acts[1]["h1"])
        save(1, "h1")

    def need(l, pair, what, buf):
        def go():
            first = 1 + 6 * l + PAIR * pair
            ready(first, first + 1)
            fetch(l, what, buf)
        return go

    before = {6: need(0, 0, "a", w_even), PLANE: need(0, 1, "u", w_odd), 10: need(0, PAIR, "d", w_even),
              12: need(1, 0, "a", w_odd), 14: need(1, 1, "u", w_even)}
    after = {5: begin, 6: lambda: project(0, w_even), 7: lambda: attend(0, w_even), PLANE: lambda: grow(0, w_odd),
             10: lambda: shrink(w_even), 12: lambda: project(1, w_odd), 13: lambda: attend(1, w_odd),
             14: lambda: grow(1, w_even)}
    stages = (stage0, stage1, stage2, stage3)
    count = len(UNITS)
    for rnd in range(count + STAGE_LAG[TRIO]):
        before.get(rnd, lambda: None)()
        for k in range(LINE):
            if k == 0:
                todo = range(AHEAD + 1) if rnd == 0 else [rnd + AHEAD]
            else:
                todo = [rnd - STAGE_LAG[k]]
            for u in todo:
                if 0 <= u < count:
                    stages[k](u)
        after.get(rnd, lambda: None)()
    ready(count - PAIR, count - 1)

    per_layer = HEAD_DIM * LAYERS
    drain(fd.at[pl.ds(0, 60 * per_layer), :], xy_sem.at[0])
    drain(fs.at[pl.ds(0, 9 * PLANE), :], xy_sem.at[1])
    ends = jnp.logical_or(zc == 0, zc == TRIO)

    @pl.when(ends)
    def _():
        drain(fd.at[pl.ds(0, 10 * per_layer), :], z_sem.at[0])
        drain(fs.at[pl.ds(0, PAIR * PLANE), :], z_sem.at[1])

    @pl.when(jnp.logical_not(ends))
    def _():
        drain(fd.at[pl.ds(0, 50 * per_layer), :], z_sem.at[0])
        drain(fs.at[pl.ds(0, 10 * PLANE), :], z_sem.at[1])

    halves = (fa.at[0], fu.at[0], fd.at[pl.ds(0, FFN), :], fs.at[pl.ds(0, TILE), :])
    for i, half in enumerate(halves):
        drain(half, push_send.at[i])
    for l in range(LAYERS):
        for i, name in enumerate(SAVED):
            drain(saved[l][name], save_sem.at[l, i])
    drain(out_vec, save_sem.at[0, PLANE])
    drain(out_mid, save_sem.at[1, PLANE])


def forward(w_attn, w_up, w_down, small, x, keep, cos, sin):
    shape, hbm, vmem = jax.ShapeDtypeStruct, pl.BlockSpec(memory_space=pltpu.HBM), pl.BlockSpec(memory_space=pltpu.VMEM)
    kept = [shape(SAVED_SHAPES[name], saved_type(name)) for name in SAVED] * LAYERS
    outs = pl.pallas_call(
        forward_kernel,
        out_shape=[shape((LAYERS, LINE, DIM, DIM), BF16), shape((LAYERS, DIM, FFN), BF16),
                   shape((LAYERS * FFN, DIM), BF16), shape((BAND, TILE), BF16), shape((SHARD, DIM), F32),
                   shape((SEQ, DIM), BF16)] + kept,
        in_specs=[hbm] * LINE + [vmem] * LINE,
        out_specs=[hbm] * (6 + len(kept)),
        scratch_shapes=[pltpu.VMEM(w.shape, BF16) for w in (w_attn, w_up, w_down, small)]
        + [pltpu.VMEM(k.shape, k.dtype) for k in kept]
        + [pltpu.VMEM((SEQ, DIM), BF16), pltpu.VMEM((SHARD, DIM), F32), pltpu.VMEM((BAND, TILE), BF16),
           pltpu.VMEM((BAND, TILE), F32), pltpu.VMEM((FFN, DIM), BF16), pltpu.VMEM((FFN, DIM), BF16),
           DMA((LINE,)), DMA((PAIR, 9)), DMA((len(UNITS),)), DMA((PAIR,)), DMA((PAIR,)), DMA((LINE,)), DMA((len(UNITS),)),
           DMA((len(UNITS), 9))],
        compiler_params=pltpu.CompilerParams(collective_id=0, has_side_effects=True, vmem_limit_bytes=60 * DIM * DIM),
        name="forward",
    )(w_attn, w_up, w_down, small, x, keep, cos, sin)
    return outs[:TRIO], outs[LINE], outs[5], [dict(zip(SAVED, outs[6 + PLANE * l:14 + PLANE * l])) for l in range(LAYERS)]


PIECES = [(layer, name) for layer in (1, 0) for name in "DUOQ"]
WIDTH = {"D": WIDE, "U": WIDE, "O": TILE, "Q": 384}
ROWS = SEQ
LAG = (1, PAIR, TRIO)


def acc_shape(name):
    return (WIDE, DIM) if name == "D" else (DIM, WIDTH[name])


def backward_kernel(*refs):
    n = len(PIECES)
    (fa, fu, fd, vec, cos, sin, x_in, y_in, d_y), refs = refs[:9], refs[9:]
    saved = [dict(zip(SAVED, refs[PLANE * l:PLANE * l + PLANE])) for l in range(LAYERS)]
    refs = refs[HEADS:]
    (g_attn, g_up, g_down, g_small, d_x, bc_far), refs = refs[:6], refs[6:]
    sl_far, refs = refs[:n], refs[n:]
    (d_pre_far, d_mid_far, d_proj_far, d_top), refs = refs[:LINE], refs[LINE:]
    (bc_v, sl_v), refs = refs[:PAIR], refs[PAIR:]
    acc, got, refs = refs[:n], refs[n:PAIR * n], refs[PAIR * n:]
    (sum_v, sum_got, sum_line, square, wide, slope_v, qkv_v, probs_v, mid_v, x_v, d_out, d_pre, d_mid, d_proj, d_ctx, d_h,
     g_vec), refs = refs[:17], refs[17:]
    (bc_send, bc_recv, push_send, push_recv, sl_send, sl_recv, load_sem, rs_send, rs_recv, out_send, out_recv, own_sem,
     sum_send, sum_recv, square_sem, slope_sem, wide_sem, act_sem, spill_sem) = refs
    d_outs = (d_top, d_y)
    bc_in = [{"D": d_outs[l], "U": saved[l]["h2"], "O": saved[l]["ctx"], "Q": saved[l]["h1"]}[name] for l, name in PIECES]
    sl_in = [{"D": saved[l]["act"], "U": d_pre_far.at[l], "O": d_mid_far.at[l], "Q": d_proj_far.at[l]}[name]
             for l, name in PIECES]

    me = lax.axis_index("fsdp")
    core, xc, yc, zc = me % PAIR, (me // PAIR) % PAIR, (me // LINE) % PAIR, me // PLANE
    place = me % PLANE

    def peer(r):
        out = me
        if r & 1:
            out = out + 1 - PAIR * core
        if r & PAIR:
            out = out + PAIR - LINE * xc
        if r & LINE:
            out = out + LINE - PLANE * yc
        return out

    def line(k):
        return place + PLANE * lax.rem(zc + k, LINE)

    barrier = pltpu.get_barrier_semaphore()
    for r in range(1, PLANE):
        pl.semaphore_signal(barrier, inc=1, device_id=(peer(r),), device_id_type=MESH)
    for k in range(1, LINE):
        pl.semaphore_signal(barrier, inc=1, device_id=(line(k),), device_id_type=MESH)
    pl.semaphore_wait(barrier, 10)

    def far(u, r, half=None):
        start = FAR * u + SEQ * (r - 1)
        return bc_far.at[pl.ds(start, SEQ), :] if half is None else bc_far.at[pl.ds(start + HALF_SEQ * half, HALF_SEQ), :]

    def blocks(u, where):
        name = PIECES[u][1]
        if name == "D":
            return [(pl.multiple_of(DIM * i + TILE * where, TILE), TILE * i, TILE) for i in range(LINE)]
        if name == "Q":
            return [(pl.multiple_of(DIM * i + TILE * where, TILE), TILE * i, TILE) for i in range(TRIO)]
        return [(pl.multiple_of(WIDTH[name] * where, TILE), 0, WIDTH[name])]

    def send_bc(u):
        for r in (PAIR, LINE):
            for half in (0, 1):
                slot = (0 if r == PAIR else PAIR) + half
                remote(bc_in[u].at[pl.ds(HALF_SEQ * half, HALF_SEQ), :], far(u, r, half), bc_send, bc_recv.at[u, slot], peer(r)).start()
        remote(bc_in[u], far(u, 1), push_send, push_recv.at[u], peer(1)).start()

    def send_sl(u):
        for r in (PAIR, 6, LINE, TRIO, 7, 5, 1):
            for src, dst, width in blocks(u, peer(r) % PLANE):
                remote(sl_in[u].at[:, pl.ds(src, width)], sl_far[u].at[pl.ds(SEQ * (r - 1), SEQ), pl.ds(dst, width)],
                       sl_send.at[u], sl_recv.at[u], peer(r)).start()

    def push(u, r, half):
        remote(far(u, r, half), far(u, r + 1, half), push_send, push_recv.at[u], peer(1)).start()

    def relay_bc(u):
        for slot, r, half, onward in ((0, PAIR, 0, LINE), (TRIO, LINE, 1, PAIR), (1, PAIR, 1, None), (PAIR, LINE, 0, None)):
            drain(far(u, r, half), bc_recv.at[u, slot])
            if onward is not None:
                remote(far(u, r, half), far(u, 6, half), bc_send, bc_recv.at[u, LINE + half], peer(onward)).start()
            push(u, r, half)

    def collect(u):
        name = PIECES[u][1]
        own = [local(bc_in[u], bc_v.at[pl.ds(0, SEQ), :], load_sem.at[0])]
        for i, (src, dst, width) in enumerate(blocks(u, place)):
            own.append(local(sl_in[u].at[:, pl.ds(src, width)], sl_v.at[pl.ds(0, SEQ), pl.ds(dst, width)],
                             load_sem.at[1 + i]))
        for c in own:
            c.start()
        for half in (0, 1):
            drain(far(u, 6, half), bc_recv.at[u, LINE + half])
            push(u, 6, half)
        drain(sl_far[u], sl_recv.at[u])
        drain(bc_far.at[pl.ds(0, 768), :], push_recv.at[u])
        rest = [local(bc_far.at[pl.ds(FAR * u, FAR), :], bc_v.at[pl.ds(SEQ, FAR), :], load_sem.at[5]),
                local(sl_far[u], sl_v.at[pl.ds(SEQ, FAR), pl.ds(0, WIDTH[name])], load_sem.at[6])]
        for c in rest:
            c.start()
        for c in own + rest:
            c.wait()

    def piece_rows(u):
        return acc_shape(PIECES[u][1])[0] // LINE

    def piece(ref, u, d):
        pr = piece_rows(u)
        return ref.at[pl.ds(pl.multiple_of(pr * d, pr), pr), :]

    def step_down_line(u, d, up):
        side = jnp.where(up, 0, 1)
        dst = got[u].at[side, span(d - 1 + side, piece_rows(u)), :]
        remote(piece(acc[u], u, d), dst, rs_send.at[u], rs_recv.at[u, side, d], me + jnp.where(up, PLANE, -PLANE)).start()

    def add_piece(u, side, d):
        pr = piece_rows(u)
        drain(piece(acc[u], u, d), rs_recv.at[u, side, d])
        rows = SHARD

        def body(i, carry):
            at = pl.ds(pl.multiple_of(pr * d + rows * i, rows), rows)
            there = pl.ds(pl.multiple_of(pr * (d - 1 + side) + rows * i, rows), rows)
            acc[u][at, :] = acc[u][at, :] + got[u][side, there, :]
            return carry

        lax.fori_loop(0, pr // rows, body, 0)

    def product(u):
        name = PIECES[u][1]
        pr, width = piece_rows(u), WIDTH[name]

        def body(d, carry):
            at = pl.ds(pl.multiple_of(pr * d, pr), pr)
            if name == "D":
                lhs, rhs = sl_v[:, at], bc_v[...]
            else:
                lhs, rhs = bc_v[:, at], sl_v[:, pl.ds(0, width)]
            acc[u][at, :] = lax.dot_general(lhs, rhs, (((0,), (0,)), ((), ())), preferred_element_type=jnp.float32)
            return carry

        lax.fori_loop(0, LINE, body, 0)

        @pl.when(jnp.logical_or(zc == 0, zc == TRIO))
        def _():
            for hop in range(TRIO):
                step_down_line(u, jnp.where(zc == 0, TRIO - hop, hop), zc == 0)

    def second_hop(u):
        @pl.when(jnp.logical_or(zc == 1, zc == PAIR))
        def _():
            for hop in range(PAIR):
                d = jnp.where(zc == 1, TRIO - hop, hop)
                add_piece(u, jnp.where(zc == 1, 0, 1), d)
                step_down_line(u, d, zc == 1)

    def third_hop(u):
        @pl.when(jnp.logical_or(zc == 1, zc == PAIR))
        def _():
            d = jnp.where(zc == 1, 0, TRIO)
            add_piece(u, jnp.where(zc == 1, 1, 0), d)
            step_down_line(u, d, zc == PAIR)

    def finish(u):
        layer, name = PIECES[u]

        @pl.when(zc > 0)
        def _():
            add_piece(u, 0, zc)

        @pl.when(zc < TRIO)
        def _():
            add_piece(u, 1, zc)

        if name == "D":
            local(piece(acc[u], u, zc), g_down.at[layer], own_sem.at[u]).start()
            return
        for r in range(PLANE):
            at = pl.ds(pl.multiple_of(BAND * zc + SHARD * (peer(r) % PLANE), SHARD), SHARD)
            if name == "U":
                pairs = [(acc[u].at[at, :], g_up.at[layer, :, pl.ds(pl.multiple_of(WIDE * place, WIDE), WIDE)])]
            else:
                mats = (TRIO,) if name == "O" else (0, 1, PAIR)
                pairs = [(acc[u].at[at, pl.ds(TILE * i, TILE)],
                          g_attn.at[layer, m, :, pl.ds(pl.multiple_of(TILE * place, TILE), TILE)]) for i, m in enumerate(mats)]
            for src, dst in pairs:
                if r == 0:
                    local(src, dst, own_sem.at[u]).start()
                else:
                    remote(src, dst, out_send.at[u], out_recv.at[u], peer(r)).start()

    def sums_plane():
        for r in range(1, PLANE):
            remote(sum_v.at[pl.ds(pl.multiple_of(SHARD * (peer(r) % PLANE), SHARD), SHARD), :], sum_got.at[pl.ds(SHARD * (r - 1), SHARD), :],
                   sum_send.at[0], sum_recv.at[0], peer(r)).start()

    def sums_line():
        drain(sum_got, sum_recv.at[0])
        total = sum_v[pl.ds(pl.multiple_of(SHARD * place, SHARD), SHARD), :]
        for r in range(1, PLANE):
            total = total + sum_got[pl.ds(SHARD * (r - 1), SHARD), :]
        sum_line[pl.ds(0, SHARD), :] = total
        for k in range(1, LINE):
            remote(sum_line.at[pl.ds(pl.multiple_of(PLANE * lax.rem(zc + k, LINE), PLANE), PLANE), :],
                   sum_line.at[pl.ds(SHARD + PLANE * (k - 1), PLANE), :], sum_send.at[1], sum_recv.at[1], line(k)).start()

    def sums_end():
        drain(sum_line.at[pl.ds(0, 24), :], sum_recv.at[1])
        total = sum_line[pl.ds(pl.multiple_of(PLANE * zc, PLANE), PLANE), :]
        for k in range(1, LINE):
            total = total + sum_line[pl.ds(SHARD + PLANE * (k - 1), PLANE), :]
        g_small[...] = total

    squares = [(l, k) for l in (1, 0) for k in range(PLANE)]
    wides = [(l, k) for l in (1, 0) for k in range(LINE)]
    taken = [0, 0]

    def fetch_square(i):
        if i < len(squares):
            l, k = squares[i]
            src = fd.at[pl.ds(FFN * l + DIM * k, DIM), :] if k < LINE else fa.at[l, (TRIO, 0, 1, PAIR)[k - LINE]]
            local(src, square.at[i % PAIR], square_sem.at[i % PAIR]).start()
            if k < LINE:
                local(saved[l]["slope"].at[:, pl.ds(DIM * k, DIM)], slope_v.at[i % PAIR], slope_sem.at[i % PAIR]).start()

    def fetch_wide(i):
        if i < len(wides):
            l, k = wides[i]
            local(fu.at[l, pl.ds(BAND * k, BAND), :], wide.at[i % PAIR], wide_sem.at[i % PAIR]).start()

    def with_square(body):
        i = taken[0]
        drain(square.at[i % PAIR], square_sem.at[i % PAIR])
        if squares[i][1] < LINE:
            drain(slope_v.at[i % PAIR], slope_sem.at[i % PAIR])
        body(square.at[i % PAIR], slope_v.at[i % PAIR])
        fetch_square(i + PAIR)
        taken[0] += 1

    def with_wide(body):
        i = taken[1]
        drain(wide.at[i % PAIR], wide_sem.at[i % PAIR])
        body(wide.at[i % PAIR])
        fetch_wide(i + PAIR)
        taken[1] += 1

    def loads(l):
        pairs = [(saved[l]["qkv"], qkv_v), (saved[l]["probs"], probs_v), (saved[l]["mid"], mid_v), ((x_in, y_in)[l], x_v)]
        return [local(src, dst, act_sem.at[i]) for i, (src, dst) in enumerate(pairs)]

    def spill(src, dst, i):
        local(src, dst, spill_sem.at[i]).start()
        drain(src, spill_sem.at[i])

    def chain_act(l):
        for c in loads(l):
            c.start()
        for part in range(LINE):
            with_square(lambda w, sl: act_grad_stage(part, d_out, w, sl, d_pre, g_vec, HEADS + LINE * l))
        spill(d_pre, d_pre_far.at[l], 0)

    def chain_mid(l):
        for part in range(LINE):
            def body(w, part=part):
                d_h[:, pl.ds(BAND * part, BAND)] = dot(d_pre[...], w[...], 1, 1)

            with_wide(body)
        for c in loads(l):
            c.wait()
        norm_grad_stage(mid_v, d_h, d_out, vec[pl.ds(PLANE * l + 6, 1), :], g_vec, PLANE * l + 6, PLANE * l + TRIO, 24 + l, d_mid)
        spill(d_mid, d_mid_far.at[l], 0)

    def chain_attend(l):
        def to_ctx(w, _):
            def body(i):
                d_ctx[:, span(i, BAND)] = dot(d_mid[...], w[span(i, BAND), :], 1, 1).astype(BF16)

            repeat(LINE, body)

        with_square(to_ctx)
        attend_grad_stage(l, qkv_v, probs_v, d_ctx, cos, sin, d_proj, g_vec)
        spill(d_proj, d_proj_far.at[l], 0)

    def chain_norm(l):
        for kind in range(TRIO):
            def to_h(w, _, kind=kind):
                def body(i):
                    part = dot(d_proj[:, pl.ds(DIM * kind, DIM)], w[span(i, BAND), :], 1, 1)
                    d_h[:, span(i, BAND)] = d_h[:, span(i, BAND)] + part if kind else part

                repeat(LINE, body)

            with_square(to_h)
        norm_grad_stage(x_v, d_h, d_mid, vec[pl.ds(PLANE * l + LINE, 1), :], g_vec, PLANE * l + LINE, None, None, d_out)
        spill(d_out, (d_x, d_top)[l], 0)

    for i in (0, 1):
        fetch_square(i)
        fetch_wide(i)
    send_bc(0)
    send_sl(0)
    local(d_y, d_out, load_sem.at[0]).start()
    g_vec[...] = jnp.zeros_like(g_vec)
    drain(d_out, load_sem.at[0])
    chain_act(1)
    relay_bc(0)
    send_bc(1)
    chain_mid(1)
    chain = (lambda: chain_attend(1), lambda: chain_norm(1), lambda: chain_act(0), lambda: chain_mid(0),
             lambda: chain_attend(0), lambda: chain_norm(0))
    for s in range(n + LAG[PAIR]):
        if s < n:
            if s + 1 < n:
                relay_bc(s + 1)
                send_sl(s + 1)
            if s + PAIR < n:
                send_bc(s + PAIR)
            if s < len(chain):
                chain[s]()
            collect(s)
            product(s)
        for lag, hop in zip(LAG, (second_hop, third_hop, finish)):
            if 0 <= s - lag < n:
                hop(s - lag)
        if s == len(chain):
            pack_vectors(g_vec, sum_v)
            sums_plane()
        if s == len(chain) + 1:
            sums_line()
    sums_end()

    drain(bc_far.at[pl.ds(0, n * 576), :], bc_send)
    drain(bc_far.at[pl.ds(0, n * 768), :], push_send)
    drain(sum_got, sum_send.at[0])
    drain(sum_line.at[pl.ds(0, 24), :], sum_send.at[1])
    for u in range(n):
        name = PIECES[u][1]
        drain(sl_far[u], sl_send.at[u])
        drain(acc[u].at[pl.ds(0, TRIO * piece_rows(u)), :], rs_send.at[u])
        if name == "D":
            drain(acc[u].at[pl.ds(0, TILE), :], own_sem.at[u])
        else:
            drain(acc[u].at[pl.ds(0, SHARD), :], own_sem.at[u])
            drain(acc[u].at[pl.ds(0, SPREAD), :], out_send.at[u])
            drain(acc[u].at[pl.ds(0, SPREAD), :], out_recv.at[u])


def backward(weights, vec, cos, sin, x_in, y_in, d_y, saved):
    n = len(PIECES)
    shape, hbm, vmem = jax.ShapeDtypeStruct, pl.BlockSpec(memory_space=pltpu.HBM), pl.BlockSpec(memory_space=pltpu.VMEM)
    wide = lambda cols: (SEQ, cols)
    outs = pl.pallas_call(
        backward_kernel,
        out_shape=[shape((PAIR, LINE, SHARD, DIM), F32), shape((PAIR, SHARD, FFN), F32), shape((PAIR, TILE, DIM), F32), shape((PLANE, TILE), F32),
                   shape(wide(DIM), BF16), shape((n * FAR, DIM), BF16)]
        + [shape((FAR, WIDTH[name]), BF16) for _, name in PIECES]
        + [shape((LAYERS, SEQ, cols), BF16) for cols in (FFN, DIM, 3072)] + [shape(wide(DIM), BF16)],
        in_specs=[hbm] * TRIO + [vmem] * TRIO + [hbm] * (TRIO + PAIR * len(SAVED)),
        out_specs=[hbm] * TRIO + [vmem] + [hbm] * (n + 6),
        scratch_shapes=[pltpu.VMEM((1536, DIM), BF16), pltpu.VMEM((1536, WIDE), BF16)]
        + [pltpu.VMEM(acc_shape(name), F32) for _, name in PIECES]
        + [pltpu.VMEM((PAIR, TRIO * acc_shape(name)[0] // LINE, acc_shape(name)[1]), F32) for _, name in PIECES]
        + [pltpu.VMEM((BAND, TILE), F32), pltpu.VMEM((SPREAD, TILE), F32), pltpu.VMEM((56, TILE), F32),
           pltpu.VMEM((PAIR, DIM, DIM), BF16), pltpu.VMEM((PAIR, BAND, FFN), BF16), pltpu.VMEM((PAIR, SEQ, DIM), F32)]
        + [pltpu.VMEM(s, BF16) for s in (wide(3072), (HEADS, SEQ, SEQ), wide(DIM), wide(DIM), wide(DIM), wide(FFN),
                                         wide(DIM), wide(3072), wide(DIM))]
        + [pltpu.VMEM(wide(DIM), F32), pltpu.VMEM((SHARD, DIM), F32)]
        + [DMA, DMA((n, 6)), DMA, DMA((n,)), DMA((n,)), DMA((n,)), DMA((7,)), DMA((n,)), DMA((n, PAIR, LINE)),
           DMA((n,)), DMA((n,)), DMA((n,)), DMA((PAIR,)), DMA((PAIR,)), DMA((PAIR,)), DMA((PAIR,)), DMA((PAIR,)), DMA((LINE,)), DMA((1,))],
        compiler_params=pltpu.CompilerParams(collective_id=1, has_side_effects=True, vmem_limit_bytes=67043328),
        name="backward",
    )(*weights, vec, cos, sin, x_in, y_in, d_y, *[saved[l][name] for l in range(LAYERS) for name in SAVED])
    return outs[:5]


def pack_small(b_attn, ln_par, b_up, b_down):
    rows = [b_attn.reshape(PAIR, TILE), ln_par.reshape(PAIR, TILE), b_up, jnp.pad(b_down, ((0, 0), (0, HALF_SEQ)))]
    return jnp.stack(rows, axis=1).reshape(PLANE, TILE)


def solution(mesh):
    axis_name = mesh.axis_names[0]
    batch_spec = P(axis_name)
    weight_specs = (P(None, None, axis_name, None), P(None, None, axis_name), P(None, None, axis_name),
                    P(None, axis_name, None), P(None, axis_name), P(None, axis_name, None), P(None, axis_name))

    def device_step(x, lengths, d_y, w_attn, b_attn, ln_par, w_up, b_up, w_down, b_down):
        cos, sin = rotary_tables()
        keep = (jnp.arange(SEQ)[None] < lengths[0]).astype(F32)
        weights, vec, y, saved = forward(w_attn, w_up, w_down, pack_small(b_attn, ln_par, b_up, b_down), x[0], keep, cos, sin)
        g_attn, g_up, g_down, g_small, d_x = backward(weights, vec, cos, sin, x[0], y, d_y[0], saved)
        rows = g_small.reshape(PAIR, LINE, TILE)
        return (d_x[None], g_attn, rows[:, 0].reshape(PAIR, LINE, SHARD), rows[:, 1].reshape(PAIR, LINE, SHARD), g_up, rows[:, PAIR],
                g_down, rows[:, TRIO, :SHARD])

    return jax.shard_map(device_step, mesh=mesh,
                         in_specs=(batch_spec, batch_spec, batch_spec) + weight_specs,
                         out_specs=(batch_spec,) + weight_specs,
                         check_vma=False)
```

time: 723 us -> 498 us (0.69); the launches traced: 711 us -> 497 us
  matrix products: 118 us -> 0 us
  local copies, waits for them, and re-layouts: 87.3 us -> 13.5 us
  other arithmetic: 37.1 us -> 1.23 us
  Pallas kernels: 465 us -> 481 us
    dot_general x35 -> x0, matrix products: 118 us -> none  [the longest x11 51.9 us: dot(): return jnp.dot(a, b, preferred_element_type=jnp.float32)]
    add x15 -> x0, local copies, waits for them, and re-layouts: 16.8 us -> none  [the longest x8 8.43 us: layer_forward(): dot(h_one, w_attn[i]) + b_attn[i]]
    pallas_call x2, Pallas kernels: 465 us -> 481 us  [the longest x1 277 us: backward(): pl.pallas_call(backward_kernel, out_shape=[shape((PAIR, LINE, SHARD, DIM)...]
    reduce_sum x14 -> x0, other arithmetic: 14.2 us -> none  [the longest x2 4.81 us: layer_backward(): gb_qkv = jnp.sum(d_proj, axis=0, dtype=jnp.float32)]
    convert_element_type x8 -> x0, local copies, waits for them, and re-layouts: 13.2 us -> none  [the longest x2 4.04 us: layer_forward(): values = values.astype(jnp.bfloat16)]
    another operation x17 -> x2, local copies, waits for them, and re-layouts: 11.7 us -> 1.35 us  [the longest x1 0.68 us: device_step(): rows[:, 1].reshape(PAIR, LINE, SHARD)]
    convert_element_type x13 -> x1, other arithmetic: 10.6 us -> 0.57 us  [device_step(): keep = (jnp.arange(SEQ)[None] < lengths[0]).astype(F32)]
    unnamed x190 -> x8, local copies, waits for them, and re-layouts: 15.6 us -> 6.65 us
where the time goes in v3:
time: 498 us; the launch traced here: 497 us
  Pallas kernels  481 us (97%)
  local copies, waits for them, and re-layouts  13.5 us (3%)
    pallas_call x1, Pallas kernels, backward(): pl.pallas_call(backward_kernel, out_shape=[shape((PAIR, LINE, SHARD, DIM)...  277 us
    pallas_call x1, Pallas kernels, forward(): pl.pallas_call(forward_kernel, out_shape=[shape((LAYERS, LINE, DIM, DIM),...  204 us

profile of v3, /device:TPU:0, one launch (start us, length us, event | category | flops | bytes accessed | tf_op | source)
XLA Modules:
  0.0 496.9 jit_solution(3631358050906211922)
XLA Ops:
  1.3 0.8 stack_reshape.6
  2.0 0.8 stack_reshape.7
  2.8 0.7 pad_bitcast_fusion
  3.5 0.7 pad_maximum_fusion
  4.1 0.6 copy.20
  4.7 0.6 compare_convert_fusion.refs_5_
  5.3 204.3 %forward.1 = (bf16[2,4,1024,1024]{3,2,1,0:T(8,128)(2,1)}, bf16[2,1024,4096]{2,1,0:T(8,128)(2,1)}, bf16[8192,1024]{1,0:T(8,128)(2,1)}, bf16[256,128]{1,0:T(8,128)...) custom-call(bf16[2,4,32,1024]{3,2,1,0:T(8,128)(2,1)} %refs_0_.1, ...), custom_call_target="tpu_custom_call" | custom-call | tf_op jit(solution)/shard_map/forward/pallas_call | solution.py:549
  209.6 276.5 %backward.1 = (f32[2,4,32,1024]{3,2,1,0:T(8,128)}, f32[2,32,4096]{2,1,0:T(8,128)}, f32[2,128,1024]{2,1,0:T(8,128)}, f32[8,128]{1,0:T(8,128)}, bf16[192,1024]{1,0...) custom-call(bf16[2,4,1024,1024]{3,2,1,0:T(8,128)(2,1)} %get-tuple-el, ...), custom_call_target="tpu_custom_call" | custom-call | tf_op jit(solution)/shard_map/backward/pallas_call | solution.py:924
  486.1 0.0 copy-start.1
  486.1 1.3 slice.19
  487.5 1.4 slice_reduce_fusion
  488.8 0.7 reshape_squeeze.7
  489.5 0.7 reshape_squeeze.6
  490.2 1.8 copy.30
  492.0 2.3 copy.31
  494.3 0.0 copy-done.1
  494.3 0.0 copy-start
  494.3 1.0 copy.32
  495.2 0.6 copy-done
  495.9 1.0 copy.33
Async XLA Ops:
  486.1 8.1 %copy-start.1 = (f32[2,32,4096]{2,1,0:T(8,128)S(1)}, f32[2,32,4096]{2,1,0:T(8,128)}, u32[]{:S(2)}) copy-start(f32[2,32,4096]{2,1,0:T(8,128)} %get-tuple-element.75) | copy-start | bytes 3145732
  494.3 1.6 copy-start

commit v4 on v3

v4 whole, which is shorter than its diff:
```python
import functools
import math
import jax
import jax.numpy as jnp
import numpy as np
from jax import lax
from jax.experimental import pallas as pl
from jax.experimental.pallas import tpu as pltpu
from jax.sharding import PartitionSpec as P

PAIR = 2
TRIO = 3
LINE = 4
FIVE = 5
SIX = 6
PEERS = 7
PLANE = 8
HEADS = 16
DOWN_ROW = 24
SHARD = 32
HEAD_DIM = 64
HALF_SEQ = 96
TILE = 128
SEQ = 192
SPREAD = 224
BAND = 256
WIDE = 512
DIM = 1024
FAR = 1344
QKV_COLS = 3072
FFN = 4096

MESH = pl.DeviceIdType.MESH
EPS = 1e-5
THETA = 10000.0
NEG_BIG = -1e30
SQRT_HALF = math.sqrt(0.5)
DENSITY = 1.0 / math.sqrt(2.0 * math.pi)
SCALE = HEAD_DIM ** -0.5
F32, BF16 = jnp.float32, jnp.bfloat16
DMA = pltpu.SemaphoreType.DMA


def dot(a, b, ca=1, cb=0, precision=None):
    return lax.dot_general(a, b, (((ca,), (cb,)), ((), ())), preferred_element_type=F32, precision=precision)


def span(index, size):
    return pl.ds(pl.multiple_of(size * index, size), size)


def repeat(count, body):
    def step(i, carry):
        body(i)
        return carry

    lax.fori_loop(0, count, step, 0)


def head(ref, rows):
    return ref.at[pl.ds(0, rows), :]


def local(src, dst, sem):
    return pltpu.make_async_copy(src, dst, sem)


def drain(ref, sem):
    local(ref, ref, sem).wait()


def remote(src, dst, send, recv, dev):
    return pltpu.make_async_remote_copy(src_ref=src, dst_ref=dst, send_sem=send, recv_sem=recv,
                                        device_id=(dev,), device_id_type=MESH)


def rotary_tables():
    lane = np.arange(TILE)
    angles = np.arange(SEQ)[:, None] * THETA ** (-(lane % SHARD) / SHARD)[None, :]
    sign = np.where(lane % HEAD_DIM < SHARD, -1.0, 1.0)
    return np.cos(angles).astype(np.float32), (np.sin(angles) * sign).astype(np.float32)


def rotate(block, cos, sin):
    lane = lax.broadcasted_iota(jnp.int32, block.shape, 1)
    return block * cos + jnp.where((lane & SHARD) == 0, pltpu.roll(block, HALF_SEQ, 1), pltpu.roll(block, SHARD, 1)) * sin


def head_masks(block):
    lane = lax.broadcasted_iota(jnp.int32, block.shape, 1)
    zero = jnp.zeros_like(block)
    return jnp.where(lane < HEAD_DIM, block, zero), jnp.where(lane < HEAD_DIM, zero, block)


def row_mean(x):
    return jnp.mean(x, axis=-1, keepdims=True)


def row_sum(x):
    return jnp.sum(x, axis=-1, keepdims=True)


def column_sum(x):
    return jnp.sum(x, axis=0, keepdims=True)


def normed(x):
    centered = x - row_mean(x)
    inv = lax.rsqrt(row_mean(centered * centered) + EPS)
    return centered * inv, inv


def pick(kind):
    shape = (TILE, DIM)
    return lax.broadcasted_iota(jnp.int32, shape, 0) == SHARD * kind + (lax.broadcasted_iota(jnp.int32, shape, 1) & 31)


def owned(swap):
    shape = (SHARD, DIM)
    row = lax.broadcasted_iota(jnp.int32, shape, 0)
    if swap:
        row = (row & TRIO) * PLANE + (row >> PAIR)
    return row == lax.broadcasted_iota(jnp.int32, shape, 1) >> FIVE


def unpack_vectors(small, vec):
    for l in range(PAIR):
        for t in (0, 1, TRIO):
            rows = small[pl.ds(LINE * l + t, SHARD, stride=PLANE), :].astype(BF16)
            for kind in range(1 if t == TRIO else LINE):
                spread = dot(rows, pick(kind).astype(BF16))
                at = DOWN_ROW + l if t == TRIO else PLANE * l + LINE * t + kind
                vec[pl.ds(at, 1), :] = column_sum(jnp.where(owned(False), spread, 0.0))
        for d in range(SHARD):
            vec[pl.ds(HEADS + LINE * l + d // PLANE, 1), pl.ds(d % PLANE * TILE, TILE)] = small[pl.ds(PLANE * d + LINE * l + PAIR, 1), :]


def pack_vectors(vec, packed):
    for l in range(PAIR):
        for t in (0, 1, TRIO):
            total = None
            for kind in range(1 if t == TRIO else LINE):
                at = DOWN_ROW + l if t == TRIO else PLANE * l + LINE * t + kind
                mine = jnp.where(owned(True), vec[pl.ds(at, 1), :], 0.0)
                part = dot(mine, pick(kind).astype(F32), 1, 1, lax.Precision.HIGHEST)
                total = part if total is None else total + part
            packed[pl.ds(LINE * l + t, SHARD, stride=PLANE), :] = total
        for d in range(SHARD):
            packed[pl.ds(SHARD * (d % PLANE) + PLANE * (d // PLANE) + LINE * l + PAIR, 1), :] = vec[pl.ds(HEADS + LINE * l + d // PLANE, 1),
                                                                              pl.ds(d % PLANE * TILE, TILE)]


def norm_stage(src, vec, at, dst):
    def body(i):
        rows = span(i, SHARD)
        unit, _ = normed(src[rows, :].astype(F32))
        dst[rows, :] = (unit * vec[pl.ds(at, 1), :] + vec[pl.ds(at + 1, 1), :]).astype(BF16)

    repeat(SIX, body)


def project_stage(l, h, w, vec, cos, sin, qkv, kind):
    def body(n):
        cols = span(n, BAND)
        out = dot(h[...], w[pl.ds(DIM * kind, DIM), cols]) + vec[pl.ds(PLANE * l + kind, 1), cols]
        if kind == 0:
            out = out * SCALE
        if kind < PAIR:
            out = jnp.concatenate([rotate(out[:, :TILE], cos[...], sin[...]), rotate(out[:, TILE:], cos[...], sin[...])], axis=1)
        qkv[:, pl.ds(pl.multiple_of(DIM * kind + BAND * n, BAND), BAND)] = out.astype(BF16)

    repeat(LINE, body)


def attend_stage(qkv, keep, probs, ctx, first, count):
    def body(i):
        p = first + i
        query = qkv[:, span(p, TILE)]
        keys = head_masks(qkv[:, span(p + PLANE, TILE)])
        vals = head_masks(qkv[:, span(p + HEADS, TILE)])
        out = None
        for h in range(PAIR):
            scores = jnp.where(keep[...] > 0.5, dot(query, keys[h], 1, 1), NEG_BIG)
            grown = jnp.exp(scores - jnp.max(scores, axis=-1, keepdims=True))
            weight = (grown / row_sum(grown)).astype(BF16)
            probs[PAIR * p + h] = weight
            part = dot(weight, vals[h])
            out = part if out is None else out + part
        ctx[:, span(p, TILE)] = out.astype(BF16)

    repeat(count, body)


def residual_stage(a, w, base, bias, vec, dst, first=0, count=LINE):
    def body(i):
        cols = span(first + i, BAND)
        dst[:, cols] = (base[:, cols].astype(F32) + dot(a[...], w[:, cols]) + vec[pl.ds(bias, 1), cols]).astype(BF16)

    repeat(count, body)


def gelu(pre):
    cdf = 0.5 * (1.0 + lax.erf(pre * SQRT_HALF))
    return pre * cdf, cdf + pre * (jnp.exp(-0.5 * pre * pre) * DENSITY)


def up_stage(l, h, w, vec, act, slope, part):
    def body(n):
        cols, here = span(LINE * part + n, BAND), span(n, BAND)
        pre = dot(h[...], w[pl.ds(DIM * part, DIM), here]) + vec[pl.ds(HEADS + LINE * l + part, 1), here]
        out, slope[:, cols] = gelu(pre)
        act[:, cols] = out.astype(BF16)

    repeat(LINE, body)


def fold(block):
    return sum(block[PLANE * i:PLANE * i + PLANE] for i in range(block.shape[0] // PLANE))


def act_grad_stage(part, d_out, w, slope, d_pre, vec, row):
    def body(n):
        cols, local_cols = span(LINE * part + n, BAND), span(n, BAND)
        grad = dot(d_out[...], w[span(n, BAND), :], 1, 1) * slope[:, local_cols]
        d_pre[:, cols] = grad.astype(BF16)
        vec[pl.ds(row + part, 1), local_cols] = column_sum(grad)

    repeat(LINE, body)


def norm_grad_stage(src, d_h, d_res, gain, vec, row_gain, row_out, row_res, dst):
    zero = jnp.zeros((PLANE, DIM), F32)

    def body(i, carry):
        rows = span(i, SHARD)
        unit, inv = normed(src[rows, :].astype(F32))
        grad = d_h[rows, :]
        scaled = grad * gain
        inner = scaled - row_mean(scaled) - unit * row_mean(scaled * unit)
        res = d_res[rows, :].astype(F32)
        out = (res + inv * inner).astype(BF16)
        dst[rows, :] = out
        return tuple(c + fold(v) for c, v in zip(carry, (grad * unit, grad, out.astype(F32), res)))

    sums = lax.fori_loop(0, SIX, body, (zero,) * LINE)
    for at, value in zip((row_gain, row_gain + 1, row_out, row_res), sums):
        if at is not None:
            vec[pl.ds(at, 1), :] = column_sum(value)


def attend_grad_stage(l, qkv, probs, d_ctx, cos, sin, d_proj, vec):
    def body(p):
        keys = head_masks(qkv[:, span(p + PLANE, TILE)])
        queries = head_masks(qkv[:, span(p, TILE)])
        vals = qkv[:, span(p + HEADS, TILE)]
        outs = head_masks(d_ctx[:, span(p, TILE)])
        d_q = d_k = d_v = 0.0
        for h in range(PAIR):
            weight = probs[PAIR * p + h]
            wide = weight.astype(F32)
            d_weight = dot(outs[h], vals, 1, 1)
            d_score = (wide * (d_weight - row_sum(d_weight * wide))).astype(BF16)
            d_v = d_v + dot(weight, outs[h], 0, 0)
            d_q = d_q + dot(d_score, keys[h])
            d_k = d_k + dot(d_score, queries[h], 0, 0)
        d_q = rotate(d_q, cos[...], -sin[...]) * SCALE
        d_k = rotate(d_k, cos[...], -sin[...])
        for kind, grad in enumerate((d_q, d_k, d_v)):
            grad = grad.astype(BF16)
            d_proj[:, span(p + PLANE * kind, TILE)] = grad
            vec[pl.ds(PLANE * l + kind, 1), span(p, TILE)] = column_sum(grad.astype(F32))

    repeat(PLANE, body)


FORWARD_ORDER = (
    "O0", "O1", "O2", "P1_0", "P0_0", "O3", "O4", "O5", "O6", "Z4_1", "Z0_1m", "P3_0", "O7", "P2_0", "P4_0", "O8",
    "Z4_2", "Z8_1", "Z0_1p", "Z2_1m", "Z1_1m", "Z2_1p", "Z3_1", "Z4_3", "Z1_1p", "Z8_2", "Z1_2m", "P7_0", "Z7_1",
    "Z0_2m", "aua", "Z3_2", "Z0_2p", "Z1_2p", "Z8_3", "P8_0", "Z1_3m", "P5_0", "P6_0", "Z3_3", "Z2_2m", "Z2_2p",
    "Z0_3m", "Z5_1m", "P3_1", "Z2_3m", "Z6_1m", "Z0_3p", "Z6_1p", "P4_1", "Z2_3p", "P4_2", "P3_2", "P3_3", "Q0",
    "Z1_3p", "Z5_1p", "N0", "P4_3", "Z7_2", "Z5_2m", "Q2", "Z7_3", "Q1", "Z5_2p", "PJ0", "PJ1", "Z6_2m", "Z6_2p",
    "wua", "Szu", "PJ2", "AT0", "Z6_3m", "Z6_3p", "P8_1", "AT1", "Q4", "Z5_3m", "Szd", "Q3", "Z5_3p", "P8_2", "AT2",
    "AT3", "P7_1", "RE0", "UP0", "UP1", "P7_2", "Q6", "P8_3", "Q5", "zd_1", "P7_3", "UP2", "UP3", "DN0", "DN1",
    "Bdy", "Q8", "Q7", "DN2", "zu_1", "DN3", "pj0", "pj1", "pj2", "at0", "Rdy", "at1", "at2", "at3", "re0", "Bh2",
    "zd_2", "zu_2", "Rh2", "Ldy", "Lh2", "zd_3", "zu_3", "G",
)
BACKWARD_ORDER = (
    "B2", "X1", "X1d", "P0", "X1x", "R2", "P1", "B3", "Y1", "S2", "C2", "R3", "L2", "C3", "S3", "L3", "H0a", "C4",
    "P2", "S4", "H1a", "B4", "C5", "P3", "R4", "S5", "H3a", "H2a", "L4", "P4", "B5", "I0", "S6", "H0b", "H4a",
    "H1b", "R5", "C6", "B6", "I4", "I3", "L5", "B7", "I1", "H4b", "P5", "H3b", "H5a", "R6", "R7", "I2", "S7", "H5b",
    "L7", "L6", "I5", "P6", "P7", "H6a", "H2b", "H6b", "H7a", "F5", "F3", "F2", "I6", "H7b", "F6", "I7", "F4", "F0",
    "C7", "F7", "F1", "END",
)


LAYERS = PAIR
UNITS = [(0, SIX)] + [(0, piece) for piece in range(SIX)] + [(1, 0), (1, 1)]
ROUTES = [("b", 0, 1)] + [("b", 0, 1), ("b", 1, 0), ("a", 0, 1), ("a", 1, 0)] * LAYERS


SAVED = ("h1", "qkv", "probs", "ctx", "mid", "h2", "act", "slope")
KEPT = [(l, name) for l in range(LAYERS) for name in SAVED[:PLANE - PAIR * l]]
SAVED_SHAPES = {"h1": (SEQ, DIM), "qkv": (SEQ, QKV_COLS), "probs": (HEADS, SEQ, SEQ), "ctx": (SEQ, DIM), "mid": (SEQ, DIM),
                "h2": (SEQ, DIM), "act": (SEQ, FFN), "slope": (SEQ, FFN)}


def saved_type(name):
    return F32 if name == "slope" else BF16


def plane_cast(peer, far, sems):
    send, recv, push_send, push_recv = sems

    def block(r, half):
        return far.at[pl.ds(SEQ * (r - 1) + HALF_SEQ * half, HALF_SEQ), :]

    def push(r, half):
        remote(block(r, half), block(r + 1, half), push_send, push_recv, peer(1)).start()

    def start(src):
        for r in (PAIR, LINE):
            for half in (0, 1):
                remote(src.at[pl.ds(HALF_SEQ * half, HALF_SEQ), :], block(r, half), send, recv.at[r - PAIR + half], peer(r)).start()
        remote(src, head(far, SEQ), push_send, push_recv, peer(1)).start()

    def relay():
        for r, half, onward in ((PAIR, 0, LINE), (LINE, 1, PAIR), (PAIR, 1, None), (LINE, 0, None)):
            drain(block(r, half), recv.at[r - PAIR + half])
            if onward is not None:
                remote(block(r, half), block(SIX, half), send, recv.at[LINE + half], peer(onward)).start()
            push(r, half)

    def last():
        for half in (0, 1):
            drain(block(SIX, half), recv.at[LINE + half])
            push(SIX, half)

    def arrived():
        drain(head(far, 768), push_recv)

    def sent():
        drain(head(far, 576), send)
        drain(head(far, 768), push_send)

    return start, relay, last, arrived, sent


def plane_peer(me, core, xc, yc):
    def peer(r):
        out = me
        if r & 1:
            out = out + 1 - PAIR * core
        if r & PAIR:
            out = out + PAIR - LINE * xc
        if r & LINE:
            out = out + LINE - PLANE * yc
        return out

    return peer


def in_order(order, tasks):
    assert sorted(order) == sorted(tasks)
    for name in order:
        tasks[name]()


def forward_kernel(*refs):
    (wa, wu, wd, sm, x, keep, cos, sin, d_y), refs = refs[:9], refs[9:]
    (fa, fu, fd, fs, fu_mine, fd_mine, h_far, dy_far, out_vec, out_mid), refs = refs[:10], refs[10:]
    saved, refs = dict(zip(KEPT, refs)), refs[len(KEPT):]
    (va, vu, vd, vs), refs = refs[:LINE], refs[LINE:]
    acts, refs = dict(zip(KEPT, refs)), refs[len(KEPT):]
    (y, vec, small_in, small, w_even, w_odd, load_sem, save_sem, own_sem, xy_sem, z_sem, push_send, push_recv,
     recv_sem, line_send, line_recv, spread_send, spread_recv, mine_sem, bc_send, bc_recv, bp_send, bp_recv) = refs
    me = lax.axis_index("fsdp")
    core, xc, yc, zc = me % PAIR, (me // PAIR) % PAIR, (me // LINE) % PAIR, me // PLANE
    partner = me + 1 - PAIR * core
    near = (me + PAIR - LINE * xc, me + LINE - PLANE * yc)
    up, down = me + PLANE, me - PLANE
    has_up, has_down = zc < TRIO, zc > 0

    def full(u, src):
        layer, piece = UNITS[u]
        if piece < PAIR:
            return fa.at[layer, pl.ds(PAIR * piece, PAIR), pl.ds(pl.multiple_of(SHARD * src, SHARD), SHARD), :]
        if piece < LINE:
            return fu.at[pl.ds(pl.multiple_of(SHARD * src + HEADS * (piece - PAIR), HEADS), HEADS), :]
        if piece < SIX:
            return fd.at[pl.ds(pl.multiple_of(TILE * src + HEAD_DIM * (piece - LINE), HEAD_DIM), HEAD_DIM), :]
        return fs.at[pl.ds(pl.multiple_of(PLANE * src, PLANE), PLANE), :]

    def own(u):
        layer, piece = UNITS[u]
        if piece < PAIR:
            return va.at[layer, pl.ds(PAIR * piece, PAIR)]
        if piece < LINE:
            return vu.at[layer, pl.ds(HEADS * (piece - PAIR), HEADS), :]
        if piece < SIX:
            return vd.at[layer, pl.ds(HEAD_DIM * (piece - LINE), HEAD_DIM), :]
        return vs

    def kind(u):
        return UNITS[u][1] // PAIR

    def order(u):
        return ROUTES[u]

    def tiny(u):
        return 1 if UNITS[u][1] == SIX else 0

    peer = plane_peer(me, core, xc, yc)
    barrier = pltpu.get_barrier_semaphore()
    for r in range(1, PLANE):
        pl.semaphore_signal(barrier, inc=1, device_id=(peer(r),), device_id_type=MESH)

    @pl.when(has_up)
    def _():
        pl.semaphore_signal(barrier, inc=1, device_id=(up,), device_id_type=MESH)

    @pl.when(has_down)
    def _():
        pl.semaphore_signal(barrier, inc=1, device_id=(down,), device_id_type=MESH)

    loads = [local(src, dst, load_sem.at[i])
             for i, (src, dst) in enumerate(((wa, va), (wu, vu), (wd, vd), (sm, vs)))]
    for load in loads:
        load.start()
    for load in loads:
        load.wait()
    pl.semaphore_wait(barrier, PEERS + has_up.astype(jnp.int32) + has_down.astype(jnp.int32))

    def slab(u, src_ref, src, send, recv, dev):
        return remote(src_ref, full(u, src), send, recv, dev)

    def send_z(u, src_ref, src, slot, above, below):
        if above is not None:
            @pl.when(above)
            def _():
                slab(u, src_ref, src, z_sem.at[u], recv_sem.at[u, slot], up).start()
        if below is not None:
            @pl.when(below)
            def _():
                slab(u, src_ref, src, z_sem.at[u], recv_sem.at[u, slot], down).start()

    def send_xy(u, src_ref, src, dim, slot):
        slab(u, src_ref, src, xy_sem.at[u], recv_sem.at[u, slot], near[dim]).start()

    def push(u, src_ref, src):
        slab(u, src_ref, src, push_send.at[kind(u)], push_recv.at[u], partner).start()

    def column(flip_p, p):
        base = me - PLANE * zc
        if flip_p:
            base = base + (near[p] - me)
        return base

    def arrived(u, src, slot):
        slab(u, full(u, src), src, xy_sem.at[u], recv_sem.at[u, slot], me).wait_recv()
        return full(u, src)

    def stage0(u):
        col, p, q = order(u)
        mine = own(u)
        send_z(u, mine, me, zc, has_up, has_down)
        send_xy(u, mine, me, p, LINE + zc)
        send_xy(u, mine, me, q, PLANE)
        push(u, mine, me)
        local(mine, full(u, me), own_sem.at[u]).start()

    def z_arrival(u, dz, steps, flips, send_p):
        col, p, q = order(u)
        for step in steps:
            for flip_p in flips:
                zs = zc + step * dz
                src = column(flip_p, p) + PLANE * zs
                slot = LINE * flip_p + zs
                present = (zc >= dz) if step < 0 else (zc <= TRIO - dz)

                @pl.when(present)
                def _(src=src, slot=slot, step=step):
                    ref = arrived(u, src, slot)
                    send_z(u, ref, src, slot, has_up if step < 0 else None, has_down if step > 0 else None)
                    if send_p:
                        send_xy(u, ref, src, p, LINE + slot)
                    send_xy(u, ref, src, q, PLANE)
                    push(u, ref, src)

    def p_arrival(u, hop):
        col, p, q = order(u)
        zs = lax.rem(zc + hop, LINE)
        src = column(1, p) + PLANE * zs
        ref = arrived(u, src, LINE + zs)
        if col == "b":
            send_z(u, ref, src, LINE + zs, has_up, has_down)
        send_xy(u, ref, src, q, PLANE)
        push(u, ref, src)

    def q_arrivals(u):
        col, p, q = order(u)
        rows = head(fs, HEAD_DIM) if tiny(u) else head(fd, WIDE)
        drain(rows, recv_sem.at[u, PLANE])
        for flip_p in (0, 1):
            base = column(flip_p, p) + (near[q] - me)

            def body(zs, base=base):
                src = base + PLANE * zs
                push(u, full(u, src), src)

            repeat(LINE, body)

    place = me % PLANE

    def mine_cols(where):
        return [(pl.multiple_of(DIM * i + TILE * where, TILE), TILE * i) for i in range(LINE)]

    def spread():
        rows = pl.ds(pl.multiple_of(SHARD * me, SHARD), SHARD)
        for r in (SIX, PAIR, LINE, PEERS, TRIO, FIVE, 1):
            for src, dst in mine_cols(peer(r) % PLANE):
                remote(vu.at[1, :, pl.ds(src, TILE)], fu_mine.at[rows, pl.ds(dst, TILE)], spread_send, spread_recv, peer(r)).start()
        for src, dst in mine_cols(place):
            local(vu.at[1, :, pl.ds(src, TILE)], fu_mine.at[rows, pl.ds(dst, TILE)], mine_sem.at[1]).start()
        local(vd.at[1], fd_mine.at[pl.ds(pl.multiple_of(TILE * zc, TILE), TILE), :], mine_sem.at[0]).start()

    def spread_done():
        drain(head(fu_mine, SPREAD), spread_recv)
        drain(head(fu_mine, SHARD), mine_sem.at[1])

    def line_block(k, zs):
        size = BAND if k else TILE
        return (fu_mine if k else fd_mine).at[pl.ds(pl.multiple_of(size * zs, size), size), :]

    def line_send_on(k, src, zs, above, below):
        for want, dev in ((above, up), (below, down)):
            if want is not None:
                @pl.when(want)
                def _(dev=dev):
                    remote(src, line_block(k, zs), line_send.at[k], line_recv.at[k, zs], dev).start()

    def line_start(k):
        line_send_on(k, line_block(1, zc) if k else vd.at[1], zc, has_up, has_down)

    def line_hop(k, dz):
        for step in (-1, 1):
            zs = zc + step * dz

            @pl.when((zc >= dz) if step < 0 else (zc <= TRIO - dz))
            def _(zs=zs, step=step):
                drain(line_block(k, zs), line_recv.at[k, zs])
                line_send_on(k, line_block(k, zs), zs, has_up if step < 0 else None, has_down if step > 0 else None)

    casts = [plane_cast(peer, far, (bc_send.at[i], bc_recv.at[i], bp_send.at[i], bp_recv.at[i]))
             for i, far in enumerate((dy_far, h_far))]

    def ready(*units):
        for u in units:
            drain(head(fs, TILE) if tiny(u) else head(fd, DIM), push_recv.at[u])
            drain(own(u), own_sem.at[u])

    def fetch(l, what, buf):
        for i in range(LINE):
            src = {"a": lambda: fa.at[l, i], "u": lambda: fu.at[:, pl.ds(DIM * i, DIM)],
                   "d": lambda: fd.at[pl.ds(DIM * i, DIM), :]}[what]()
            local(src, buf.at[pl.ds(DIM * i, DIM), :], load_sem.at[i]).start()

    def fetched(buf, *chunks):
        for i in chunks:
            drain(buf.at[pl.ds(DIM * i, DIM), :], load_sem.at[i])

    def save(l, *names):
        for name in names:
            local(acts[l, name], saved[l, name], save_sem.at[l, SAVED.index(name)]).start()

    def source(l):
        return y if l else x

    def begin():
        ready(0)
        local(fs, small_in, load_sem.at[0]).start()
        drain(small_in, load_sem.at[0])
        small[...] = small_in[...].astype(F32)
        unpack_vectors(small, vec)
        local(vec, out_vec, save_sem.at[0, PLANE]).start()
        norm_stage(x, vec, LINE, acts[0, "h1"])
        save(0, "h1")

    def project(l, buf, kind):
        if kind == 0:
            first = 1 + SIX * l
            ready(first, first + 1)
            fetch(l, "a", buf)
        fetched(buf, kind)
        project_stage(l, acts[l, "h1"], buf, vec, cos, sin, acts[l, "qkv"], kind)
        if kind == PAIR:
            save(l, "qkv")

    def attend(l, part):
        attend_stage(acts[l, "qkv"], keep, acts[l, "probs"], acts[l, "ctx"], PAIR * part, PAIR)

    def settle(l, buf):
        save(l, "probs", "ctx")
        fetched(buf, TRIO)
        residual_stage(acts[l, "ctx"], buf.at[pl.ds(QKV_COLS, DIM), :], source(l), PLANE * l + TRIO, vec, acts[l, "mid"])
        norm_stage(acts[l, "mid"], vec, PLANE * l + SIX, acts[l, "h2"])
        save(l, "mid", "h2")

    def grow(buf, part):
        if part == 0:
            ready(TRIO, LINE)
            fetch(0, "u", buf)
        fetched(buf, part)
        up_stage(0, acts[0, "h2"], buf, vec, acts[0, "act"], acts[0, "slope"], part)
        if part == TRIO:
            save(0, "act", "slope")

    def shrink(buf, n):
        if n == 0:
            ready(FIVE, SIX)
            fetch(0, "d", buf)
            fetched(buf, 0, 1, PAIR, TRIO)
        residual_stage(acts[0, "act"], buf, acts[0, "mid"], DOWN_ROW, vec, y, n, 1)
        if n == TRIO:
            local(y, out_mid, save_sem.at[1, PLANE]).start()
            norm_stage(y, vec, 12, acts[1, "h1"])
            save(1, "h1")

    def gathered():
        for cast in casts:
            cast[TRIO]()

    tasks = {"N0": begin, "RE0": lambda: settle(0, w_even), "re0": lambda: settle(1, w_odd), "aua": spread, "wua": spread_done,
             "Szd": lambda: line_start(0), "Szu": lambda: line_start(1), "Bdy": lambda: casts[0][0](d_y),
             "Bh2": lambda: casts[1][0](acts[1, "h2"]), "Rdy": casts[0][1], "Rh2": casts[1][1], "Ldy": casts[0][PAIR],
             "Lh2": casts[1][PAIR], "G": gathered}
    for i in range(TRIO):
        tasks[f"PJ{i}"] = functools.partial(project, 0, w_even, i)
        tasks[f"pj{i}"] = functools.partial(project, 1, w_odd, i)
        for k, name in enumerate(("zd", "zu")):
            tasks[f"{name}_{i + 1}"] = functools.partial(line_hop, k, i + 1)
    for i in range(LINE):
        tasks[f"AT{i}"] = functools.partial(attend, 0, i)
        tasks[f"at{i}"] = functools.partial(attend, 1, i)
        tasks[f"UP{i}"] = functools.partial(grow, w_odd, i)
        tasks[f"DN{i}"] = functools.partial(shrink, w_even, i)
    for u in range(len(UNITS)):
        tasks[f"O{u}"] = functools.partial(stage0, u)
        tasks[f"Q{u}"] = functools.partial(q_arrivals, u)
        for dz in (1, PAIR, TRIO):
            if order(u)[0] == "a":
                tasks[f"Z{u}_{dz}"] = functools.partial(z_arrival, u, dz, (-1, 1), (0,), True)
            else:
                tasks[f"Z{u}_{dz}m"] = functools.partial(z_arrival, u, dz, (-1,), (0, 1), False)
                tasks[f"Z{u}_{dz}p"] = functools.partial(z_arrival, u, dz, (1,), (0, 1), False)
        for hop in range(LINE if order(u)[0] == "a" else 1):
            tasks[f"P{u}_{hop}"] = functools.partial(p_arrival, u, hop)
    in_order(FORWARD_ORDER, tasks)

    ends = jnp.logical_or(zc == 0, zc == TRIO)
    middle = jnp.logical_not(ends)

    def rows_of(u, units):
        return head(fs, PLANE * units) if tiny(u) else head(fd, HEAD_DIM * units)

    for u in range(len(UNITS)):
        straight = order(u)[0] == "a"
        drain(rows_of(u, 12 if straight else 9), xy_sem.at[u])
        for case, units in ((ends, 1), (middle, FIVE)):
            @pl.when(case)
            def _(u=u, units=units, straight=straight):
                drain(rows_of(u, units if straight else PAIR * units), z_sem.at[u])
    for k in range(PAIR):
        for case, units in ((ends, 1), (middle, FIVE)):
            @pl.when(case)
            def _(k=k, units=units):
                drain(head(fd, TILE * units), line_send.at[k])
    drain(head(fu_mine, SPREAD), spread_send)
    drain(head(fd_mine, TILE), mine_sem.at[0])
    for cast in casts:
        cast[LINE]()
    halves = (fa.at[0], head(fu, WIDE), head(fd, 2048), head(fs, TILE))
    for i, half in enumerate(halves):
        drain(half, push_send.at[i])
    for l, name in KEPT:
        drain(saved[l, name], save_sem.at[l, SAVED.index(name)])
    drain(out_vec, save_sem.at[0, PLANE])
    drain(out_mid, save_sem.at[1, PLANE])


def forward(w_attn, w_up, w_down, small, x, keep, cos, sin, d_y):
    shape, hbm, vmem = jax.ShapeDtypeStruct, pl.BlockSpec(memory_space=pltpu.HBM), pl.BlockSpec(memory_space=pltpu.VMEM)
    kept = [shape(SAVED_SHAPES[name], saved_type(name)) for _, name in KEPT]
    outs = pl.pallas_call(
        forward_kernel,
        out_shape=[shape((LAYERS, LINE, DIM, DIM), BF16), shape((DIM, FFN), BF16), shape((FFN, DIM), BF16),
                   shape((BAND, TILE), BF16), shape((DIM, WIDE), BF16), shape((WIDE, DIM), BF16), shape((FAR, DIM), BF16),
                   shape((FAR, DIM), BF16), shape((SHARD, DIM), F32), shape((SEQ, DIM), BF16)] + kept,
        in_specs=[hbm] * LINE + [vmem] * LINE + [hbm],
        out_specs=[hbm] * (10 + len(kept)),
        scratch_shapes=[pltpu.VMEM(w.shape, BF16) for w in (w_attn, w_up, w_down, small)]
        + [pltpu.VMEM(k.shape, k.dtype) for k in kept]
        + [pltpu.VMEM((SEQ, DIM), BF16), pltpu.VMEM((SHARD, DIM), F32), pltpu.VMEM((BAND, TILE), BF16),
           pltpu.VMEM((BAND, TILE), F32), pltpu.VMEM((FFN, DIM), BF16), pltpu.VMEM((FFN, DIM), BF16),
           DMA((LINE,)), DMA((PAIR, 9)), DMA((len(UNITS),)), DMA((len(UNITS),)), DMA((len(UNITS),)), DMA((LINE,)), DMA((len(UNITS),)),
           DMA((len(UNITS), 9)), DMA((PAIR,)), DMA((PAIR, LINE)), DMA, DMA, DMA((PAIR,)), DMA((PAIR,)), DMA((PAIR, SIX)), DMA((PAIR,)), DMA((PAIR,))],
        compiler_params=pltpu.CompilerParams(collective_id=0, has_side_effects=True, vmem_limit_bytes=60 * DIM * DIM),
        name="forward",
    )(w_attn, w_up, w_down, small, x, keep, cos, sin, d_y)
    return outs[:TRIO], outs[LINE:PLANE], outs[PLANE], outs[9], dict(zip(KEPT, outs[10:]))


PIECES = [(1, name) for name in "UDOQ"] + [(0, name) for name in "DUOQ"]
WIDTH = {"D": WIDE, "U": WIDE, "O": TILE, "Q": 384}
ROWS = SEQ


def acc_shape(name):
    return (WIDE, DIM) if name == "D" else (DIM, WIDTH[name])


def backward_kernel(*refs):
    n = len(PIECES)
    (fa, fu, fd, vec, cos, sin, x_in, y_in, d_y, fu_mine, fd_mine, h_far, dy_far), refs = refs[:13], refs[13:]
    saved, refs = dict(zip(KEPT, refs)), refs[len(KEPT):]
    (g_attn, g_up, g_down, g_small, d_x), refs = refs[:FIVE], refs[FIVE:]
    bc_far, sl_far, refs = (None, None) + refs[:n - PAIR], (None, None) + refs[n - PAIR:PAIR * n - LINE], refs[PAIR * n - LINE:]
    (d_pre_far, d_mid_far, d_proj_far, d_top, pair_far, cross_far), refs = refs[:SIX], refs[SIX:]
    (bc_v, sl_v, sl_w), refs = refs[:TRIO], refs[TRIO:]
    acc, got, refs = refs[:n], refs[n:PAIR * n], refs[PAIR * n:]
    (sum_v, sum_got, sum_line, square, wide, slope_v, qkv_v, probs_v, mid_v, x_v, d_out, d_pre, d_mid, d_proj, d_ctx, d_h,
     g_vec, up_v, down_v, odd_v, even_v), refs = refs[:21], refs[21:]
    (bc_send, bc_recv, push_send, push_recv, sl_send, sl_recv, load_sem, rs_send, rs_recv, out_send, out_recv, own_sem,
     sum_send, sum_recv, square_sem, slope_sem, wide_sem, act_sem, spill_sem, pair_send, pair_recv, cross_send,
     cross_recv) = refs
    bc_in = [None, None, saved[1, "ctx"], saved[1, "h1"], d_top, saved[0, "h2"], saved[0, "ctx"], saved[0, "h1"]]
    sl_in = [None, None, d_mid_far.at[1], d_proj_far.at[1], saved[0, "act"], d_pre_far, d_mid_far.at[0], d_proj_far.at[0]]

    me = lax.axis_index("fsdp")
    core, xc, yc, zc = me % PAIR, (me // PAIR) % PAIR, (me // LINE) % PAIR, me // PLANE
    place = me % PLANE

    peer = plane_peer(me, core, xc, yc)

    def line(k):
        return place + PLANE * lax.rem(zc + k, LINE)

    barrier = pltpu.get_barrier_semaphore()
    for r in range(1, PLANE):
        pl.semaphore_signal(barrier, inc=1, device_id=(peer(r),), device_id_type=MESH)
    for k in range(1, LINE):
        pl.semaphore_signal(barrier, inc=1, device_id=(line(k),), device_id_type=MESH)
    pl.semaphore_wait(barrier, 10)

    casts = [None, None] + [plane_cast(peer, bc_far[u], (bc_send.at[u], bc_recv.at[u], push_send.at[u], push_recv.at[u]))
                            for u in range(PAIR, n)]

    def blocks(u, where):
        name = PIECES[u][1]
        if name == "D":
            return [(pl.multiple_of(DIM * i + TILE * where, TILE), TILE * i, TILE) for i in range(LINE)]
        if name == "Q":
            return [(pl.multiple_of(DIM * i + TILE * where, TILE), TILE * i, TILE) for i in range(TRIO)]
        return [(pl.multiple_of(WIDTH[name] * where, TILE), 0, WIDTH[name])]

    def send_sl(u):
        for r in (PAIR, SIX, LINE, TRIO, PEERS, FIVE, 1):
            for src, dst, width in blocks(u, peer(r) % PLANE):
                remote(sl_in[u].at[:, pl.ds(src, width)], sl_far[u].at[pl.ds(SEQ * (r - 1), SEQ), pl.ds(dst, width)],
                       sl_send.at[u], sl_recv.at[u], peer(r)).start()

    def collect(u):
        name = PIECES[u][1]
        own = [local(bc_in[u], head(bc_v, SEQ), load_sem.at[0])]
        for i, (src, dst, width) in enumerate(blocks(u, place)):
            own.append(local(sl_in[u].at[:, pl.ds(src, width)], sl_v.at[pl.ds(0, SEQ), pl.ds(dst, width)],
                             load_sem.at[1 + i]))
        for c in own:
            c.start()
        drain(sl_far[u], sl_recv.at[u])
        casts[u][TRIO]()
        rest = [local(bc_far[u], bc_v.at[pl.ds(SEQ, FAR), :], load_sem.at[FIVE]),
                local(sl_far[u], sl_v.at[pl.ds(SEQ, FAR), pl.ds(0, WIDTH[name])], load_sem.at[SIX])]
        for c in rest:
            c.start()
        for c in own + rest:
            c.wait()

    def piece_rows(u):
        return acc_shape(PIECES[u][1])[0] // LINE

    def piece(ref, u, d):
        pr = piece_rows(u)
        return ref.at[pl.ds(pl.multiple_of(pr * d, pr), pr), :]

    def step_down_line(u, d, up):
        side = jnp.where(up, 0, 1)
        dst = got[u].at[side, span(d - 1 + side, piece_rows(u)), :]
        remote(piece(acc[u], u, d), dst, rs_send.at[u], rs_recv.at[u, side, d], me + jnp.where(up, PLANE, -PLANE)).start()

    def add_piece(u, side, d):
        pr = piece_rows(u)
        drain(piece(acc[u], u, d), rs_recv.at[u, side, d])
        rows = SHARD

        def body(i, carry):
            at = pl.ds(pl.multiple_of(pr * d + rows * i, rows), rows)
            there = pl.ds(pl.multiple_of(pr * (d - 1 + side) + rows * i, rows), rows)
            acc[u][at, :] = acc[u][at, :] + got[u][side, there, :]
            return carry

        lax.fori_loop(0, pr // rows, body, 0)

    def product(u):
        if u > 1:
            collect(u)
        if u == 1:
            load_all(d_y, dy_far)
        name = PIECES[u][1]
        pr, width = piece_rows(u), WIDTH[name]
        cols_v = sl_w if u == 0 else sl_v

        def body(d, carry):
            at = pl.ds(pl.multiple_of(pr * d, pr), pr)
            if name == "D":
                lhs, rhs = cols_v[:, at], bc_v[...]
            else:
                lhs, rhs = bc_v[:, at], cols_v[:, pl.ds(0, width)]
            acc[u][at, :] = lax.dot_general(lhs, rhs, (((0,), (0,)), ((), ())), preferred_element_type=jnp.float32)
            return carry

        lax.fori_loop(0, LINE, body, 0)

        @pl.when(jnp.logical_or(zc == 0, zc == TRIO))
        def _():
            for hop in range(TRIO):
                step_down_line(u, jnp.where(zc == 0, TRIO - hop, hop), zc == 0)

    def second_hop(u, hop):
        @pl.when(jnp.logical_or(zc == 1, zc == PAIR))
        def _():
            d = jnp.where(zc == 1, TRIO - hop, hop)
            add_piece(u, jnp.where(zc == 1, 0, 1), d)
            step_down_line(u, d, zc == 1)

    def third_hop(u):
        @pl.when(jnp.logical_or(zc == 1, zc == PAIR))
        def _():
            d = jnp.where(zc == 1, 0, TRIO)
            add_piece(u, jnp.where(zc == 1, 1, 0), d)
            step_down_line(u, d, zc == PAIR)

    def finish(u):
        layer, name = PIECES[u]

        @pl.when(zc > 0)
        def _():
            add_piece(u, 0, zc)

        @pl.when(zc < TRIO)
        def _():
            add_piece(u, 1, zc)

        if name == "D":
            local(piece(acc[u], u, zc), g_down.at[layer], own_sem.at[u]).start()
            return
        for r in range(PLANE):
            at = pl.ds(pl.multiple_of(BAND * zc + SHARD * (peer(r) % PLANE), SHARD), SHARD)
            if name == "U" and layer:
                pairs = [(acc[u].at[at, pl.ds(TILE * i, TILE)],
                          g_up.at[layer, :, pl.ds(pl.multiple_of(DIM * i + TILE * place, TILE), TILE)]) for i in range(LINE)]
            elif name == "U":
                pairs = [(acc[u].at[at, :], g_up.at[layer, :, pl.ds(pl.multiple_of(WIDE * place, WIDE), WIDE)])]
            else:
                mats = (TRIO,) if name == "O" else (0, 1, PAIR)
                pairs = [(acc[u].at[at, pl.ds(TILE * i, TILE)],
                          g_attn.at[layer, m, :, pl.ds(pl.multiple_of(TILE * place, TILE), TILE)]) for i, m in enumerate(mats)]
            for src, dst in pairs:
                if r == 0:
                    local(src, dst, own_sem.at[u]).start()
                else:
                    remote(src, dst, out_send.at[u], out_recv.at[u], peer(r)).start()

    def sums_plane():
        for r in range(1, PLANE):
            remote(sum_v.at[pl.ds(pl.multiple_of(SHARD * (peer(r) % PLANE), SHARD), SHARD), :], sum_got.at[pl.ds(SHARD * (r - 1), SHARD), :],
                   sum_send.at[0], sum_recv.at[0], peer(r)).start()

    def sums_line():
        drain(sum_got, sum_recv.at[0])
        total = sum_v[pl.ds(pl.multiple_of(SHARD * place, SHARD), SHARD), :]
        for r in range(1, PLANE):
            total = total + sum_got[pl.ds(SHARD * (r - 1), SHARD), :]
        sum_line[pl.ds(0, SHARD), :] = total
        for i in range(LINE):
            at = pl.ds(PLANE * i + SIX, 1)
            sum_line[at, :] = sum_line[at, :] + g_vec[pl.ds(30, 1), pl.ds(TILE * i, TILE)]
        for k in range(1, LINE):
            remote(sum_line.at[pl.ds(pl.multiple_of(PLANE * lax.rem(zc + k, LINE), PLANE), PLANE), :],
                   sum_line.at[pl.ds(SHARD + PLANE * (k - 1), PLANE), :], sum_send.at[1], sum_recv.at[1], line(k)).start()

    def sums_end():
        drain(head(sum_line, DOWN_ROW), sum_recv.at[1])
        total = sum_line[pl.ds(pl.multiple_of(PLANE * zc, PLANE), PLANE), :]
        for k in range(1, LINE):
            total = total + sum_line[pl.ds(SHARD + PLANE * (k - 1), PLANE), :]
        g_small[...] = total

    squares = [(1, k) for k in range(LINE, PLANE)] + [(0, k) for k in range(PLANE)]
    taken = [0, 0]

    def fetch_square(i):
        if i < len(squares):
            l, k = squares[i]
            src = fd.at[pl.ds(DIM * k, DIM), :] if k < LINE else fa.at[l, (TRIO, 0, 1, PAIR)[k - LINE]]
            local(src, square.at[i % PAIR], square_sem.at[i % PAIR]).start()
            if k < LINE:
                local(saved[0, "slope"].at[:, pl.ds(DIM * k, DIM)], slope_v.at[i % PAIR], slope_sem.at[i % PAIR]).start()

    def fetch_wide(i):
        if i < PLANE:
            local(fu.at[pl.ds(TILE * i, TILE), :], wide.at[i % PAIR], wide_sem.at[i % PAIR]).start()

    def with_square(body):
        i = taken[0]
        drain(square.at[i % PAIR], square_sem.at[i % PAIR])
        if squares[i][1] < LINE:
            drain(slope_v.at[i % PAIR], slope_sem.at[i % PAIR])
        body(square.at[i % PAIR], slope_v.at[i % PAIR])
        fetch_square(i + PAIR)
        taken[0] += 1

    def with_wide(body):
        i = taken[1]
        drain(wide.at[i % PAIR], wide_sem.at[i % PAIR])
        body(wide.at[i % PAIR])
        fetch_wide(i + PAIR)
        taken[1] += 1

    def loads(l):
        pairs = [(saved[l, "qkv"], qkv_v), (saved[l, "probs"], probs_v), (saved[l, "mid"], mid_v), ((x_in, y_in)[l], x_v)]
        return [local(src, dst, act_sem.at[i]) for i, (src, dst) in enumerate(pairs)]

    def spill(src, dst):
        local(src, dst, spill_sem).start()
        drain(src, spill_sem)

    def load_all(mine, others):
        both = [local(mine, head(bc_v, SEQ), load_sem.at[0]), local(others, bc_v.at[pl.ds(SEQ, FAR), :], load_sem.at[FIVE])]
        for c in both:
            c.start()
        for c in both:
            c.wait()

    spare = (x_v, mid_v)

    def token_load(i, r):
        src = d_y if r == 0 else dy_far.at[pl.ds(SEQ * (r - 1), SEQ), :]
        return local(src, spare[i % PAIR], act_sem.at[i % PAIR])

    def token_block(i, r, dst):
        token_load(i, r).wait()
        rows = pl.ds(SEQ * r, SEQ)
        for half in (0, 1):
            cols = pl.ds(BAND * half, BAND)
            out, slope = gelu(dot(bc_v[rows, :], up_v[:, cols]) + g_vec[pl.ds(31, 1), cols])
            grad = dot(spare[i % PAIR][...], down_v[cols, :], 1, 1) * slope
            sl_v[rows, cols] = out.astype(BF16)
            sl_w[rows, cols] = grad.astype(BF16)
            g_vec[pl.ds(30, 1), cols] = g_vec[pl.ds(30, 1), cols] + column_sum(grad)

        def body(k):
            dst[:, span(k, BAND)] = dot(sl_w[rows, :], up_v[span(k, BAND), :], 1, 1)

        repeat(LINE, body)

    BLOCKS = (PEERS, FIVE, TRIO, 1, SIX, PAIR, LINE, 0)

    def even(r):
        return even_v.at[r // PAIR - 1] if r else d_h

    def tokens():
        weights = [local(fu_mine, up_v, square_sem.at[0]), local(fd_mine, down_v, square_sem.at[1])]
        for c in weights:
            c.start()
        token_load(0, BLOCKS[0]).start()
        load_all(saved[1, "h2"], h_far)
        for c in weights:
            c.wait()
        for i in range(LINE):
            g_vec[pl.ds(31, 1), pl.ds(TILE * i, TILE)] = vec[pl.ds(20 + i, 1), pl.ds(pl.multiple_of(TILE * place, TILE), TILE)]
        for i, r in enumerate(BLOCKS):
            if i + 1 < len(BLOCKS):
                token_load(i + 1, BLOCKS[i + 1]).start()
            if r % PAIR:
                buf = odd_v.at[i % PAIR]
                if i > 1:
                    drain(buf, pair_send.at[i - PAIR])
                token_block(i, r, buf)
                remote(buf, pair_far.at[pl.ds(SEQ * (r // PAIR), SEQ), :], pair_send.at[i], pair_recv.at[r // PAIR], peer(1)).start()
            else:
                token_block(i, r, even(r))
        for i in (0, 1):
            drain(odd_v.at[i], pair_send.at[i + PAIR])
            fetch_square(i)
            fetch_wide(i)
        for c in loads(1):
            c.start()

    def add_rows(dst, src):
        def body(i):
            at = span(i, SHARD)
            dst[at, :] = dst[at, :] + src[at, :]

        repeat(SIX, body)

    def pair_add(r):
        buf = odd_v.at[0]
        block = pair_far.at[pl.ds(SEQ * (r // PAIR), SEQ), :]
        drain(block, pair_recv.at[r // PAIR])
        local(block, buf, load_sem.at[0]).start()
        drain(buf, load_sem.at[0])
        add_rows(even(r), buf)
        if r:
            i = r // PAIR - 1
            remote(even(r), cross_far.at[pl.ds(SEQ * i, SEQ), :], cross_send.at[i], cross_recv.at[i], peer(r)).start()

    def cross_end():
        pair_add(0)
        for i in (PAIR, 0, 1):
            block, buf = cross_far.at[pl.ds(SEQ * i, SEQ), :], odd_v.at[i % PAIR]
            drain(block, cross_recv.at[i])
            local(block, buf, load_sem.at[i % PAIR]).start()
            drain(buf, load_sem.at[i % PAIR])
            add_rows(d_h, buf)
        for c in loads(1):
            c.wait()
        local(d_y, d_out, load_sem.at[0]).start()
        drain(d_out, load_sem.at[0])
        norm_mid(1)

    def norm_mid(l):
        norm_grad_stage(mid_v, d_h, d_out, vec[pl.ds(PLANE * l + SIX, 1), :], g_vec, PLANE * l + SIX, PLANE * l + TRIO, DOWN_ROW + l, d_mid)
        spill(d_mid, d_mid_far.at[l])

    def chain_act():
        for c in loads(0):
            c.start()
        for part in range(LINE):
            with_square(lambda w, sl: act_grad_stage(part, d_out, w, sl, d_pre, g_vec, HEADS))
        spill(d_pre, d_pre_far)

    def chain_mid():
        for part in range(PLANE):
            def body(w, part=part):
                d_h[:, pl.ds(TILE * part, TILE)] = dot(d_pre[...], w[...], 1, 1)

            with_wide(body)
        for c in loads(0):
            c.wait()
        norm_mid(0)

    def chain_attend(l):
        def to_ctx(w, _):
            def body(i):
                d_ctx[:, span(i, BAND)] = dot(d_mid[...], w[span(i, BAND), :], 1, 1).astype(BF16)

            repeat(LINE, body)

        with_square(to_ctx)
        attend_grad_stage(l, qkv_v, probs_v, d_ctx, cos, sin, d_proj, g_vec)
        spill(d_proj, d_proj_far.at[l])

    def chain_norm(l):
        for kind in range(TRIO):
            def to_h(w, _, kind=kind):
                def body(i):
                    part = dot(d_proj[:, pl.ds(DIM * kind, DIM)], w[span(i, BAND), :], 1, 1)
                    d_h[:, span(i, BAND)] = d_h[:, span(i, BAND)] + part if kind else part

                repeat(LINE, body)

            with_square(to_h)
        norm_grad_stage(x_v, d_h, d_mid, vec[pl.ds(PLANE * l + LINE, 1), :], g_vec, PLANE * l + LINE, None, None, d_out)
        spill(d_out, (d_x, d_top)[l])
        if l == 0:
            pack_vectors(g_vec, sum_v)
            sums_plane()

    def end():
        sums_line()
        sums_end()

    g_vec[...] = jnp.zeros_like(g_vec)
    tasks = {"X1": tokens, "X1d": lambda: pair_add(SIX), "X1x": lambda: [pair_add(r) for r in (PAIR, LINE)], "Y1": cross_end,
             "C2": lambda: chain_attend(1), "C3": lambda: chain_norm(1), "C4": chain_act, "C5": chain_mid,
             "C6": lambda: chain_attend(0), "C7": lambda: chain_norm(0), "END": end}
    for u in range(n):
        if u > 1:
            tasks[f"B{u}"] = functools.partial(casts[u][0], bc_in[u])
            tasks[f"R{u}"], tasks[f"L{u}"] = casts[u][1], casts[u][PAIR]
            tasks[f"S{u}"] = functools.partial(send_sl, u)
        tasks[f"P{u}"] = functools.partial(product, u)
        for hop, name in enumerate("ab"):
            tasks[f"H{u}{name}"] = functools.partial(second_hop, u, hop)
        tasks[f"I{u}"] = functools.partial(third_hop, u)
        tasks[f"F{u}"] = functools.partial(finish, u)
    in_order(BACKWARD_ORDER, tasks)

    for i in range(TRIO):
        drain(even_v.at[i], cross_send.at[i])
    drain(sum_got, sum_send.at[0])
    drain(head(sum_line, DOWN_ROW), sum_send.at[1])
    for u in range(n):
        name = PIECES[u][1]
        if u > 1:
            casts[u][LINE]()
            drain(sl_far[u], sl_send.at[u])
        drain(head(acc[u], TRIO * piece_rows(u)), rs_send.at[u])
        if name == "D":
            drain(head(acc[u], TILE), own_sem.at[u])
        else:
            drain(head(acc[u], SHARD), own_sem.at[u])
            drain(head(acc[u], SPREAD), out_send.at[u])
            drain(head(acc[u], SPREAD), out_recv.at[u])


def backward(weights, mine, vec, cos, sin, x_in, y_in, d_y, saved):
    n = len(PIECES)
    shape, hbm, vmem = jax.ShapeDtypeStruct, pl.BlockSpec(memory_space=pltpu.HBM), pl.BlockSpec(memory_space=pltpu.VMEM)
    wide = lambda cols: (SEQ, cols)
    far = PIECES[PAIR:]
    outs = pl.pallas_call(
        backward_kernel,
        out_shape=[shape((PAIR, LINE, SHARD, DIM), F32), shape((PAIR, SHARD, FFN), F32), shape((PAIR, TILE, DIM), F32), shape((PLANE, TILE), F32),
                   shape(wide(DIM), BF16)]
        + [shape((FAR, DIM), BF16) for _ in far] + [shape((FAR, WIDTH[name]), BF16) for _, name in far]
        + [shape(wide(FFN), BF16), shape((LAYERS, SEQ, DIM), BF16), shape((LAYERS, SEQ, QKV_COLS), BF16), shape(wide(DIM), BF16),
           shape((768, DIM), F32), shape((576, DIM), F32)],
        in_specs=[hbm] * TRIO + [vmem] * TRIO + [hbm] * (PEERS + len(KEPT)),
        out_specs=[hbm] * TRIO + [vmem] + [hbm] * (PAIR * len(far) + PEERS),
        scratch_shapes=[pltpu.VMEM((1536, DIM), BF16), pltpu.VMEM((1536, WIDE), BF16), pltpu.VMEM((1536, WIDE), BF16)]
        + [pltpu.VMEM(acc_shape(name), F32) for _, name in PIECES]
        + [pltpu.VMEM((PAIR, TRIO * acc_shape(name)[0] // LINE, acc_shape(name)[1]), F32) for _, name in PIECES]
        + [pltpu.VMEM((BAND, TILE), F32), pltpu.VMEM((SPREAD, TILE), F32), pltpu.VMEM((56, TILE), F32),
           pltpu.VMEM((PAIR, DIM, DIM), BF16), pltpu.VMEM((PAIR, TILE, FFN), BF16), pltpu.VMEM((PAIR, SEQ, DIM), F32)]
        + [pltpu.VMEM(s, BF16) for s in (wide(QKV_COLS), (HEADS, SEQ, SEQ), wide(DIM), wide(DIM), wide(DIM), wide(FFN),
                                         wide(DIM), wide(QKV_COLS), wide(DIM))]
        + [pltpu.VMEM(wide(DIM), F32), pltpu.VMEM((SHARD, DIM), F32), pltpu.VMEM((DIM, WIDE), BF16), pltpu.VMEM((WIDE, DIM), BF16),
           pltpu.VMEM((PAIR, SEQ, DIM), F32), pltpu.VMEM((TRIO, SEQ, DIM), F32)]
        + [DMA((n,)), DMA((n, SIX)), DMA((n,)), DMA((n,)), DMA((n,)), DMA((n,)), DMA((PEERS,)), DMA((n,)), DMA((n, PAIR, LINE)),
           DMA((n,)), DMA((n,)), DMA((n,)), DMA((PAIR,)), DMA((PAIR,)), DMA((PAIR,)), DMA((PAIR,)), DMA((PAIR,)), DMA((LINE,)), DMA,
           DMA((LINE,)), DMA((LINE,)), DMA((TRIO,)), DMA((TRIO,))],
        compiler_params=pltpu.CompilerParams(collective_id=1, has_side_effects=True, vmem_limit_bytes=67043328),
        name="backward",
    )(*weights, vec, cos, sin, x_in, y_in, d_y, *mine, *[saved[key] for key in KEPT])
    return outs[:FIVE]


def pack_small(b_attn, ln_par, b_up, b_down):
    rows = [b_attn.reshape(PAIR, TILE), ln_par.reshape(PAIR, TILE), b_up, jnp.pad(b_down, ((0, 0), (0, HALF_SEQ)))]
    return jnp.stack(rows, axis=1).reshape(PLANE, TILE)


def solution(mesh):
    axis_name = mesh.axis_names[0]
    batch_spec = P(axis_name)
    by_row, by_input = P(None, axis_name), P(None, None, axis_name)
    weight_specs = (by_input, by_input, by_input, by_row, by_row, by_row, by_row)

    def device_step(x, lengths, d_y, w_attn, b_attn, ln_par, w_up, b_up, w_down, b_down):
        cos, sin = rotary_tables()
        keep = (jnp.arange(SEQ)[None] < lengths[0]).astype(F32)
        weights, mine, vec, y, saved = forward(w_attn, w_up, w_down, pack_small(b_attn, ln_par, b_up, b_down), x[0], keep,
                                               cos, sin, d_y[0])
        g_attn, g_up, g_down, g_small, d_x = backward(weights, mine, vec, cos, sin, x[0], y, d_y[0], saved)
        rows = g_small.reshape(PAIR, LINE, TILE)
        return (d_x[None], g_attn, rows[:, 0].reshape(PAIR, LINE, SHARD), rows[:, 1].reshape(PAIR, LINE, SHARD), g_up, rows[:, PAIR],
                g_down, rows[:, TRIO, :SHARD])

    return jax.shard_map(device_step, mesh=mesh,
                         in_specs=(batch_spec, batch_spec, batch_spec) + weight_specs,
                         out_specs=(batch_spec,) + weight_specs,
                         check_vma=False)
```

time: 498 us -> 436 us (0.88)
  Pallas kernels: 481 us -> 420 us
    pallas_call x1, Pallas kernels: 204 us -> 166 us  [forward(): pl.pallas_call(forward_kernel, out_shape=[shape((LAYERS, LINE, DIM, DIM),...]
    pallas_call x1, Pallas kernels: 277 us -> 254 us  [backward(): pl.pallas_call(backward_kernel, out_shape=[shape((PAIR, LINE, SHARD, DIM)...]
where the time goes in v4:
time: 436 us; the launch traced here: 435 us
  Pallas kernels  420 us (96%)
  local copies, waits for them, and re-layouts  12.9 us (3%)
    pallas_call x1, Pallas kernels, backward(): pl.pallas_call(backward_kernel, out_shape=[shape((PAIR, LINE, SHARD, DIM)...  254 us
    pallas_call x1, Pallas kernels, forward(): pl.pallas_call(forward_kernel, out_shape=[shape((LAYERS, LINE, DIM, DIM),...  166 us

profile of v4, /device:TPU:0, one launch (start us, length us, event | category | flops | bytes accessed | tf_op | source)
XLA Modules:
  0.0 435.2 jit_solution(12807159484842998482)
XLA Ops:
  1.3 0.8 stack_reshape.6
  2.0 0.8 stack_reshape.7
  2.8 0.7 pad_bitcast_fusion
  3.5 0.7 pad_maximum_fusion
  4.1 0.6 copy.20
  4.7 0.6 compare_convert_fusion.refs_5_
  5.3 165.6 %forward.1 = (bf16[2,4,1024,1024]{3,2,1,0:T(8,128)(2,1)}, bf16[1024,4096]{1,0:T(8,128)(2,1)}, bf16[4096,1024]{1,0:T(8,128)(2,1)}, bf16[256,128]{1,0:T(8,128)(2,1...) custom-call(bf16[2,4,32,1024]{3,2,1,0:T(8,128)(2,1)} %refs_0_.1, ...), custom_call_target="tpu_custom_call" | custom-call | tf_op jit(solution)/shard_map/forward/pallas_call | solution.py:693
  170.9 254.2 %backward.1 = (f32[2,4,32,1024]{3,2,1,0:T(8,128)}, f32[2,32,4096]{2,1,0:T(8,128)}, f32[2,128,1024]{2,1,0:T(8,128)}, f32[8,128]{1,0:T(8,128)}, bf16[192,1024]{1,0...) custom-call(bf16[2,4,1024,1024]{3,2,1,0:T(8,128)(2,1)} %get-tuple-el, ...), custom_call_target="tpu_custom_call" | custom-call | tf_op jit(solution)/shard_map/backward/pallas_call | solution.py:1132
  425.1 0.0 copy-start.1
  425.1 0.0 copy-start
  425.1 1.4 slice.19
  426.5 1.4 slice_reduce_fusion
  427.8 0.7 reshape_squeeze.7
  428.5 0.7 reshape_squeeze.6
  429.2 1.8 copy.30
  431.0 2.3 copy.31
  433.3 0.0 copy-done.1
  433.3 1.0 copy.32
  434.2 0.0 copy-done
  434.2 1.0 copy.33
Async XLA Ops:
  425.1 8.2 %copy-start.1 = (f32[2,32,4096]{2,1,0:T(8,128)S(1)}, f32[2,32,4096]{2,1,0:T(8,128)}, u32[]{:S(2)}) copy-start(f32[2,32,4096]{2,1,0:T(8,128)} %get-tuple-element.79) | copy-start | bytes 3145732
  425.1 9.1 %copy-start = (f32[2,128,1024]{2,1,0:T(8,128)S(1)}, f32[2,128,1024]{2,1,0:T(8,128)}, u32[]{:S(2)}) copy-start(f32[2,128,1024]{2,1,0:T(8,128)} %get-tuple-element.81) | copy-start | bytes 3145732

commit v5 on v4

--- a/solution.py
+++ b/solution.py
@@ -15,6 +15,9 @@
 SIX = 6
 PEERS = 7
 PLANE = 8
+NINE = 9
+DOZEN = 12
+FOURTEEN = 14
 HEADS = 16
 DOWN_ROW = 24
 SHARD = 32
@@ -25,8 +28,10 @@
 SPREAD = 224
 BAND = 256
 WIDE = 512
+HALF_PLANE = 768
 DIM = 1024
 FAR = 1344
+PLANE_SEQ = 1536
 QKV_COLS = 3072
 FFN = 4096
 
@@ -36,6 +41,7 @@
 NEG_BIG = -1e30
 SQRT_HALF = math.sqrt(0.5)
 DENSITY = 1.0 / math.sqrt(2.0 * math.pi)
+KEEP = True
 SCALE = HEAD_DIM ** -0.5
 F32, BF16 = jnp.float32, jnp.bfloat16
 DMA = pltpu.SemaphoreType.DMA
@@ -93,15 +99,15 @@
 
 
 def row_mean(x):
-    return jnp.mean(x, axis=-1, keepdims=True)
+    return jnp.mean(x, axis=-1, keepdims=KEEP)
 
 
 def row_sum(x):
-    return jnp.sum(x, axis=-1, keepdims=True)
+    return jnp.sum(x, axis=-1, keepdims=KEEP)
 
 
 def column_sum(x):
-    return jnp.sum(x, axis=0, keepdims=True)
+    return jnp.sum(x, axis=0, keepdims=KEEP)
 
 
 def normed(x):
@@ -121,6 +127,20 @@
     if swap:
         row = (row & TRIO) * PLANE + (row >> PAIR)
     return row == lax.broadcasted_iota(jnp.int32, shape, 1) >> FIVE
+
+
+def lane_shift(to):
+    shape = (SHARD, TILE)
+    return lax.broadcasted_iota(jnp.int32, shape, 0) + to == lax.broadcasted_iota(jnp.int32, shape, 1)
+
+
+def pack_parameters(b_attn, ln_par, b_up, b_down, wide, out):
+    for l in range(PAIR):
+        for t, src in enumerate((b_attn, ln_par)):
+            wide[pl.ds(LINE * l + t, 1), :] = sum(dot(src[l, pl.ds(k, 1), :], lane_shift(SHARD * k).astype(BF16)) for k in range(LINE))
+        wide[pl.ds(LINE * l + PAIR, 1), :] = b_up[pl.ds(l, 1), :].astype(F32)
+        wide[pl.ds(LINE * l + TRIO, 1), :] = dot(b_down[pl.ds(l, 1), :], lane_shift(0).astype(BF16))
+    out[...] = wide[pl.ds(0, PLANE), :].astype(BF16)
 
 
 def unpack_vectors(small, vec):
@@ -180,8 +200,8 @@
         vals = head_masks(qkv[:, span(p + HEADS, TILE)])
         out = None
         for h in range(PAIR):
-            scores = jnp.where(keep[...] > 0.5, dot(query, keys[h], 1, 1), NEG_BIG)
-            grown = jnp.exp(scores - jnp.max(scores, axis=-1, keepdims=True))
+            scores = jnp.where(keep, dot(query, keys[h], 1, 1), NEG_BIG)
+            grown = jnp.exp(scores - jnp.max(scores, axis=-1, keepdims=KEEP))
             weight = (grown / row_sum(grown)).astype(BF16)
             probs[PAIR * p + h] = weight
             part = dot(weight, vals[h])
@@ -274,28 +294,27 @@
 
 
 FORWARD_ORDER = (
-    "O0", "O1", "O2", "P1_0", "P0_0", "O3", "O4", "O5", "O6", "Z4_1", "Z0_1m", "P3_0", "O7", "P2_0", "P4_0", "O8",
-    "Z4_2", "Z8_1", "Z0_1p", "Z2_1m", "Z1_1m", "Z2_1p", "Z3_1", "Z4_3", "Z1_1p", "Z8_2", "Z1_2m", "P7_0", "Z7_1",
-    "Z0_2m", "aua", "Z3_2", "Z0_2p", "Z1_2p", "Z8_3", "P8_0", "Z1_3m", "P5_0", "P6_0", "Z3_3", "Z2_2m", "Z2_2p",
-    "Z0_3m", "Z5_1m", "P3_1", "Z2_3m", "Z6_1m", "Z0_3p", "Z6_1p", "P4_1", "Z2_3p", "P4_2", "P3_2", "P3_3", "Q0",
-    "Z1_3p", "Z5_1p", "N0", "P4_3", "Z7_2", "Z5_2m", "Q2", "Z7_3", "Q1", "Z5_2p", "PJ0", "PJ1", "Z6_2m", "Z6_2p",
-    "wua", "Szu", "PJ2", "AT0", "Z6_3m", "Z6_3p", "P8_1", "AT1", "Q4", "Z5_3m", "Szd", "Q3", "Z5_3p", "P8_2", "AT2",
-    "AT3", "P7_1", "RE0", "UP0", "UP1", "P7_2", "Q6", "P8_3", "Q5", "zd_1", "P7_3", "UP2", "UP3", "DN0", "DN1",
-    "Bdy", "Q8", "Q7", "DN2", "zu_1", "DN3", "pj0", "pj1", "pj2", "at0", "Rdy", "at1", "at2", "at3", "re0", "Bh2",
-    "zd_2", "zu_2", "Rh2", "Ldy", "Lh2", "zd_3", "zu_3", "G",
+    "O0", "O1", "O2", "O3", "Z11", "O4", "O5", "Z12", "P00", "Z21", "P30", "Z01", "P20", "P10", "Z22", "Z31", "P40",
+    "Z23", "Z13", "Y01", "P50", "Z41", "O6", "Z02", "P21", "O7", "Y31", "Y02", "P11", "Y41", "Z42", "P22", "P12",
+    "P13", "P60", "O8", "as", "Z03", "Y03", "Z32", "P23", "Y42", "Z61", "Z71", "Z51", "Y32", "Z33", "Q0", "Y33",
+    "Q1", "Z81", "Z43", "Y61", "Q2", "Y51", "N0", "Z52", "Z62", "J0", "Y62", "Z82", "Y52", "J1", "Z72", "Z53", "J2",
+    "Y43", "A0", "A1", "Z63", "A2", "Sd", "Q3", "A3", "Y63", "Y53", "E0", "Q4", "Z83", "ws", "Z73", "Q6", "Su",
+    "U0", "P80", "d0", "Q5", "P70", "P81", "P82", "U1", "P71", "U2", "P83", "U3", "P72", "u0", "P73", "D0", "D1",
+    "D2", "By", "D3", "d1", "Q7", "Q8", "u1", "j0", "j1", "j2", "Ry", "a0", "a1", "d2", "a2", "a3", "u2", "e0",
+    "Bh", "W", "T1", "Ly", "T0", "Rh", "T4", "T2", "T3", "Lh", "T5", "T7", "T6", "G",
 )
 BACKWARD_ORDER = (
-    "B2", "X1", "X1d", "P0", "X1x", "R2", "P1", "B3", "Y1", "S2", "C2", "R3", "L2", "C3", "S3", "L3", "H0a", "C4",
-    "P2", "S4", "H1a", "B4", "C5", "P3", "R4", "S5", "H3a", "H2a", "L4", "P4", "B5", "I0", "S6", "H0b", "H4a",
-    "H1b", "R5", "C6", "B6", "I4", "I3", "L5", "B7", "I1", "H4b", "P5", "H3b", "H5a", "R6", "R7", "I2", "S7", "H5b",
-    "L7", "L6", "I5", "P6", "P7", "H6a", "H2b", "H6b", "H7a", "F5", "F3", "F2", "I6", "H7b", "F6", "I7", "F4", "F0",
-    "C7", "F7", "F1", "END",
+    "X", "P0", "P1", "B2", "B3", "Y", "R2", "S2", "C2", "L2", "S3", "R3", "C3", "H0a", "C4", "S4", "B4", "H0b",
+    "P2", "H1a", "L3", "P3", "R4", "H2a", "H2b", "B5", "L4", "H3a", "P4", "S5", "I2", "C5", "I1", "H3b", "R5", "C6",
+    "L5", "I0", "H4a", "H1b", "H4b", "B7", "B6", "P5", "S6", "R6", "I3", "C7", "S7", "H5a", "L6", "F0", "I4", "H5b",
+    "R7", "P6", "F2", "F1", "I5", "H6a", "H6b", "L7", "P7", "F5", "F3", "F4", "I6", "H7a", "H7b", "F6", "I7", "F7",
+    "END",
 )
 
 
 LAYERS = PAIR
 UNITS = [(0, SIX)] + [(0, piece) for piece in range(SIX)] + [(1, 0), (1, 1)]
-ROUTES = [("b", 0, 1)] + [("b", 0, 1), ("b", 1, 0), ("a", 0, 1), ("a", 1, 0)] * LAYERS
+ROUTES = [("b", 0, 1)] + [(kind, p, 1 - p) for kind in "abba" for p in range(PAIR)]
 
 
 SAVED = ("h1", "qkv", "probs", "ctx", "mid", "h2", "act", "slope")
@@ -314,14 +333,16 @@
     def block(r, half):
         return far.at[pl.ds(SEQ * (r - 1) + HALF_SEQ * half, HALF_SEQ), :]
 
+    def whole(r):
+        return far.at[pl.ds(SEQ * (r - 1), SEQ), :]
+
     def push(r, half):
-        remote(block(r, half), block(r + 1, half), push_send, push_recv, peer(1)).start()
+        remote(block(r, half), block(r + 1, half), push_send, push_recv.at[r // PAIR], peer(1)).start()
 
     def start(src):
-        for r in (PAIR, LINE):
-            for half in (0, 1):
-                remote(src.at[pl.ds(HALF_SEQ * half, HALF_SEQ), :], block(r, half), send, recv.at[r - PAIR + half], peer(r)).start()
-        remote(src, head(far, SEQ), push_send, push_recv, peer(1)).start()
+        for r, half in ((PAIR, 0), (LINE, 1), (PAIR, 1), (LINE, 0)):
+            remote(src.at[pl.ds(HALF_SEQ * half, HALF_SEQ), :], block(r, half), send, recv.at[r - PAIR + half], peer(r)).start()
+        remote(src, whole(1), push_send, push_recv.at[0], peer(1)).start()
 
     def relay():
         for r, half, onward in ((PAIR, 0, LINE), (LINE, 1, PAIR), (PAIR, 1, None), (LINE, 0, None)):
@@ -335,12 +356,12 @@
             drain(block(SIX, half), recv.at[LINE + half])
             push(SIX, half)
 
-    def arrived():
-        drain(head(far, 768), push_recv)
+    def arrived(r):
+        drain(whole(r), push_recv.at[r // PAIR])
 
     def sent():
         drain(head(far, 576), send)
-        drain(head(far, 768), push_send)
+        drain(head(far, HALF_PLANE), push_send)
 
     return start, relay, last, arrived, sent
 
@@ -360,19 +381,45 @@
 
 
 def in_order(order, tasks):
-    assert sorted(order) == sorted(tasks)
+    assert sorted(order) == sorted(tasks), set(order) ^ set(tasks)
     for name in order:
         tasks[name]()
 
 
+def token_block(h, d_y, up, down, bias, row, rows, act, d_pre, dst):
+    for half in (0, 1):
+        cols = pl.ds(BAND * half, BAND)
+        out, slope = gelu(dot(h[...], up[:, cols]) + bias[pl.ds(0, 1), cols])
+        grad = dot(d_y[...], down[cols, :], 1, 1) * slope
+        act[rows, cols] = out.astype(BF16)
+        d_pre[rows, cols] = grad.astype(BF16)
+        bias[pl.ds(1, 1), cols] = bias[pl.ds(1, 1), cols] + column_sum(grad)
+
+    def body(k):
+        dst[:, span(k, BAND)] = dot(d_pre[rows, :], up[span(k, BAND), :], 1, 1)
+
+    repeat(LINE, body)
+
+
+def add_rows(dst, src):
+    def body(i):
+        at = span(i, SHARD)
+        dst[at, :] = dst[at, :] + src[at, :]
+
+    repeat(SIX, body)
+
+
 def forward_kernel(*refs):
-    (wa, wu, wd, sm, x, keep, cos, sin, d_y), refs = refs[:9], refs[9:]
-    (fa, fu, fd, fs, fu_mine, fd_mine, h_far, dy_far, out_vec, out_mid), refs = refs[:10], refs[10:]
+    (wa, wu, wd, b_attn, ln_par, b_up, b_down, x, length, cos, sin, d_y), refs = refs[:DOZEN], refs[DOZEN:]
+    (fa, fu, fd, fs, fu_mine, fd_mine, out_h, out_dy, out_act, out_pre, out_part, out_bias, out_vec, out_mid), refs = (
+        refs[:FOURTEEN], refs[FOURTEEN:])
     saved, refs = dict(zip(KEPT, refs)), refs[len(KEPT):]
     (va, vu, vd, vs), refs = refs[:LINE], refs[LINE:]
     acts, refs = dict(zip(KEPT, refs)), refs[len(KEPT):]
-    (y, vec, small_in, small, w_even, w_odd, load_sem, save_sem, own_sem, xy_sem, z_sem, push_send, push_recv,
-     recv_sem, line_send, line_recv, spread_send, spread_recv, mine_sem, bc_send, bc_recv, bp_send, bp_recv) = refs
+    (y, vec, small_in, small, w_even, w_odd, dy_v, h_far, dy_far, up_v, down_v, act_v, pre_v, bias_v, part_v, odd_v, pair_v,
+     load_sem, save_sem, own_sem, xy_sem, z_sem, push_send, push_recv, recv_sem, line_send, line_recv, spread_send,
+     spread_recv, mine_sem, bc_send, bc_recv, bp_send, bp_recv, pair_send, pair_recv, late_sem) = refs
+    keep = lax.broadcasted_iota(jnp.int32, (1, SEQ), 1) < length[0]
     me = lax.axis_index("fsdp")
     core, xc, yc, zc = me % PAIR, (me // PAIR) % PAIR, (me // LINE) % PAIR, me // PLANE
     partner = me + 1 - PAIR * core
@@ -423,9 +470,11 @@
         pl.semaphore_signal(barrier, inc=1, device_id=(down,), device_id_type=MESH)
 
     loads = [local(src, dst, load_sem.at[i])
-             for i, (src, dst) in enumerate(((wa, va), (wu, vu), (wd, vd), (sm, vs)))]
+             for i, (src, dst) in enumerate(((wa, va), (wu, vu), (wd, vd), (d_y, dy_v)))]
     for load in loads:
         load.start()
+    pack_parameters(b_attn, ln_par, b_up, b_down, small, vs)
+    bias_v[...] = jnp.zeros_like(bias_v)
     for load in loads:
         load.wait()
     pl.semaphore_wait(barrier, PEERS + has_up.astype(jnp.int32) + has_down.astype(jnp.int32))
@@ -518,13 +567,13 @@
         rows = pl.ds(pl.multiple_of(SHARD * me, SHARD), SHARD)
         for r in (SIX, PAIR, LINE, PEERS, TRIO, FIVE, 1):
             for src, dst in mine_cols(peer(r) % PLANE):
-                remote(vu.at[1, :, pl.ds(src, TILE)], fu_mine.at[rows, pl.ds(dst, TILE)], spread_send, spread_recv, peer(r)).start()
+                remote(vu.at[1, :, pl.ds(src, TILE)], fu_mine.at[rows, pl.ds(dst, TILE)], spread_send.at[0], spread_recv.at[0], peer(r)).start()
         for src, dst in mine_cols(place):
             local(vu.at[1, :, pl.ds(src, TILE)], fu_mine.at[rows, pl.ds(dst, TILE)], mine_sem.at[1]).start()
         local(vd.at[1], fd_mine.at[pl.ds(pl.multiple_of(TILE * zc, TILE), TILE), :], mine_sem.at[0]).start()
 
     def spread_done():
-        drain(head(fu_mine, SPREAD), spread_recv)
+        drain(head(fu_mine, SPREAD), spread_recv.at[0])
         drain(head(fu_mine, SHARD), mine_sem.at[1])
 
     def line_block(k, zs):
@@ -622,38 +671,68 @@
         residual_stage(acts[0, "act"], buf, acts[0, "mid"], DOWN_ROW, vec, y, n, 1)
         if n == TRIO:
             local(y, out_mid, save_sem.at[1, PLANE]).start()
-            norm_stage(y, vec, 12, acts[1, "h1"])
+            norm_stage(y, vec, DOZEN, acts[1, "h1"])
             save(1, "h1")
 
+    def load_mine():
+        drain(head(fd_mine, TILE), mine_sem.at[0])
+        pairs = [local(fu_mine, up_v, late_sem.at[0]), local(fd_mine, down_v, late_sem.at[1])]
+        for c in pairs:
+            c.start()
+        for c in pairs:
+            c.wait()
+        for i in range(LINE):
+            bias_v[pl.ds(0, 1), pl.ds(TILE * i, TILE)] = vec[pl.ds(20 + i, 1), pl.ds(pl.multiple_of(TILE * place, TILE), TILE)]
+
+    def tokens(r):
+        rows = pl.ds(SEQ * r, SEQ)
+        there = pl.ds(SEQ * (r - 1), SEQ)
+        if r % PAIR:
+            for cast in casts:
+                cast[TRIO](r)
+        h, grad = (h_far.at[there, :], dy_far.at[there, :]) if r else (acts[1, "h2"], dy_v)
+        dst = (odd_v if r % PAIR else part_v).at[r // PAIR]
+        token_block(h, grad, up_v, down_v, bias_v, 0, rows, act_v, pre_v, dst)
+        if r % PAIR:
+            remote(dst, pair_v.at[r // PAIR], pair_send.at[r // PAIR], pair_recv.at[r // PAIR], partner).start()
+
+    LATE = ((h_far, out_h), (dy_far, out_dy), (act_v, out_act), (pre_v, out_pre), (bias_v, out_bias))
+
     def gathered():
-        for cast in casts:
-            cast[TRIO]()
-
-    tasks = {"N0": begin, "RE0": lambda: settle(0, w_even), "re0": lambda: settle(1, w_odd), "aua": spread, "wua": spread_done,
-             "Szd": lambda: line_start(0), "Szu": lambda: line_start(1), "Bdy": lambda: casts[0][0](d_y),
-             "Bh2": lambda: casts[1][0](acts[1, "h2"]), "Rdy": casts[0][1], "Rh2": casts[1][1], "Ldy": casts[0][PAIR],
-             "Lh2": casts[1][PAIR], "G": gathered}
+        for i, (src, dst) in enumerate(LATE):
+            local(src, dst, late_sem.at[i]).start()
+        for k in range(LINE):
+            drain(pair_v.at[k], pair_recv.at[k])
+            add_rows(part_v.at[k], pair_v.at[k])
+            local(part_v.at[k], out_part.at[pl.ds(SEQ * k, SEQ), :], late_sem.at[FIVE + k]).start()
+
+    tasks = {"N0": begin, "E0": lambda: settle(0, w_even), "e0": lambda: settle(1, w_odd), "as": spread, "ws": spread_done,
+             "Sd": lambda: line_start(0), "Su": lambda: line_start(1), "By": lambda: casts[0][0](dy_v),
+             "Bh": lambda: casts[1][0](acts[1, "h2"]), "Ry": casts[0][1], "Rh": casts[1][1], "Ly": casts[0][PAIR],
+             "Lh": casts[1][PAIR], "W": load_mine, "G": gathered}
+    for r in range(PLANE):
+        tasks[f"T{r}"] = functools.partial(tokens, r)
     for i in range(TRIO):
-        tasks[f"PJ{i}"] = functools.partial(project, 0, w_even, i)
-        tasks[f"pj{i}"] = functools.partial(project, 1, w_odd, i)
-        for k, name in enumerate(("zd", "zu")):
-            tasks[f"{name}_{i + 1}"] = functools.partial(line_hop, k, i + 1)
+        tasks[f"J{i}"] = functools.partial(project, 0, w_even, i)
+        tasks[f"j{i}"] = functools.partial(project, 1, w_odd, i)
+        for k, name in enumerate("du"):
+            tasks[f"{name}{i}"] = functools.partial(line_hop, k, i + 1)
     for i in range(LINE):
-        tasks[f"AT{i}"] = functools.partial(attend, 0, i)
-        tasks[f"at{i}"] = functools.partial(attend, 1, i)
-        tasks[f"UP{i}"] = functools.partial(grow, w_odd, i)
-        tasks[f"DN{i}"] = functools.partial(shrink, w_even, i)
+        tasks[f"A{i}"] = functools.partial(attend, 0, i)
+        tasks[f"a{i}"] = functools.partial(attend, 1, i)
+        tasks[f"U{i}"] = functools.partial(grow, w_odd, i)
+        tasks[f"D{i}"] = functools.partial(shrink, w_even, i)
     for u in range(len(UNITS)):
         tasks[f"O{u}"] = functools.partial(stage0, u)
         tasks[f"Q{u}"] = functools.partial(q_arrivals, u)
         for dz in (1, PAIR, TRIO):
             if order(u)[0] == "a":
-                tasks[f"Z{u}_{dz}"] = functools.partial(z_arrival, u, dz, (-1, 1), (0,), True)
+                tasks[f"Z{u}{dz}"] = functools.partial(z_arrival, u, dz, (-1, 1), (0,), True)
             else:
-                tasks[f"Z{u}_{dz}m"] = functools.partial(z_arrival, u, dz, (-1,), (0, 1), False)
-                tasks[f"Z{u}_{dz}p"] = functools.partial(z_arrival, u, dz, (1,), (0, 1), False)
+                tasks[f"Z{u}{dz}"] = functools.partial(z_arrival, u, dz, (-1,), (0, 1), False)
+                tasks[f"Y{u}{dz}"] = functools.partial(z_arrival, u, dz, (1,), (0, 1), False)
         for hop in range(LINE if order(u)[0] == "a" else 1):
-            tasks[f"P{u}_{hop}"] = functools.partial(p_arrival, u, hop)
+            tasks[f"P{u}{hop}"] = functools.partial(p_arrival, u, hop)
     in_order(FORWARD_ORDER, tasks)
 
     ends = jnp.logical_or(zc == 0, zc == TRIO)
@@ -664,7 +743,7 @@
 
     for u in range(len(UNITS)):
         straight = order(u)[0] == "a"
-        drain(rows_of(u, 12 if straight else 9), xy_sem.at[u])
+        drain(rows_of(u, DOZEN if straight else NINE), xy_sem.at[u])
         for case, units in ((ends, 1), (middle, FIVE)):
             @pl.when(case)
             def _(u=u, units=units, straight=straight):
@@ -674,10 +753,14 @@
             @pl.when(case)
             def _(k=k, units=units):
                 drain(head(fd, TILE * units), line_send.at[k])
-    drain(head(fu_mine, SPREAD), spread_send)
-    drain(head(fd_mine, TILE), mine_sem.at[0])
+    drain(head(fu_mine, SPREAD), spread_send.at[0])
     for cast in casts:
         cast[LINE]()
+    for i, (src, _) in enumerate(LATE):
+        drain(src, late_sem.at[i])
+    for k in range(LINE):
+        drain(part_v.at[k], late_sem.at[FIVE + k])
+        drain(odd_v.at[k], pair_send.at[k])
     halves = (fa.at[0], head(fu, WIDE), head(fd, 2048), head(fs, TILE))
     for i, half in enumerate(halves):
         drain(half, push_send.at[i])
@@ -687,29 +770,32 @@
     drain(out_mid, save_sem.at[1, PLANE])
 
 
-def forward(w_attn, w_up, w_down, small, x, keep, cos, sin, d_y):
+def forward(w_attn, w_up, w_down, b_attn, ln_par, b_up, b_down, x, lengths, cos, sin, d_y):
     shape, hbm, vmem = jax.ShapeDtypeStruct, pl.BlockSpec(memory_space=pltpu.HBM), pl.BlockSpec(memory_space=pltpu.VMEM)
     kept = [shape(SAVED_SHAPES[name], saved_type(name)) for _, name in KEPT]
+    tokens, far, hidden = shape((SEQ, DIM), BF16), shape((FAR, DIM), BF16), shape((PLANE_SEQ, WIDE), BF16)
+    up, down, vectors, bias = shape((DIM, WIDE), BF16), shape((WIDE, DIM), BF16), shape((SHARD, DIM), F32), shape((PLANE, WIDE), F32)
+    small, blocks = shape((BAND, TILE), BF16), shape((LINE, SEQ, DIM), F32)
+    mine = shape((PLANE, TILE), BF16)
+    scratch = [w_attn, w_up, w_down, mine] + kept + [tokens, vectors, small, shape((BAND, TILE), F32)]
+    scratch += [shape((FFN, DIM), BF16)] * PAIR + [tokens, far, far, up, down, hidden, hidden, bias, blocks, blocks, blocks]
+    count = len(UNITS)
+    sems = [(LINE,), (PAIR, NINE), (count,), (count,), (count,), (LINE,), (count,), (count, NINE), (PAIR,), (PAIR, LINE), (1,), (1,), (PAIR,), (PAIR,), (PAIR, SIX),
+            (PAIR,), (PAIR, LINE), (LINE,), (LINE,), (NINE,)]
     outs = pl.pallas_call(
         forward_kernel,
-        out_shape=[shape((LAYERS, LINE, DIM, DIM), BF16), shape((DIM, FFN), BF16), shape((FFN, DIM), BF16),
-                   shape((BAND, TILE), BF16), shape((DIM, WIDE), BF16), shape((WIDE, DIM), BF16), shape((FAR, DIM), BF16),
-                   shape((FAR, DIM), BF16), shape((SHARD, DIM), F32), shape((SEQ, DIM), BF16)] + kept,
-        in_specs=[hbm] * LINE + [vmem] * LINE + [hbm],
-        out_specs=[hbm] * (10 + len(kept)),
-        scratch_shapes=[pltpu.VMEM(w.shape, BF16) for w in (w_attn, w_up, w_down, small)]
-        + [pltpu.VMEM(k.shape, k.dtype) for k in kept]
-        + [pltpu.VMEM((SEQ, DIM), BF16), pltpu.VMEM((SHARD, DIM), F32), pltpu.VMEM((BAND, TILE), BF16),
-           pltpu.VMEM((BAND, TILE), F32), pltpu.VMEM((FFN, DIM), BF16), pltpu.VMEM((FFN, DIM), BF16),
-           DMA((LINE,)), DMA((PAIR, 9)), DMA((len(UNITS),)), DMA((len(UNITS),)), DMA((len(UNITS),)), DMA((LINE,)), DMA((len(UNITS),)),
-           DMA((len(UNITS), 9)), DMA((PAIR,)), DMA((PAIR, LINE)), DMA, DMA, DMA((PAIR,)), DMA((PAIR,)), DMA((PAIR, SIX)), DMA((PAIR,)), DMA((PAIR,))],
-        compiler_params=pltpu.CompilerParams(collective_id=0, has_side_effects=True, vmem_limit_bytes=60 * DIM * DIM),
+        out_shape=[shape((LAYERS, LINE, DIM, DIM), BF16), shape((DIM, FFN), BF16), shape((FFN, DIM), BF16), small, up, down,
+                   far, far, hidden, hidden, shape((HALF_PLANE, DIM), F32), bias, vectors, tokens] + kept,
+        in_specs=[hbm] * TRIO + [vmem] * FIVE + [pl.BlockSpec(memory_space=pltpu.SMEM)] + [vmem] * PAIR + [hbm],
+        out_specs=[hbm] * (FOURTEEN + len(kept)),
+        scratch_shapes=[pltpu.VMEM(s.shape, s.dtype) for s in scratch] + [DMA(s) for s in sems],
+        compiler_params=pltpu.CompilerParams(collective_id=0, has_side_effects=True, vmem_limit_bytes=67043328),
         name="forward",
-    )(w_attn, w_up, w_down, small, x, keep, cos, sin, d_y)
-    return outs[:TRIO], outs[LINE:PLANE], outs[PLANE], outs[9], dict(zip(KEPT, outs[10:]))
-
-
-PIECES = [(1, name) for name in "UDOQ"] + [(0, name) for name in "DUOQ"]
+    )(w_attn, w_up, w_down, b_attn, ln_par, b_up, b_down, x, lengths, cos, sin, d_y)
+    return outs[:TRIO], outs[SIX:DOZEN], outs[DOZEN], outs[13], dict(zip(KEPT, outs[FOURTEEN:]))
+
+
+PIECES = [(1, name) for name in "UDOQ"] + [(0, name) for name in "DUQO"]
 WIDTH = {"D": WIDE, "U": WIDE, "O": TILE, "Q": 384}
 ROWS = SEQ
 
@@ -720,20 +806,22 @@
 
 def backward_kernel(*refs):
     n = len(PIECES)
-    (fa, fu, fd, vec, cos, sin, x_in, y_in, d_y, fu_mine, fd_mine, h_far, dy_far), refs = refs[:13], refs[13:]
+    (fa, fu, fd, vec, cos, sin, x_in, y_in, d_y, h_far, dy_far, act_mine, pre_mine, part_in, bias_in), refs = refs[:15], refs[15:]
     saved, refs = dict(zip(KEPT, refs)), refs[len(KEPT):]
     (g_attn, g_up, g_down, g_small, d_x), refs = refs[:FIVE], refs[FIVE:]
     bc_far, sl_far, refs = (None, None) + refs[:n - PAIR], (None, None) + refs[n - PAIR:PAIR * n - LINE], refs[PAIR * n - LINE:]
-    (d_pre_far, d_mid_far, d_proj_far, d_top, pair_far, cross_far), refs = refs[:SIX], refs[SIX:]
-    (bc_v, sl_v, sl_w), refs = refs[:TRIO], refs[TRIO:]
+    (d_pre_far, d_mid_far, d_proj_far, d_top, cross_far), refs = refs[:FIVE], refs[FIVE:]
+    (bc_v, sl_v), refs = refs[:PAIR], refs[PAIR:]
     acc, got, refs = refs[:n], refs[n:PAIR * n], refs[PAIR * n:]
     (sum_v, sum_got, sum_line, square, wide, slope_v, qkv_v, probs_v, mid_v, x_v, d_out, d_pre, d_mid, d_proj, d_ctx, d_h,
-     g_vec, up_v, down_v, odd_v, even_v), refs = refs[:21], refs[21:]
+     g_vec, odd_v), refs = refs[:18], refs[18:]
     (bc_send, bc_recv, push_send, push_recv, sl_send, sl_recv, load_sem, rs_send, rs_recv, out_send, out_recv, own_sem,
-     sum_send, sum_recv, square_sem, slope_sem, wide_sem, act_sem, spill_sem, pair_send, pair_recv, cross_send,
-     cross_recv) = refs
-    bc_in = [None, None, saved[1, "ctx"], saved[1, "h1"], d_top, saved[0, "h2"], saved[0, "ctx"], saved[0, "h1"]]
-    sl_in = [None, None, d_mid_far.at[1], d_proj_far.at[1], saved[0, "act"], d_pre_far, d_mid_far.at[0], d_proj_far.at[0]]
+     sum_send, sum_recv, square_sem, slope_sem, wide_sem, act_sem, spill_sem, cross_send, cross_recv, early_sem) = refs
+    whole = {(1, "O"): saved[1, "ctx"], (1, "Q"): saved[1, "h1"], (0, "D"): d_top, (0, "U"): saved[0, "h2"],
+             (0, "O"): saved[0, "ctx"], (0, "Q"): saved[0, "h1"]}
+    sliced = {(1, "O"): d_mid_far.at[1], (1, "Q"): d_proj_far.at[1], (0, "D"): saved[0, "act"], (0, "U"): d_pre_far,
+              (0, "O"): d_mid_far.at[0], (0, "Q"): d_proj_far.at[0]}
+    bc_in, sl_in = [[where.get(piece) for piece in PIECES] for where in (whole, sliced)]
 
     me = lax.axis_index("fsdp")
     core, xc, yc, zc = me % PAIR, (me // PAIR) % PAIR, (me // LINE) % PAIR, me // PLANE
@@ -777,7 +865,8 @@
         for c in own:
             c.start()
         drain(sl_far[u], sl_recv.at[u])
-        casts[u][TRIO]()
+        for r in (1, TRIO, FIVE, PEERS):
+            casts[u][TRIO](r)
         rest = [local(bc_far[u], bc_v.at[pl.ds(SEQ, FAR), :], load_sem.at[FIVE]),
                 local(sl_far[u], sl_v.at[pl.ds(SEQ, FAR), pl.ds(0, WIDTH[name])], load_sem.at[SIX])]
         for c in rest:
@@ -813,18 +902,19 @@
     def product(u):
         if u > 1:
             collect(u)
-        if u == 1:
-            load_all(d_y, dy_far)
+        elif u == 0:
+            load_all(saved[1, "h2"], h_far, pre_mine)
+        else:
+            load_all(d_y, dy_far, act_mine)
         name = PIECES[u][1]
         pr, width = piece_rows(u), WIDTH[name]
-        cols_v = sl_w if u == 0 else sl_v
 
         def body(d, carry):
             at = pl.ds(pl.multiple_of(pr * d, pr), pr)
             if name == "D":
-                lhs, rhs = cols_v[:, at], bc_v[...]
+                lhs, rhs = sl_v[:, at], bc_v[...]
             else:
-                lhs, rhs = bc_v[:, at], cols_v[:, pl.ds(0, width)]
+                lhs, rhs = bc_v[:, at], sl_v[:, pl.ds(0, width)]
             acc[u][at, :] = lax.dot_general(lhs, rhs, (((0,), (0,)), ((), ())), preferred_element_type=jnp.float32)
             return carry
 
@@ -893,7 +983,7 @@
         sum_line[pl.ds(0, SHARD), :] = total
         for i in range(LINE):
             at = pl.ds(PLANE * i + SIX, 1)
-            sum_line[at, :] = sum_line[at, :] + g_vec[pl.ds(30, 1), pl.ds(TILE * i, TILE)]
+            sum_line[at, :] = sum_line[at, :] + bias_in[pl.ds(1, 1), pl.ds(TILE * i, TILE)]
         for k in range(1, LINE):
             remote(sum_line.at[pl.ds(pl.multiple_of(PLANE * lax.rem(zc + k, LINE), PLANE), PLANE), :],
                    sum_line.at[pl.ds(SHARD + PLANE * (k - 1), PLANE), :], sum_send.at[1], sum_recv.at[1], line(k)).start()
@@ -941,101 +1031,46 @@
         return [local(src, dst, act_sem.at[i]) for i, (src, dst) in enumerate(pairs)]
 
     def spill(src, dst):
-        local(src, dst, spill_sem).start()
-        drain(src, spill_sem)
-
-    def load_all(mine, others):
-        both = [local(mine, head(bc_v, SEQ), load_sem.at[0]), local(others, bc_v.at[pl.ds(SEQ, FAR), :], load_sem.at[FIVE])]
-        for c in both:
+        local(src, dst, spill_sem.at[0]).start()
+        drain(src, spill_sem.at[0])
+
+    def load_all(mine, others, columns):
+        parts = [local(mine, head(bc_v, SEQ), load_sem.at[0]), local(others, bc_v.at[pl.ds(SEQ, FAR), :], load_sem.at[FIVE]),
+                 local(columns, sl_v, load_sem.at[SIX])]
+        for c in parts:
             c.start()
-        for c in both:
+        for c in parts:
             c.wait()
 
-    spare = (x_v, mid_v)
-
-    def token_load(i, r):
-        src = d_y if r == 0 else dy_far.at[pl.ds(SEQ * (r - 1), SEQ), :]
-        return local(src, spare[i % PAIR], act_sem.at[i % PAIR])
-
-    def token_block(i, r, dst):
-        token_load(i, r).wait()
-        rows = pl.ds(SEQ * r, SEQ)
-        for half in (0, 1):
-            cols = pl.ds(BAND * half, BAND)
-            out, slope = gelu(dot(bc_v[rows, :], up_v[:, cols]) + g_vec[pl.ds(31, 1), cols])
-            grad = dot(spare[i % PAIR][...], down_v[cols, :], 1, 1) * slope
-            sl_v[rows, cols] = out.astype(BF16)
-            sl_w[rows, cols] = grad.astype(BF16)
-            g_vec[pl.ds(30, 1), cols] = g_vec[pl.ds(30, 1), cols] + column_sum(grad)
-
-        def body(k):
-            dst[:, span(k, BAND)] = dot(sl_w[rows, :], up_v[span(k, BAND), :], 1, 1)
-
-        repeat(LINE, body)
-
-    BLOCKS = (PEERS, FIVE, TRIO, 1, SIX, PAIR, LINE, 0)
-
-    def even(r):
-        return even_v.at[r // PAIR - 1] if r else d_h
-
-    def tokens():
-        weights = [local(fu_mine, up_v, square_sem.at[0]), local(fd_mine, down_v, square_sem.at[1])]
-        for c in weights:
-            c.start()
-        token_load(0, BLOCKS[0]).start()
-        load_all(saved[1, "h2"], h_far)
-        for c in weights:
-            c.wait()
-        for i in range(LINE):
-            g_vec[pl.ds(31, 1), pl.ds(TILE * i, TILE)] = vec[pl.ds(20 + i, 1), pl.ds(pl.multiple_of(TILE * place, TILE), TILE)]
-        for i, r in enumerate(BLOCKS):
-            if i + 1 < len(BLOCKS):
-                token_load(i + 1, BLOCKS[i + 1]).start()
-            if r % PAIR:
-                buf = odd_v.at[i % PAIR]
-                if i > 1:
-                    drain(buf, pair_send.at[i - PAIR])
-                token_block(i, r, buf)
-                remote(buf, pair_far.at[pl.ds(SEQ * (r // PAIR), SEQ), :], pair_send.at[i], pair_recv.at[r // PAIR], peer(1)).start()
-            else:
-                token_block(i, r, even(r))
+    def cross_start():
+        for r in (SIX, PAIR, LINE):
+            i = r // PAIR - 1
+            remote(part_in.at[pl.ds(HALF_SEQ * r, SEQ), :], cross_far.at[pl.ds(SEQ * i, SEQ), :], cross_send.at[i], cross_recv.at[i],
+                   peer(r)).start()
         for i in (0, 1):
-            drain(odd_v.at[i], pair_send.at[i + PAIR])
             fetch_square(i)
             fetch_wide(i)
         for c in loads(1):
             c.start()
-
-    def add_rows(dst, src):
-        def body(i):
-            at = span(i, SHARD)
-            dst[at, :] = dst[at, :] + src[at, :]
-
-        repeat(SIX, body)
-
-    def pair_add(r):
-        buf = odd_v.at[0]
-        block = pair_far.at[pl.ds(SEQ * (r // PAIR), SEQ), :]
-        drain(block, pair_recv.at[r // PAIR])
-        local(block, buf, load_sem.at[0]).start()
-        drain(buf, load_sem.at[0])
-        add_rows(even(r), buf)
-        if r:
-            i = r // PAIR - 1
-            remote(even(r), cross_far.at[pl.ds(SEQ * i, SEQ), :], cross_send.at[i], cross_recv.at[i], peer(r)).start()
+        local(head(part_in, SEQ), d_h, early_sem.at[0]).start()
+        local(d_y, d_out, early_sem.at[1]).start()
 
     def cross_end():
-        pair_add(0)
+        drain(d_h, early_sem.at[0])
+        drain(d_out, early_sem.at[1])
         for i in (PAIR, 0, 1):
-            block, buf = cross_far.at[pl.ds(SEQ * i, SEQ), :], odd_v.at[i % PAIR]
+            block = cross_far.at[pl.ds(SEQ * i, SEQ), :]
             drain(block, cross_recv.at[i])
-            local(block, buf, load_sem.at[i % PAIR]).start()
-            drain(buf, load_sem.at[i % PAIR])
-            add_rows(d_h, buf)
+            local(block, odd_v, load_sem.at[0]).start()
+            drain(odd_v, load_sem.at[0])
+
+            def body(k):
+                at = span(k, SHARD)
+                d_h[at, :] = d_h[at, :] + odd_v[at, :]
+
+            repeat(SIX, body)
         for c in loads(1):
             c.wait()
-        local(d_y, d_out, load_sem.at[0]).start()
-        drain(d_out, load_sem.at[0])
         norm_mid(1)
 
     def norm_mid(l):
@@ -1091,7 +1126,7 @@
         sums_end()
 
     g_vec[...] = jnp.zeros_like(g_vec)
-    tasks = {"X1": tokens, "X1d": lambda: pair_add(SIX), "X1x": lambda: [pair_add(r) for r in (PAIR, LINE)], "Y1": cross_end,
+    tasks = {"X": cross_start, "Y": cross_end,
              "C2": lambda: chain_attend(1), "C3": lambda: chain_norm(1), "C4": chain_act, "C5": chain_mid,
              "C6": lambda: chain_attend(0), "C7": lambda: chain_norm(0), "END": end}
     for u in range(n):
@@ -1107,7 +1142,7 @@
     in_order(BACKWARD_ORDER, tasks)
 
     for i in range(TRIO):
-        drain(even_v.at[i], cross_send.at[i])
+        drain(head(part_in, SEQ), cross_send.at[i])
     drain(sum_got, sum_send.at[0])
     drain(head(sum_line, DOWN_ROW), sum_send.at[1])
     for u in range(n):
@@ -1127,38 +1162,66 @@
 def backward(weights, mine, vec, cos, sin, x_in, y_in, d_y, saved):
     n = len(PIECES)
     shape, hbm, vmem = jax.ShapeDtypeStruct, pl.BlockSpec(memory_space=pltpu.HBM), pl.BlockSpec(memory_space=pltpu.VMEM)
-    wide = lambda cols: (SEQ, cols)
+
+    def tokens(cols, dtype=BF16):
+        return shape((SEQ, cols), dtype)
+
     far = PIECES[PAIR:]
+    sums = [shape((rows, TILE), F32) for rows in (BAND, SPREAD, 56)]
+    scratch = [shape((PLANE_SEQ, DIM), BF16), shape((PLANE_SEQ, WIDE), BF16)] + [shape(acc_shape(name), F32) for _, name in PIECES]
+    scratch += [shape((PAIR, TRIO * acc_shape(name)[0] // LINE, acc_shape(name)[1]), F32) for _, name in PIECES] + sums
+    scratch += [shape((PAIR, DIM, DIM), BF16), shape((PAIR, TILE, FFN), BF16), shape((PAIR, SEQ, DIM), F32), tokens(QKV_COLS),
+                shape((HEADS, SEQ, SEQ), BF16), tokens(DIM), tokens(DIM), tokens(DIM), tokens(FFN), tokens(DIM), tokens(QKV_COLS),
+                tokens(DIM), tokens(DIM, F32), shape((SHARD, DIM), F32), tokens(DIM, F32)]
+    sems = [(n,), (n, SIX), (n,), (n, LINE), (n,), (n,), (PEERS,), (n,), (n, PAIR, LINE), (n,), (n,), (n,), (PAIR,), (PAIR,), (PAIR,), (PAIR,), (PAIR,), (LINE,),
+            (1,), (TRIO,), (TRIO,), (PAIR,)]
     outs = pl.pallas_call(
         backward_kernel,
         out_shape=[shape((PAIR, LINE, SHARD, DIM), F32), shape((PAIR, SHARD, FFN), F32), shape((PAIR, TILE, DIM), F32), shape((PLANE, TILE), F32),
-                   shape(wide(DIM), BF16)]
+                   tokens(DIM)]
         + [shape((FAR, DIM), BF16) for _ in far] + [shape((FAR, WIDTH[name]), BF16) for _, name in far]
-        + [shape(wide(FFN), BF16), shape((LAYERS, SEQ, DIM), BF16), shape((LAYERS, SEQ, QKV_COLS), BF16), shape(wide(DIM), BF16),
-           shape((768, DIM), F32), shape((576, DIM), F32)],
-        in_specs=[hbm] * TRIO + [vmem] * TRIO + [hbm] * (PEERS + len(KEPT)),
-        out_specs=[hbm] * TRIO + [vmem] + [hbm] * (PAIR * len(far) + PEERS),
-        scratch_shapes=[pltpu.VMEM((1536, DIM), BF16), pltpu.VMEM((1536, WIDE), BF16), pltpu.VMEM((1536, WIDE), BF16)]
-        + [pltpu.VMEM(acc_shape(name), F32) for _, name in PIECES]
-        + [pltpu.VMEM((PAIR, TRIO * acc_shape(name)[0] // LINE, acc_shape(name)[1]), F32) for _, name in PIECES]
-        + [pltpu.VMEM((BAND, TILE), F32), pltpu.VMEM((SPREAD, TILE), F32), pltpu.VMEM((56, TILE), F32),
-           pltpu.VMEM((PAIR, DIM, DIM), BF16), pltpu.VMEM((PAIR, TILE, FFN), BF16), pltpu.VMEM((PAIR, SEQ, DIM), F32)]
-        + [pltpu.VMEM(s, BF16) for s in (wide(QKV_COLS), (HEADS, SEQ, SEQ), wide(DIM), wide(DIM), wide(DIM), wide(FFN),
-                                         wide(DIM), wide(QKV_COLS), wide(DIM))]
-        + [pltpu.VMEM(wide(DIM), F32), pltpu.VMEM((SHARD, DIM), F32), pltpu.VMEM((DIM, WIDE), BF16), pltpu.VMEM((WIDE, DIM), BF16),
-           pltpu.VMEM((PAIR, SEQ, DIM), F32), pltpu.VMEM((TRIO, SEQ, DIM), F32)]
-        + [DMA((n,)), DMA((n, SIX)), DMA((n,)), DMA((n,)), DMA((n,)), DMA((n,)), DMA((PEERS,)), DMA((n,)), DMA((n, PAIR, LINE)),
-           DMA((n,)), DMA((n,)), DMA((n,)), DMA((PAIR,)), DMA((PAIR,)), DMA((PAIR,)), DMA((PAIR,)), DMA((PAIR,)), DMA((LINE,)), DMA,
-           DMA((LINE,)), DMA((LINE,)), DMA((TRIO,)), DMA((TRIO,))],
+        + [tokens(FFN), shape((LAYERS, SEQ, DIM), BF16), shape((LAYERS, SEQ, QKV_COLS), BF16), tokens(DIM),
+           shape((576, DIM), F32)],
+        in_specs=[hbm] * TRIO + [vmem] * TRIO + [hbm] * PLANE + [vmem] + [hbm] * len(KEPT),
+        out_specs=[hbm] * TRIO + [vmem] + [hbm] * (PAIR * len(far) + SIX),
+        scratch_shapes=[pltpu.VMEM(s.shape, s.dtype) for s in scratch] + [DMA(s) for s in sems],
         compiler_params=pltpu.CompilerParams(collective_id=1, has_side_effects=True, vmem_limit_bytes=67043328),
         name="backward",
     )(*weights, vec, cos, sin, x_in, y_in, d_y, *mine, *[saved[key] for key in KEPT])
     return outs[:FIVE]
 
 
-def pack_small(b_attn, ln_par, b_up, b_down):
-    rows = [b_attn.reshape(PAIR, TILE), ln_par.reshape(PAIR, TILE), b_up, jnp.pad(b_down, ((0, 0), (0, HALF_SEQ)))]
-    return jnp.stack(rows, axis=1).reshape(PLANE, TILE)
+def hand_over_kernel(*refs):
+    big, small, refs = refs[:LINE], refs[LINE], refs[FIVE:]
+    outs, (gb_attn, g_ln, gb_up, gb_down), refs = refs[:LINE], refs[LINE:PLANE], refs[PLANE:]
+    held, (in_sem, out_sem) = refs[:LINE], refs[LINE:]
+    for i in range(LINE):
+        local(big[i], held[i], in_sem.at[i]).start()
+    for l in range(PAIR):
+        for t, dst in enumerate((gb_attn, g_ln)):
+            row = small[pl.ds(LINE * l + t, 1), :]
+            for k in range(LINE):
+                dst[l, pl.ds(k, 1), :] = (pltpu.roll(row, TILE - SHARD * k, 1) if k else row)[:, :SHARD]
+        gb_up[pl.ds(l, 1), :] = small[pl.ds(LINE * l + PAIR, 1), :]
+        gb_down[pl.ds(l, 1), :] = small[pl.ds(LINE * l + TRIO, 1), :][:, :SHARD]
+    for i in range(LINE):
+        drain(held[i], in_sem.at[i])
+        local(held[i], outs[i], out_sem.at[i]).start()
+    for i in range(LINE):
+        drain(held[i], out_sem.at[i])
+
+
+def hand_over(big, small):
+    shape, hbm, vmem = jax.ShapeDtypeStruct, pl.BlockSpec(memory_space=pltpu.HBM), pl.BlockSpec(memory_space=pltpu.VMEM)
+    tails = [shape(s, F32) for s in ((PAIR, LINE, SHARD), (PAIR, LINE, SHARD), (PAIR, TILE), (PAIR, SHARD))]
+    return pl.pallas_call(
+        hand_over_kernel,
+        out_shape=[shape(b.shape, b.dtype) for b in big] + tails,
+        in_specs=[hbm] * LINE + [vmem],
+        out_specs=[hbm] * LINE + [vmem] * LINE,
+        scratch_shapes=[pltpu.VMEM(b.shape, b.dtype) for b in big] + [DMA((LINE,)), DMA((LINE,))],
+        name="hand_over",
+    )(*big, small)
 
 
 def solution(mesh):
@@ -1169,13 +1232,11 @@
 
     def device_step(x, lengths, d_y, w_attn, b_attn, ln_par, w_up, b_up, w_down, b_down):
         cos, sin = rotary_tables()
-        keep = (jnp.arange(SEQ)[None] < lengths[0]).astype(F32)
-        weights, mine, vec, y, saved = forward(w_attn, w_up, w_down, pack_small(b_attn, ln_par, b_up, b_down), x[0], keep,
-                                               cos, sin, d_y[0])
+        weights, mine, vec, y, saved = forward(w_attn, w_up, w_down, b_attn, ln_par, b_up, b_down, x[0], lengths, cos, sin,
+                                               d_y[0])
         g_attn, g_up, g_down, g_small, d_x = backward(weights, mine, vec, cos, sin, x[0], y, d_y[0], saved)
-        rows = g_small.reshape(PAIR, LINE, TILE)
-        return (d_x[None], g_attn, rows[:, 0].reshape(PAIR, LINE, SHARD), rows[:, 1].reshape(PAIR, LINE, SHARD), g_up, rows[:, PAIR],
-                g_down, rows[:, TRIO, :SHARD])
+        outs = hand_over((d_x, g_attn, g_up, g_down), g_small)
+        return (outs[0][None], outs[1], outs[LINE], outs[FIVE], outs[PAIR], outs[SIX], outs[TRIO], outs[PEERS])
 
     return jax.shard_map(device_step, mesh=mesh,
                          in_specs=(batch_spec, batch_spec, batch_spec) + weight_specs,

time: 436 us -> 412 us (0.945)
  local copies, waits for them, and re-layouts: 12.9 us -> 0 us
  Pallas kernels: 420 us -> 410 us
    pallas_call x1, Pallas kernels: 254 us -> 232 us  [backward(): pl.pallas_call(backward_kernel, out_shape=[shape((PAIR, LINE, SHARD, DIM)...]
    pallas_call x1, Pallas kernels: 166 us -> 174 us  [forward(): pl.pallas_call(forward_kernel, out_shape=[shape((LAYERS, LINE, DIM, DIM),...]
    unnamed x8 -> x0, local copies, waits for them, and re-layouts: 6.02 us -> none
    pallas_call x0 -> x1, Pallas kernels: none -> 4.45 us  [hand_over(): pl.pallas_call(hand_over_kernel, out_shape=[shape(b.shape, b.dtype) for b...]
where the time goes in v5:
time: 412 us; the launch traced here: 411 us
  Pallas kernels  410 us (100%)
    pallas_call x1, Pallas kernels, backward(): pl.pallas_call(backward_kernel, out_shape=[shape((PAIR, LINE, SHARD, DIM)...  232 us
    pallas_call x1, Pallas kernels, forward(): pl.pallas_call(forward_kernel, out_shape=[shape((LAYERS, LINE, DIM, DIM),...  174 us

profile of v5, /device:TPU:0, one launch (start us, length us, event | category | flops | bytes accessed | tf_op | source)
XLA Modules:
  0.0 411.3 jit_solution(7101120400057163964)
XLA Ops:
  1.3 173.7 %forward.1 = (bf16[2,4,1024,1024]{3,2,1,0:T(8,128)(2,1)}, bf16[1024,4096]{1,0:T(8,128)(2,1)}, bf16[4096,1024]{1,0:T(8,128)(2,1)}, bf16[256,128]{1,0:T(8,128)(2,1...) custom-call(bf16[2,4,32,1024]{3,2,1,0:T(8,128)(2,1)} %refs_0_.1, ...), custom_call_target="tpu_custom_call" | custom-call | tf_op jit(solution)/shard_map/forward/pallas_call | solution.py:785
  175.0 231.7 %backward.1 = (f32[2,4,32,1024]{3,2,1,0:T(8,128)}, f32[2,32,4096]{2,1,0:T(8,128)}, f32[2,128,1024]{2,1,0:T(8,128)}, f32[8,128]{1,0:T(8,128)}, bf16[192,1024]{1,0...) custom-call(bf16[2,4,1024,1024]{3,2,1,0:T(8,128)(2,1)} %get-tuple-el, ...), custom_call_target="tpu_custom_call" | custom-call | tf_op jit(solution)/shard_map/backward/pallas_call | solution.py:1178
  406.7 4.5 %hand_over.1 = (bf16[192,1024]{1,0:T(8,128)(2,1)}, f32[2,4,32,1024]{3,2,1,0:T(8,128)}, f32[2,32,4096]{2,1,0:T(8,128)}, f32[2,128,1024]{2,1,0:T(8,128)}, f32[2,4,...) custom-call(bf16[192,1024]{1,0:T(8,128)(2,1)} %get-tuple-element.71.refs_0_, ...), custom_call_target="tpu_custom_call" | custom-call | tf_op jit(solution)/shard_map/hand_over/pallas_call | solution.py:1217
